TPU v7x, 512 devices: a 8x2x16 block of a 8x8x16 slice. The times are simulated.
512 devices in a mesh: period: 2 (over y), gx: 16 (over z), gy: 8 (over x), gz: 2 (over core).
Axes of the slice: x: 8, y: 2, z: 16, core: 2. Of those that a mesh axis runs over, the one named last changes fastest.
The devices are a block of a 8x8x16 slice.
Arguments:
- residual: float32 [4, 3, 64, 64, 256], P('period', None, 'gx', 'gy', 'gz'), parts along dimension 0, may hold values from -6 to 6
- classes: int32 [64, 64, 256], P('gx', 'gy', 'gz'), may hold values from 0 to 15
- edge_mask: int32 [3, 64, 64, 256], P(None, 'gx', 'gy', 'gz'), may hold values from 0 to 1
- class_weight: float32 [32], P('period'), parts along dimension 0, may hold values from 0.01 to 1
Outputs:
- preconditioned: float32 [4, 3, 64, 64, 256], P('period', None, 'gx', 'gy', 'gz'), parts along dimension 0
There are 2 independent parts, one for each index of `period`. A program takes and returns all parts, laid end to end along the dimension named above; an argument that names none is the same for every part. Nothing has to cross between parts.
All inputs are finite; a program needn't handle non-finite values.
Results may differ from a plain program's by a relative error of at most 0.00025.
Values sent between devices are 32-bit elements; how exact they have to be, the bound alone decides.
No kernel may reach another device: no remote copies, remote signals or barrier semaphores. Data moves between devices by JAX's collectives and lax.ppermute only.
A program may use at most 64 MiB of HBM per device.

v0:
```python
import functools

import jax
import jax.numpy as jnp
from jax import lax
from jax.experimental import pallas as pl
from jax.experimental.pallas import tpu as pltpu
from jax.sharding import PartitionSpec as P

aspect = 2.0
face_weight = (1.0 / (aspect * aspect), 1.0, 1.0)
mass_factor = (aspect * aspect, 1.0, 1.0)
stiff_weight = (
    2.0 * (face_weight[1] + face_weight[2]),
    2.0 * (face_weight[0] + face_weight[2]),
    2.0 * (face_weight[0] + face_weight[1]),
)
edge_damping = 0.6
shift_ratio = 0.0001
shift_added = 0.05
coarse_scale = (0.5625, 0.1875, 0.1875)

f32 = jnp.float32
TILE = 8
ROWS = 3 * TILE
GROUPS = 4
DEPTH = 32


def lanes(shape):
    return lax.broadcasted_iota(jnp.int32, shape, 1)


def block_transpose(values, width):
    values = list(values)
    count = len(values)
    group = lanes(values[0].shape) // width
    bit = 1
    while bit < count:
        clear = (group & bit) == 0
        for low in range(count):
            if low & bit:
                continue
            high = low | bit
            first, second = values[low], values[high]
            values[low] = jnp.where(clear, first, pltpu.roll(second, bit * width, 1))
            values[high] = jnp.where(clear, pltpu.roll(first, 128 - bit * width, 1), second)
        bit *= 2
    return values


def loop(count, body, carry, unroll=1, reverse=False):
    def step(turn, state):
        for part in range(unroll):
            index = turn * unroll + part
            state = body(count - 1 - index if reverse else index, state)
        return state

    return lax.fori_loop(0, count // unroll, step, carry)


def y_next(v, by=1):
    return pltpu.roll(v, v.shape[0] - by, 0)


def y_back(v, by=1):
    return pltpu.roll(v, by, 0)


def z_next(v, by=1):
    return pltpu.roll(v, 128 - by, 1)


def z_back(v, by=1):
    return pltpu.roll(v, by, 1)


def pack_body(residual, classes, edge_mask, class_weight, out):
    thick = classes.shape[0]
    slots = []
    for part in range(2):
        for comp in range(3):
            slots += [residual[part, comp, i] for i in range(thick)]
    for i in range(thick):
        labels = classes[i]
        cells = jnp.zeros(labels.shape, f32)
        for label in range(class_weight.shape[0]):
            cells = jnp.where(labels == label, class_weight[label], cells)
        slots.append(cells)
    for comp in range(3):
        slots += [(1 - edge_mask[comp, i]).astype(f32) for i in range(thick)]
    zero = jnp.zeros((TILE, 128), f32)
    while len(slots) % 16:
        slots.append(zero)
    for part in range(len(slots) // 16):
        moved = block_transpose(slots[16 * part : 16 * part + 16], TILE)
        for target in range(16):
            out[target, TILE * part : TILE * part + TILE, :] = moved[target]


def unpack_body(packed, out):
    zero = jnp.zeros((TILE, 128), f32)
    for part in range(2):
        moved = block_transpose(
            [packed[source, TILE * part : TILE * part + TILE, :] for source in range(16)], TILE
        )
        for slot in range(16):
            field, i = divmod(16 * part + slot, 4)
            if field < 6:
                out[field // 3, field % 3, i] = moved[slot]


def line_body(
    place,
    middle,
    shallow,
    deep,
    out,
    W,
    E,
    M,
    Dm,
    Rm,
    KW,
    CW,
    FI,
    FB,
    FQ,
    CI,
    CB,
    CQ,
    NS,
    SM,
    CS,
    TY,
    OUT,
):
    extent_y, extent_z = place[2], place[3]
    shape = (ROWS, 128)
    lane = lanes(shape)
    row = lax.broadcasted_iota(jnp.int32, shape, 0)
    at_y = row + place[0]
    at_z = lane % DEPTH + place[1]
    inside = jnp.where(
        (at_y >= 0) & (at_y < extent_y) & (at_z >= 0) & (at_z < extent_z), 1.0, 0.0
    ).astype(f32)
    not_first = jnp.where(lane < DEPTH, 0.0, 1.0).astype(f32)
    not_last = jnp.where(lane >= 128 - DEPTH, 0.0, 1.0).astype(f32)
    even_row = row % 2 == 0
    even_lane = lane % 2 == 0

    def pad_low(ref, field):
        ref[field, 0] = pltpu.roll(ref[field, 16], DEPTH, 1) * not_first

    def pad_high(ref, field):
        ref[field, 17] = pltpu.roll(ref[field, 1], 128 - DEPTH, 1) * not_last

    zero8 = jnp.zeros((TILE, 128), f32)
    windows = (shallow, middle, deep)

    def spread_out(a, state):
        for y in range(3):
            for part in range(3):
                pieces = []
                for p in range(16):
                    g, t = divmod(p, 4)
                    if t == 3:
                        pieces.append(zero8)
                    else:
                        pieces.append(
                            windows[t][y * 16 + 4 * g + a, TILE * part : TILE * part + TILE, :]
                        )
                moved = block_transpose(pieces, TILE)
                for slot in range(16):
                    field, i = divmod(16 * part + slot, 4)
                    if field < 10:
                        W[field, 4 * a + i + 1, TILE * y : TILE * y + TILE, :] = moved[slot]
        return state

    loop(4, spread_out, 0)
    pad_low(W, 6)

    def coefficients(l, state):
        c = W[6, l + 1]
        cx = W[6, l]
        cy = y_back(c)
        cz = z_back(c)
        averages = (
            0.25 * (((c + cy) + cz) + z_back(cy)),
            0.25 * (((c + cx) + cz) + z_back(cx)),
            0.25 * (((c + cx) + cy) + y_back(cx)),
        )
        for d in range(3):
            free = W[7 + d, l + 1]
            masses = mass_factor[d] * averages[d] * free
            diagonal = stiff_weight[d] + masses
            damp = edge_damping * free / diagonal
            M[d, l] = masses
            Dm[d, l] = damp
            for part in range(2):
                source = W[3 * part + d, l + 1] * free
                W[3 * part + d, l + 1] = source
                E[3 * part + d, l + 1] = source * damp
            stiff = diagonal * free
            for g, values in enumerate(block_transpose([masses, stiff, stiff, stiff], DEPTH)):
                KW[d, 16 * g + l + 1] = values
        return state

    loop(16, coefficients, 0)

    for d in range(3):
        KW[d, 0] = jnp.zeros(shape, f32)

    def side_fluxes(part, l):
        e1, e2, e3 = (E[3 * part + d, l] for d in range(3))
        b2 = face_weight[1] * ((z_next(e1) - e1) - (E[3 * part + 2, l + 1] - e3))
        b3 = face_weight[2] * ((E[3 * part + 1, l + 1] - e2) - (y_next(e1) - e1))
        return b2, b3

    def curl(part, l, before):
        e1, e2, e3 = (E[3 * part + d, l] for d in range(3))
        b2, b3 = side_fluxes(part, l)
        b1 = face_weight[0] * ((y_next(e3) - e3) - (z_next(e2) - e2))
        b2_before, b3_before = before
        results = (
            (z_back(b2) - b2) - (y_back(b3) - b3) + M[0, l - 1] * e1,
            (b3_before - b3) - (z_back(b1) - b1) + M[1, l - 1] * e2,
            (y_back(b1) - b1) - (b2_before - b2) + M[2, l - 1] * e3,
        )
        return results, (b2, b3)

    for field in range(6):
        pad_low(E, field)
        pad_high(E, field)

    def first_remainder(l, state):
        after = []
        for part in range(2):
            results, fluxes = curl(part, l + 1, state[part])
            after.append(fluxes)
            for d in range(3):
                Rm[3 * part + d, l + 1] = (
                    W[3 * part + d, l + 1] - results[d] * W[7 + d, l + 1]
                )
        return tuple(after)

    loop(16, first_remainder, (side_fluxes(0, 0), side_fluxes(1, 0)))
    pad_low(Rm, 0)
    pad_low(Rm, 3)

    def to_nodes(l, state):
        for part in range(2):
            r1, r2, r3 = (Rm[3 * part + d, l + 1] for d in range(3))
            r1b = Rm[3 * part, l]
            r2b = y_back(r2)
            r3b = z_back(r3)
            members = [
                ((r1b - r1) + (r2b - r2)) + (r3b - r3),
                0.5 * (r1 + r1b),
                0.5 * (r2 + r2b),
                0.5 * (r3 + r3b),
            ]
            for g, values in enumerate(block_transpose(members, DEPTH)):
                NS[part, 16 * g + l] = values
        return state

    loop(16, to_nodes, 0)

    def factors(x, state):
        fine_before, coarse_before, cw1_before = state
        w1b, w1, w2, w3 = KW[0, x], KW[0, x + 1], KW[1, x + 1], KW[2, x + 1]
        total = ((((w1 + w1b) + w2) + y_back(w2)) + w3) + z_back(w3)
        pivot = ((1.0 + shift_ratio) * total + shift_added) - w1b * fine_before
        inverse = inside / pivot
        quotient = w1 * inverse
        FI[x] = inverse
        FB[x] = w1b * inverse
        FQ[x] = quotient
        cw = []
        for d, w in enumerate((w1, w2, w3)):
            pair = w + y_next(w)
            cw.append(coarse_scale[d] * (pair + z_next(pair)))
        CW[0, x] = cw[1]
        CW[1, x] = cw[2]
        total = ((((cw[0] + cw1_before) + cw[1]) + y_back(cw[1], 2)) + cw[2]) + z_back(cw[2], 2)
        pivot = ((1.0 + shift_ratio) * total + shift_added) - cw1_before * coarse_before
        inverse = inside / pivot
        coarse_quotient = cw[0] * inverse
        CI[x] = inverse
        CB[x] = cw1_before * inverse
        CQ[x] = coarse_quotient
        return quotient, coarse_quotient, cw[0]

    nothing = jnp.zeros(shape, f32)
    loop(64, factors, (nothing, nothing, nothing))

    def eliminate(source, inverse, back):
        def step(x, state):
            scale, couple = inverse[x], back[x]
            after = []
            for part in range(2):
                value = source[part, x] * scale + couple * state[part]
                TY[part, x] = value
                after.append(value)
            return tuple(after)

        loop(64, step, (nothing, nothing), unroll=4)

    def substitute(quotient, then):
        def step(x, state):
            factor = quotient[x]
            after = []
            for part in range(2):
                value = TY[part, x] + factor * state[part]
                after.append(value)
                then(part, x, value)
            return tuple(after)

        loop(64, step, (nothing, nothing), unroll=2, reverse=True)

    def sides(v, w2, w3, by):
        return ((w2 * y_next(v, by) + y_back(w2 * v, by)) + w3 * z_next(v, by)) + z_back(
            w3 * v, by
        )

    def after_smoothing(part, x, value):
        SM[part, x] = value
        residue = sides(value, KW[1, x + 1], KW[2, x + 1], 1)
        halved = residue + 0.5 * (y_back(residue) + y_next(residue))
        CS[part, x] = halved + 0.5 * (z_back(halved) + z_next(halved))

    def after_coarse(part, x, value):
        CS[part, x] = CS[part, x] + sides(value, CW[0, x], CW[1, x], 2)

    def after_correction(part, x, value):
        rows = jnp.where(even_row, value, 0.5 * (y_back(value) + y_next(value)))
        both = jnp.where(even_lane, rows, 0.5 * (z_back(rows) + z_next(rows)))
        smoothed = SM[part, x] + both
        CS[part, x] = NS[part, x] + sides(smoothed, KW[1, x + 1], KW[2, x + 1], 1)

    def after_potential(part, x, value):
        NS[part, x] = value

    eliminate(NS, FI, FB)
    substitute(FQ, after_smoothing)
    eliminate(CS, CI, CB)
    substitute(CQ, after_coarse)
    eliminate(CS, CI, CB)
    substitute(CQ, after_correction)
    eliminate(CS, FI, FB)
    substitute(FQ, after_potential)

    def from_nodes(l, state):
        for part in range(2):
            members = block_transpose([NS[part, 16 * g + l] for g in range(4)], DEPTH)
            p0, p1, p2, p3 = members
            Rm[3 * part, l + 1] = p0
            Rm[3 * part + 1, l + 1] = p1
            for d, (g_part, h_part) in (
                (1, (y_next(p0) - p0, 0.5 * (p2 + y_next(p2)))),
                (2, (z_next(p0) - p0, 0.5 * (p3 + z_next(p3)))),
            ):
                E[3 * part + d, l + 1] = (
                    E[3 * part + d, l + 1] + (g_part + h_part) * W[7 + d, l + 1]
                )
        return state

    loop(16, from_nodes, 0)
    for part in range(2):
        pad_high(Rm, 3 * part)
        pad_high(Rm, 3 * part + 1)

    def second_first(l, state):
        for part in range(2):
            p0, p1 = Rm[3 * part, l + 1], Rm[3 * part + 1, l + 1]
            g_part = Rm[3 * part, l + 2] - p0
            h_part = 0.5 * (p1 + Rm[3 * part + 1, l + 2])
            E[3 * part, l + 1] = E[3 * part, l + 1] + (g_part + h_part) * W[7, l + 1]
        return state

    loop(16, second_first, 0)
    for field in range(6):
        pad_low(E, field)
        pad_high(E, field)

    def last_step(l, state):
        after = []
        for part in range(2):
            results, fluxes = curl(part, l + 1, state[part])
            after.append(fluxes)
            for d in range(3):
                field = 3 * part + d
                remainder = W[field, l + 1] - results[d] * W[7 + d, l + 1]
                value = E[field, l + 1] + Dm[d, l] * remainder
                OUT[field, l] = value[TILE : 2 * TILE]
        return tuple(after)

    loop(16, last_step, (side_fluxes(0, 0), side_fluxes(1, 0)))

    def gather_up(a, state):
        for part in range(2):
            pieces = []
            for slot in range(16):
                field, i = divmod(16 * part + slot, 4)
                pieces.append(OUT[field, 4 * a + i] if field < 6 else zero8)
            moved = block_transpose(pieces, TILE)
            for g in range(4):
                out[4 * g + a, TILE * part : TILE * part + TILE, :] = moved[4 * g + 1]
        return state

    loop(4, gather_up, 0)


def vmem():
    return pl.BlockSpec(memory_space=pltpu.VMEM)


def smem():
    return pl.BlockSpec(memory_space=pltpu.SMEM)


def pack(residual, classes, edge_mask, class_weight, **options):
    return pl.pallas_call(
        pack_body,
        out_shape=jax.ShapeDtypeStruct((16, ROWS, 128), f32),
        in_specs=[vmem(), vmem(), vmem(), smem()],
        out_specs=vmem(),
        name="pack",
        **options,
    )(residual, classes, edge_mask, class_weight)


def unpack(packed, shape, **options):
    return pl.pallas_call(
        unpack_body,
        out_shape=jax.ShapeDtypeStruct(shape, f32),
        in_specs=[vmem()],
        out_specs=vmem(),
        name="unpack",
        **options,
    )(packed)


def lines(place, middle, shallow, deep, **options):
    edge = lambda count, levels: pltpu.VMEM((count, levels, ROWS, 128), f32)
    line = pltpu.VMEM((64, ROWS, 128), f32)
    pair = pltpu.VMEM((2, 64, ROWS, 128), f32)
    return pl.pallas_call(
        line_body,
        out_shape=jax.ShapeDtypeStruct((16, 2 * TILE, 128), f32),
        in_specs=[smem(), vmem(), vmem(), vmem()],
        out_specs=vmem(),
        scratch_shapes=[
            edge(10, 18),
            edge(6, 18),
            edge(3, 16),
            edge(3, 16),
            edge(6, 18),
            pltpu.VMEM((3, 65, ROWS, 128), f32),
            pair,
            line,
            line,
            line,
            line,
            line,
            line,
            pair,
            pair,
            pair,
            pair,
            pltpu.VMEM((6, 16, TILE, 128), f32),
        ],
        name="lines",
        **options,
    )(place, middle, shallow, deep)


def swap(values):
    return lax.all_to_all(values, "gx", 0, 0, tiled=True)


def per_device(residual, classes, edge_mask, class_weight):
    size_x, size_y, size_z = (lax.axis_size(name) for name in ("gx", "gy", "gz"))
    axes = ("gx", "gy", "gz")
    tiles = size_x * size_z

    def position(y, tile):
        z, x = divmod(tile, size_x)
        return (x * size_y + y) * size_z + z

    def from_side(values, step_y, step_tile):
        pairs = [
            (position(y, tile), position(y + step_y, tile + step_tile))
            for y in range(size_y)
            for tile in range(tiles)
            if 0 <= y + step_y < size_y and 0 <= tile + step_tile < tiles
        ]
        return lax.ppermute(values, axes, pairs)

    own = swap(
        pack(
            residual,
            classes,
            edge_mask,
            class_weight,
        )
    )
    middle = jnp.concatenate([from_side(own, 1, 0), own, from_side(own, -1, 0)], axis=0)
    shallow = from_side(middle, 0, 1)
    deep = from_side(middle, 0, -1)
    tile = lax.axis_index("gz") * size_x + lax.axis_index("gx")
    place = jnp.stack(
        [
            lax.axis_index("gy") * TILE - TILE,
            tile * TILE - TILE,
            jnp.int32(size_y * TILE),
            jnp.int32(tiles * TILE),
        ]
    ).astype(jnp.int32)
    options = dict(compiler_params=pltpu.CompilerParams(vmem_limit_bytes=50 * 2**20))
    result = swap(lines(place, middle, shallow, deep, **options))
    return unpack(result, residual.shape)


def solution(mesh):
    return jax.shard_map(
        per_device,
        mesh=mesh,
        in_specs=(
            P("period", None, "gx", "gy", "gz"),
            P("gx", "gy", "gz"),
            P(None, "gx", "gy", "gz"),
            P("period"),
        ),
        out_specs=P("period", None, "gx", "gy", "gz"),
        check_vma=False,
    )
```

profile of v0, /device:TPU:86, one launch (start us, length us, event | category | flops | bytes accessed | tf_op | source)
XLA Modules:
  0.0 168.1 jit_solution(6493013649325444413)
XLA Ops:
  0.0 1.9 %pack.1 = f32[16,24,128]{2,1,0:T(8,128)} custom-call(f32[2,3,4,8,128]{4,3,2,1,0:T(8,128)} %residual.1, s32[4,8,128]{2,1,0:T(8,128)} %classes.1, s32[3,4,8,128]{3,2,1,0:T(8,128)} %edge_mask.1, f32[16]{0:T(128)} %class_weight.1), custom_call_target="tpu_custom_call" | custom-call | tf_op jit(solution)/shard_map/pack/pallas_call | solution.py:423
  1.9 59.9 %all_to_all.10 = f32[16,24,128]{2,1,0:T(8,128)S(1)} all-to-all(f32[16,24,128]{2,1,0:T(8,128)} %pack.1), channel_id=1, replica_groups=mesh['period'=2,'gx'=16,'gy'=8,'gz'=2] {'gx'}, dimensions={0} | all-to-all | bytes 393216 | tf_op jit(solution)/shard_map/all_to_all | solution.py:479
  61.8 4.8 %collective-permute-start = (f32[16,24,128]{2,1,0:T(8,128)S(1)}, f32[16,24,128]{2,1,0:T(8,128)S(1)}, u32[]{:S(2)}, u32[]{:S(2)}) collective-permute-start(f32[16,24,128]{2,1,0:T(8,128)S(1)} %all_to_all.10), channel_id=1, source_target_pairs={{0,2},{16,18},{32,34},{48,50},{64,66},{80,82},{96,98},{112,114},{1... | collective-permute-start | bytes 589832 | tf_op jit(solution)/shard_map/ppermute | solution.py:498
  66.6 2.0 %collective-permute-start.1 = (f32[16,24,128]{2,1,0:T(8,128)S(1)}, f32[16,24,128]{2,1,0:T(8,128)S(1)}, u32[]{:S(2)}, u32[]{:S(2)}) collective-permute-start(f32[16,24,128]{2,1,0:T(8,128)S(1)} %all_to_all.10), channel_id=1, source_target_pairs={{2,0},{18,16},{34,32},{50,48},{66,64},{82,80},{98,96},{114,112},{1... | collective-permute-start | bytes 589832 | tf_op jit(solution)/shard_map/ppermute | solution.py:498
  68.5 1.2 collective-permute-done
  69.8 5.6 %collective-permute-done.1 = f32[16,24,128]{2,1,0:T(8,128)S(1)} collective-permute-done((f32[16,24,128]{2,1,0:T(8,128)S(1)}, f32[16,24,128]{2,1,0:T(8,128)S(1)}, u32[]{:S(2)}, u32[]{:S(2)}) %collective-permute-start.1) | collective-permute-done | bytes 196640 | tf_op jit(solution)/shard_map/ppermute | solution.py:498
  75.4 1.3 collective-permute-start.3
  76.7 4.6 %collective-permute-start.2 = (f32[48,24,128]{2,1,0:T(8,128)S(1)}, f32[48,24,128]{2,1,0:T(8,128)S(1)}, u32[]{:S(2)}, u32[]{:S(2)}) collective-permute-start(f32[48,24,128]{2,1,0:T(8,128)S(1)} %constant_dynamic-update-slice_fusion.middle), channel_id=1, source_target_pairs={{0,16},{16,32},{32,48},{48,64},{64,80},{80,96},{96,112},{112,128},... | collective-permute-start | bytes 1769480 | tf_op jit(solution)/shard_map/ppermute | solution.py:498
  81.4 0.1 pad_add_fusion.place
  81.4 9.3 %collective-permute-done.3.deep = f32[48,24,128]{2,1,0:T(8,128)S(1)} collective-permute-done((f32[48,24,128]{2,1,0:T(8,128)S(1)}, f32[48,24,128]{2,1,0:T(8,128)S(1)}, u32[]{:S(2)}, u32[]{:S(2)}) %collective-permute-start.3) | collective-permute-done | bytes 589856 | tf_op jit(solution)/shard_map/ppermute | solution.py:498
  90.8 3.3 %collective-permute-done.2.shallow = f32[48,24,128]{2,1,0:T(8,128)S(1)} collective-permute-done((f32[48,24,128]{2,1,0:T(8,128)S(1)}, f32[48,24,128]{2,1,0:T(8,128)S(1)}, u32[]{:S(2)}, u32[]{:S(2)}) %collective-permute-start.2) | collective-permute-done | bytes 589856 | tf_op jit(solution)/shard_map/ppermute | solution.py:498
  94.1 50.5 %lines.1 = f32[16,16,128]{2,1,0:T(8,128)S(1)} custom-call(s32[4]{0:T(128)S(1)} %pad_add_fusion.place, f32[48,24,128]{2,1,0:T(8,128)S(1)} %constant_dynamic-update-slice_fusion.middle, f32[48,24,128]{2,1,0:T(8,128)S(1)} %collective-permute-done.2.shallow, f32[48,24,128]{2,1,0:T(8,128)S(1)} %collective-permute-done.3.deep), custom_call_target="tpu_custom_call" | custom-call | tf_op jit(solution)/shard_map/lines/pallas_call | solution.py:448
  144.6 21.6 %all_to_all.11.packed = f32[16,16,128]{2,1,0:T(8,128)} all-to-all(f32[16,16,128]{2,1,0:T(8,128)S(1)} %lines.1), channel_id=1, replica_groups=mesh['period'=2,'gx'=16,'gy'=8,'gz'=2] {'gx'}, dimensions={0} | all-to-all | bytes 262144 | tf_op jit(solution)/shard_map/all_to_all | solution.py:479
  166.3 1.9 %unpack.1 = f32[2,3,4,8,128]{4,3,2,1,0:T(8,128)} custom-call(f32[16,16,128]{2,1,0:T(8,128)} %all_to_all.11.packed), custom_call_target="tpu_custom_call" | custom-call | tf_op jit(solution)/shard_map/unpack/pallas_call | solution.py:434
  (3 shorter events, 0.0 us)
Async XLA Ops:
  61.8 7.9 %collective-permute-start = (f32[16,24,128]{2,1,0:T(8,128)S(1)}, f32[16,24,128]{2,1,0:T(8,128)S(1)}, u32[]{:S(2)}, u32[]{:S(2)}) collective-permute-start(f32[16,24,128]{2,1,0:T(8,128)S(1)} %all_to_all.10), channel_id=1, source_target_pairs={{0,2},{16,18},{32,34},{48,50},{64,66},{80,82},{96,98},{112,114},{1... | collective-permute-start | bytes 589832 | tf_op jit(solution)/shard_map/ppermute | solution.py:498
  66.6 8.8 %collective-permute-start.1 = (f32[16,24,128]{2,1,0:T(8,128)S(1)}, f32[16,24,128]{2,1,0:T(8,128)S(1)}, u32[]{:S(2)}, u32[]{:S(2)}) collective-permute-start(f32[16,24,128]{2,1,0:T(8,128)S(1)} %all_to_all.10), channel_id=1, source_target_pairs={{2,0},{18,16},{34,32},{50,48},{66,64},{82,80},{98,96},{114,112},{1... | collective-permute-start | bytes 589832 | tf_op jit(solution)/shard_map/ppermute | solution.py:498
  75.4 15.3 %collective-permute-start.3 = (f32[48,24,128]{2,1,0:T(8,128)S(1)}, f32[48,24,128]{2,1,0:T(8,128)S(1)}, u32[]{:S(2)}, u32[]{:S(2)}) collective-permute-start(f32[48,24,128]{2,1,0:T(8,128)S(1)} %constant_dynamic-update-slice_fusion.middle), channel_id=1, source_target_pairs={{16,0},{32,16},{48,32},{64,48},{80,64},{96,80},{112,96},{128,112},... | collective-permute-start | bytes 1769480 | tf_op jit(solution)/shard_map/ppermute | solution.py:498
  76.7 17.4 %collective-permute-start.2 = (f32[48,24,128]{2,1,0:T(8,128)S(1)}, f32[48,24,128]{2,1,0:T(8,128)S(1)}, u32[]{:S(2)}, u32[]{:S(2)}) collective-permute-start(f32[48,24,128]{2,1,0:T(8,128)S(1)} %constant_dynamic-update-slice_fusion.middle), channel_id=1, source_target_pairs={{0,16},{16,32},{32,48},{48,64},{64,80},{80,96},{96,112},{112,128},... | collective-permute-start | bytes 1769480 | tf_op jit(solution)/shard_map/ppermute | solution.py:498
where the time goes:
time: 168 us
  blocking collectives  81.5 us (49%)
  Pallas kernels  54.3 us (32%)
  waiting for transfers between devices  19.5 us (12%)
  starting transfers between devices  12.7 us (8%)
    all_to_all x2, blocking collectives, swap(): return lax.all_to_all(values, 'gx', 0, 0, tiled=True)  81.5 us
    pallas_call x1, Pallas kernels, lines(): pl.pallas_call(line_body, out_shape=jax.ShapeDtypeStruct((16, 2 * TILE, 1...  50.5 us
    ppermute x4, waiting for transfers between devices, from_side(): return lax.ppermute(values, axes, pairs)  19.5 us
    ppermute x4, starting transfers between devices, from_side(): return lax.ppermute(values, axes, pairs)  12.7 us
  transfers between devices with their start and end apart: 4, of which 4 were waited for; matrix products, arithmetic and copies ran while one was open for 0% of the time, Pallas kernels for 0%

commit v1 on v0

--- a/solution.py
+++ b/solution.py
@@ -31,22 +31,10 @@
     return lax.broadcasted_iota(jnp.int32, shape, 1)
 
 
-def block_transpose(values, width):
-    values = list(values)
-    count = len(values)
-    group = lanes(values[0].shape) // width
-    bit = 1
-    while bit < count:
-        clear = (group & bit) == 0
-        for low in range(count):
-            if low & bit:
-                continue
-            high = low | bit
-            first, second = values[low], values[high]
-            values[low] = jnp.where(clear, first, pltpu.roll(second, bit * width, 1))
-            values[high] = jnp.where(clear, pltpu.roll(first, 128 - bit * width, 1), second)
-        bit *= 2
-    return values
+def turned(values):
+    gap = jnp.zeros((DEPTH - ROWS, 128), f32)
+    stacked = jnp.concatenate([piece for value in values for piece in (value, gap)], axis=0).T
+    return [stacked[DEPTH * g : DEPTH * g + ROWS] for g in range(4)]
 
 
 def loop(count, body, carry, unroll=1, reverse=False):
@@ -73,6 +61,9 @@
 
 def z_back(v, by=1):
     return pltpu.roll(v, by, 1)
+
+
+row_next, row_back, lane_next, lane_back = y_next, y_back, z_next, z_back
 
 
 def pack_body(residual, classes, edge_mask, class_weight, out):
@@ -93,21 +84,22 @@
     while len(slots) % 16:
         slots.append(zero)
     for part in range(len(slots) // 16):
-        moved = block_transpose(slots[16 * part : 16 * part + 16], TILE)
+        moved = jnp.concatenate(slots[16 * part : 16 * part + 16], axis=0).T
         for target in range(16):
-            out[target, TILE * part : TILE * part + TILE, :] = moved[target]
+            out[target, TILE * part : TILE * part + TILE, :] = moved[
+                TILE * target : TILE * target + TILE
+            ]
 
 
 def unpack_body(packed, out):
-    zero = jnp.zeros((TILE, 128), f32)
     for part in range(2):
-        moved = block_transpose(
-            [packed[source, TILE * part : TILE * part + TILE, :] for source in range(16)], TILE
-        )
+        moved = jnp.concatenate(
+            [packed[source, TILE * part : TILE * part + TILE, :] for source in range(16)], axis=0
+        ).T
         for slot in range(16):
             field, i = divmod(16 * part + slot, 4)
             if field < 6:
-                out[field // 3, field % 3, i] = moved[slot]
+                out[field // 3, field % 3, i] = moved[TILE * slot : TILE * slot + TILE]
 
 
 def line_body(
@@ -133,17 +125,19 @@
     SM,
     CS,
     TY,
+    RH,
     OUT,
 ):
     extent_y, extent_z = place[2], place[3]
     shape = (ROWS, 128)
     lane = lanes(shape)
     row = lax.broadcasted_iota(jnp.int32, shape, 0)
-    at_y = row + place[0]
-    at_z = lane % DEPTH + place[1]
+    at_y = lane % DEPTH + place[0]
+    at_z = row + place[1]
     inside = jnp.where(
         (at_y >= 0) & (at_y < extent_y) & (at_z >= 0) & (at_z < extent_z), 1.0, 0.0
     ).astype(f32)
+    coarse_inside = jnp.where(row % 2 == 0, inside, row_back(inside))
     not_first = jnp.where(lane < DEPTH, 0.0, 1.0).astype(f32)
     not_last = jnp.where(lane >= 128 - DEPTH, 0.0, 1.0).astype(f32)
     even_row = row % 2 == 0
@@ -170,11 +164,13 @@
                         pieces.append(
                             windows[t][y * 16 + 4 * g + a, TILE * part : TILE * part + TILE, :]
                         )
-                moved = block_transpose(pieces, TILE)
+                moved = jnp.concatenate(pieces, axis=0).T
                 for slot in range(16):
                     field, i = divmod(16 * part + slot, 4)
                     if field < 10:
-                        W[field, 4 * a + i + 1, TILE * y : TILE * y + TILE, :] = moved[slot]
+                        W[field, 4 * a + i + 1, TILE * y : TILE * y + TILE, :] = moved[
+                            TILE * slot : TILE * slot + TILE
+                        ]
         return state
 
     loop(4, spread_out, 0)
@@ -202,11 +198,11 @@
                 W[3 * part + d, l + 1] = source
                 E[3 * part + d, l + 1] = source * damp
             stiff = diagonal * free
-            for g, values in enumerate(block_transpose([masses, stiff, stiff, stiff], DEPTH)):
+            for g, values in enumerate(turned([masses, stiff, stiff, stiff])):
                 KW[d, 16 * g + l + 1] = values
         return state
 
-    loop(16, coefficients, 0)
+    loop(16, coefficients, 0, unroll=2)
 
     for d in range(3):
         KW[d, 0] = jnp.zeros(shape, f32)
@@ -244,7 +240,7 @@
                 )
         return tuple(after)
 
-    loop(16, first_remainder, (side_fluxes(0, 0), side_fluxes(1, 0)))
+    loop(16, first_remainder, (side_fluxes(0, 0), side_fluxes(1, 0)), unroll=4)
     pad_low(Rm, 0)
     pad_low(Rm, 3)
 
@@ -260,100 +256,114 @@
                 0.5 * (r2 + r2b),
                 0.5 * (r3 + r3b),
             ]
-            for g, values in enumerate(block_transpose(members, DEPTH)):
+            for g, values in enumerate(turned(members)):
                 NS[part, 16 * g + l] = values
         return state
 
-    loop(16, to_nodes, 0)
-
-    def factors(x, state):
-        fine_before, coarse_before, cw1_before = state
+    loop(16, to_nodes, 0, unroll=4)
+
+    def diagonals(x, cw1_before):
         w1b, w1, w2, w3 = KW[0, x], KW[0, x + 1], KW[1, x + 1], KW[2, x + 1]
-        total = ((((w1 + w1b) + w2) + y_back(w2)) + w3) + z_back(w3)
-        pivot = ((1.0 + shift_ratio) * total + shift_added) - w1b * fine_before
-        inverse = inside / pivot
-        quotient = w1 * inverse
-        FI[x] = inverse
-        FB[x] = w1b * inverse
-        FQ[x] = quotient
+        total = ((((w1 + w1b) + w3) + row_back(w3)) + w2) + lane_back(w2)
+        FI[x] = (1.0 + shift_ratio) * total + shift_added
         cw = []
         for d, w in enumerate((w1, w2, w3)):
-            pair = w + y_next(w)
-            cw.append(coarse_scale[d] * (pair + z_next(pair)))
-        CW[0, x] = cw[1]
-        CW[1, x] = cw[2]
-        total = ((((cw[0] + cw1_before) + cw[1]) + y_back(cw[1], 2)) + cw[2]) + z_back(cw[2], 2)
-        pivot = ((1.0 + shift_ratio) * total + shift_added) - cw1_before * coarse_before
-        inverse = inside / pivot
-        coarse_quotient = cw[0] * inverse
-        CI[x] = inverse
-        CB[x] = cw1_before * inverse
+            pair = w + row_next(w)
+            pair = jnp.where(even_row, pair, row_back(pair))
+            cw.append(coarse_scale[d] * (pair + lane_next(pair)))
+            CW[d, x + 1] = cw[d]
+        total = (
+            (((cw[0] + cw1_before) + cw[2]) + row_back(cw[2], 2)) + cw[1]
+        ) + lane_back(cw[1], 2)
+        CI[x] = (1.0 + shift_ratio) * total + shift_added
+        return cw[0]
+
+    nothing = jnp.zeros(shape, f32)
+    CW[0, 0] = nothing
+    loop(64, diagonals, nothing, unroll=4)
+
+    def factors(x, state):
+        fine_before, coarse_before = state
+        w1b, c1b = KW[0, x], CW[0, x]
+        inverse = inside / (FI[x] - w1b * fine_before)
+        coarse_inverse = coarse_inside / (CI[x] - c1b * coarse_before)
+        FI[x] = inverse
+        CI[x] = coarse_inverse
+        FB[x] = w1b * inverse
+        CB[x] = c1b * coarse_inverse
+        quotient = KW[0, x + 1] * inverse
+        coarse_quotient = CW[0, x + 1] * coarse_inverse
+        FQ[x] = quotient
         CQ[x] = coarse_quotient
-        return quotient, coarse_quotient, cw[0]
-
-    nothing = jnp.zeros(shape, f32)
-    loop(64, factors, (nothing, nothing, nothing))
-
-    def eliminate(source, inverse, back):
+        return quotient, coarse_quotient
+
+    loop(64, factors, (nothing, nothing), unroll=2)
+
+    def eliminate(source, inverse, back, parts):
         def step(x, state):
             scale, couple = inverse[x], back[x]
             after = []
-            for part in range(2):
+            for part in range(parts):
                 value = source[part, x] * scale + couple * state[part]
                 TY[part, x] = value
                 after.append(value)
             return tuple(after)
 
-        loop(64, step, (nothing, nothing), unroll=4)
-
-    def substitute(quotient, then):
+        loop(64, step, (nothing,) * parts, unroll=4)
+
+    def substitute(quotient, parts, then, unroll):
         def step(x, state):
             factor = quotient[x]
-            after = []
-            for part in range(2):
-                value = TY[part, x] + factor * state[part]
-                after.append(value)
-                then(part, x, value)
-            return tuple(after)
-
-        loop(64, step, (nothing, nothing), unroll=2, reverse=True)
+            after = tuple(TY[part, x] + factor * state[part] for part in range(parts))
+            then(x, *after)
+            return after
+
+        loop(64, step, (nothing,) * parts, unroll=unroll, reverse=True)
 
     def sides(v, w2, w3, by):
-        return ((w2 * y_next(v, by) + y_back(w2 * v, by)) + w3 * z_next(v, by)) + z_back(
-            w3 * v, by
+        return ((w3 * row_next(v, by) + row_back(w3 * v, by)) + w2 * lane_next(v, by)) + lane_back(
+            w2 * v, by
         )
 
-    def after_smoothing(part, x, value):
-        SM[part, x] = value
-        residue = sides(value, KW[1, x + 1], KW[2, x + 1], 1)
-        halved = residue + 0.5 * (y_back(residue) + y_next(residue))
-        CS[part, x] = halved + 0.5 * (z_back(halved) + z_next(halved))
-
-    def after_coarse(part, x, value):
-        CS[part, x] = CS[part, x] + sides(value, CW[0, x], CW[1, x], 2)
-
-    def after_correction(part, x, value):
-        rows = jnp.where(even_row, value, 0.5 * (y_back(value) + y_next(value)))
-        both = jnp.where(even_lane, rows, 0.5 * (z_back(rows) + z_next(rows)))
-        smoothed = SM[part, x] + both
-        CS[part, x] = NS[part, x] + sides(smoothed, KW[1, x + 1], KW[2, x + 1], 1)
-
-    def after_potential(part, x, value):
-        NS[part, x] = value
-
-    eliminate(NS, FI, FB)
-    substitute(FQ, after_smoothing)
-    eliminate(CS, CI, CB)
-    substitute(CQ, after_coarse)
-    eliminate(CS, CI, CB)
-    substitute(CQ, after_correction)
-    eliminate(CS, FI, FB)
-    substitute(FQ, after_potential)
+    def after_smoothing(x, *values):
+        halved = []
+        for part, value in enumerate(values):
+            SM[part, x] = value
+            residue = sides(value, KW[1, x + 1], KW[2, x + 1], 1)
+            halved.append(residue + 0.5 * (row_back(residue) + row_next(residue)))
+        merged = jnp.where(even_row, halved[0], row_back(halved[1]))
+        CS[0, x] = merged + 0.5 * (lane_back(merged) + lane_next(merged))
+
+    def after_coarse(x, value):
+        CS[0, x] = CS[0, x] + sides(value, CW[1, x + 1], CW[2, x + 1], 2)
+
+    def after_correction(x, value):
+        wide = jnp.where(even_lane, value, 0.5 * (lane_back(value) + lane_next(value)))
+        above = row_next(wide)
+        corrections = (
+            jnp.where(even_row, wide, 0.5 * (row_back(wide) + above)),
+            jnp.where(even_row, above, 0.5 * (wide + row_next(wide, 2))),
+        )
+        for part in range(2):
+            smoothed = SM[part, x] + corrections[part]
+            RH[part, x] = NS[part, x] + sides(smoothed, KW[1, x + 1], KW[2, x + 1], 1)
+
+    def after_potential(x, *values):
+        for part in range(2):
+            NS[part, x] = values[part]
+
+    eliminate(NS, FI, FB, 2)
+    substitute(FQ, 2, after_smoothing, 8)
+    eliminate(CS, CI, CB, 1)
+    substitute(CQ, 1, after_coarse, 8)
+    eliminate(CS, CI, CB, 1)
+    substitute(CQ, 1, after_correction, 8)
+    eliminate(RH, FI, FB, 2)
+    substitute(FQ, 2, after_potential, 4)
 
     def from_nodes(l, state):
         for part in range(2):
-            members = block_transpose([NS[part, 16 * g + l] for g in range(4)], DEPTH)
-            p0, p1, p2, p3 = members
+            p0, p1, p2, p3 = turned([NS[part, 16 * g + l] for g in range(4)])
             Rm[3 * part, l + 1] = p0
             Rm[3 * part + 1, l + 1] = p1
             for d, (g_part, h_part) in (
@@ -365,7 +375,7 @@
                 )
         return state
 
-    loop(16, from_nodes, 0)
+    loop(16, from_nodes, 0, unroll=4)
     for part in range(2):
         pad_high(Rm, 3 * part)
         pad_high(Rm, 3 * part + 1)
@@ -378,7 +388,7 @@
             E[3 * part, l + 1] = E[3 * part, l + 1] + (g_part + h_part) * W[7, l + 1]
         return state
 
-    loop(16, second_first, 0)
+    loop(16, second_first, 0, unroll=4)
     for field in range(6):
         pad_low(E, field)
         pad_high(E, field)
@@ -395,7 +405,7 @@
                 OUT[field, l] = value[TILE : 2 * TILE]
         return tuple(after)
 
-    loop(16, last_step, (side_fluxes(0, 0), side_fluxes(1, 0)))
+    loop(16, last_step, (side_fluxes(0, 0), side_fluxes(1, 0)), unroll=4)
 
     def gather_up(a, state):
         for part in range(2):
@@ -403,9 +413,10 @@
             for slot in range(16):
                 field, i = divmod(16 * part + slot, 4)
                 pieces.append(OUT[field, 4 * a + i] if field < 6 else zero8)
-            moved = block_transpose(pieces, TILE)
+            moved = jnp.concatenate(pieces, axis=0).T
             for g in range(4):
-                out[4 * g + a, TILE * part : TILE * part + TILE, :] = moved[4 * g + 1]
+                start = TILE * (4 * g + 1)
+                out[4 * g + a, TILE * part : TILE * part + TILE, :] = moved[start : start + TILE]
         return state
 
     loop(4, gather_up, 0)
@@ -457,7 +468,7 @@
             edge(3, 16),
             edge(6, 18),
             pltpu.VMEM((3, 65, ROWS, 128), f32),
-            pair,
+            pltpu.VMEM((3, 65, ROWS, 128), f32),
             line,
             line,
             line,
@@ -466,6 +477,7 @@
             line,
             pair,
             pair,
+            pltpu.VMEM((1, 64, ROWS, 128), f32),
             pair,
             pair,
             pltpu.VMEM((6, 16, TILE, 128), f32),

time: 168 us -> 136 us (0.81)
  Pallas kernels: 54.3 us -> 22.1 us
    pallas_call x1, Pallas kernels: 50.5 us -> 18.7 us  [lines(): pl.pallas_call(line_body, out_shape=jax.ShapeDtypeStruct((16, 2 * TILE, 1...]
where the time goes in v1:
time: 136 us
  blocking collectives  81.5 us (60%)
  Pallas kernels  22.1 us (16%)
  waiting for transfers between devices  19.5 us (14%)
  starting transfers between devices  12.7 us (9%)
    all_to_all x2, blocking collectives, swap(): return lax.all_to_all(values, 'gx', 0, 0, tiled=True)  81.5 us
    ppermute x4, waiting for transfers between devices, from_side(): return lax.ppermute(values, axes, pairs)  19.5 us
    pallas_call x1, Pallas kernels, lines(): pl.pallas_call(line_body, out_shape=jax.ShapeDtypeStruct((16, 2 * TILE, 1...  18.7 us
    ppermute x4, starting transfers between devices, from_side(): return lax.ppermute(values, axes, pairs)  12.7 us
  transfers between devices with their start and end apart: 4, of which 4 were waited for; matrix products, arithmetic and copies ran while one was open for 0% of the time, Pallas kernels for 0%

profile of v1, /device:TPU:86, one launch (start us, length us, event | category | flops | bytes accessed | tf_op | source)
XLA Modules:
  0.0 135.9 jit_solution(4469353017853141621)
XLA Ops:
  0.0 1.7 %pack.1 = f32[16,24,128]{2,1,0:T(8,128)} custom-call(f32[2,3,4,8,128]{4,3,2,1,0:T(8,128)} %residual.1, s32[4,8,128]{2,1,0:T(8,128)} %classes.1, s32[3,4,8,128]{3,2,1,0:T(8,128)} %edge_mask.1, f32[16]{0:T(128)} %class_weight.1), custom_call_target="tpu_custom_call" | custom-call | tf_op jit(solution)/shard_map/pack/pallas_call | solution.py:434
  1.7 59.9 %all_to_all.10 = f32[16,24,128]{2,1,0:T(8,128)S(1)} all-to-all(f32[16,24,128]{2,1,0:T(8,128)} %pack.1), channel_id=1, replica_groups=mesh['period'=2,'gx'=16,'gy'=8,'gz'=2] {'gx'}, dimensions={0} | all-to-all | bytes 393216 | tf_op jit(solution)/shard_map/all_to_all | solution.py:491
  61.6 4.8 %collective-permute-start = (f32[16,24,128]{2,1,0:T(8,128)S(1)}, f32[16,24,128]{2,1,0:T(8,128)S(1)}, u32[]{:S(2)}, u32[]{:S(2)}) collective-permute-start(f32[16,24,128]{2,1,0:T(8,128)S(1)} %all_to_all.10), channel_id=1, source_target_pairs={{0,2},{16,18},{32,34},{48,50},{64,66},{80,82},{96,98},{112,114},{1... | collective-permute-start | bytes 589832 | tf_op jit(solution)/shard_map/ppermute | solution.py:510
  66.4 2.0 %collective-permute-start.1 = (f32[16,24,128]{2,1,0:T(8,128)S(1)}, f32[16,24,128]{2,1,0:T(8,128)S(1)}, u32[]{:S(2)}, u32[]{:S(2)}) collective-permute-start(f32[16,24,128]{2,1,0:T(8,128)S(1)} %all_to_all.10), channel_id=1, source_target_pairs={{2,0},{18,16},{34,32},{50,48},{66,64},{82,80},{98,96},{114,112},{1... | collective-permute-start | bytes 589832 | tf_op jit(solution)/shard_map/ppermute | solution.py:510
  68.3 1.2 collective-permute-done
  69.6 5.6 %collective-permute-done.1 = f32[16,24,128]{2,1,0:T(8,128)S(1)} collective-permute-done((f32[16,24,128]{2,1,0:T(8,128)S(1)}, f32[16,24,128]{2,1,0:T(8,128)S(1)}, u32[]{:S(2)}, u32[]{:S(2)}) %collective-permute-start.1) | collective-permute-done | bytes 196640 | tf_op jit(solution)/shard_map/ppermute | solution.py:510
  75.2 1.3 collective-permute-start.3
  76.5 4.6 %collective-permute-start.2 = (f32[48,24,128]{2,1,0:T(8,128)S(1)}, f32[48,24,128]{2,1,0:T(8,128)S(1)}, u32[]{:S(2)}, u32[]{:S(2)}) collective-permute-start(f32[48,24,128]{2,1,0:T(8,128)S(1)} %constant_dynamic-update-slice_fusion.middle), channel_id=1, source_target_pairs={{0,16},{16,32},{32,48},{48,64},{64,80},{80,96},{96,112},{112,128},... | collective-permute-start | bytes 1769480 | tf_op jit(solution)/shard_map/ppermute | solution.py:510
  81.1 0.1 pad_add_fusion.place
  81.2 9.3 %collective-permute-done.3.deep = f32[48,24,128]{2,1,0:T(8,128)S(1)} collective-permute-done((f32[48,24,128]{2,1,0:T(8,128)S(1)}, f32[48,24,128]{2,1,0:T(8,128)S(1)}, u32[]{:S(2)}, u32[]{:S(2)}) %collective-permute-start.3) | collective-permute-done | bytes 589856 | tf_op jit(solution)/shard_map/ppermute | solution.py:510
  90.5 3.3 %collective-permute-done.2.shallow = f32[48,24,128]{2,1,0:T(8,128)S(1)} collective-permute-done((f32[48,24,128]{2,1,0:T(8,128)S(1)}, f32[48,24,128]{2,1,0:T(8,128)S(1)}, u32[]{:S(2)}, u32[]{:S(2)}) %collective-permute-start.2) | collective-permute-done | bytes 589856 | tf_op jit(solution)/shard_map/ppermute | solution.py:510
  93.9 18.7 %lines.1 = f32[16,16,128]{2,1,0:T(8,128)S(1)} custom-call(s32[4]{0:T(128)S(1)} %pad_add_fusion.place, f32[48,24,128]{2,1,0:T(8,128)S(1)} %constant_dynamic-update-slice_fusion.middle, f32[48,24,128]{2,1,0:T(8,128)S(1)} %collective-permute-done.2.shallow, f32[48,24,128]{2,1,0:T(8,128)S(1)} %collective-permute-done.3.deep), custom_call_target="tpu_custom_call" | custom-call | tf_op jit(solution)/shard_map/lines/pallas_call | solution.py:459
  112.6 21.6 %all_to_all.11.packed = f32[16,16,128]{2,1,0:T(8,128)} all-to-all(f32[16,16,128]{2,1,0:T(8,128)S(1)} %lines.1), channel_id=1, replica_groups=mesh['period'=2,'gx'=16,'gy'=8,'gz'=2] {'gx'}, dimensions={0} | all-to-all | bytes 262144 | tf_op jit(solution)/shard_map/all_to_all | solution.py:491
  134.2 1.6 %unpack.1 = f32[2,3,4,8,128]{4,3,2,1,0:T(8,128)} custom-call(f32[16,16,128]{2,1,0:T(8,128)} %all_to_all.11.packed), custom_call_target="tpu_custom_call" | custom-call | tf_op jit(solution)/shard_map/unpack/pallas_call | solution.py:445
  (3 shorter events, 0.0 us)
Async XLA Ops:
  61.6 7.9 %collective-permute-start = (f32[16,24,128]{2,1,0:T(8,128)S(1)}, f32[16,24,128]{2,1,0:T(8,128)S(1)}, u32[]{:S(2)}, u32[]{:S(2)}) collective-permute-start(f32[16,24,128]{2,1,0:T(8,128)S(1)} %all_to_all.10), channel_id=1, source_target_pairs={{0,2},{16,18},{32,34},{48,50},{64,66},{80,82},{96,98},{112,114},{1... | collective-permute-start | bytes 589832 | tf_op jit(solution)/shard_map/ppermute | solution.py:510
  66.4 8.8 %collective-permute-start.1 = (f32[16,24,128]{2,1,0:T(8,128)S(1)}, f32[16,24,128]{2,1,0:T(8,128)S(1)}, u32[]{:S(2)}, u32[]{:S(2)}) collective-permute-start(f32[16,24,128]{2,1,0:T(8,128)S(1)} %all_to_all.10), channel_id=1, source_target_pairs={{2,0},{18,16},{34,32},{50,48},{66,64},{82,80},{98,96},{114,112},{1... | collective-permute-start | bytes 589832 | tf_op jit(solution)/shard_map/ppermute | solution.py:510
  75.2 15.3 %collective-permute-start.3 = (f32[48,24,128]{2,1,0:T(8,128)S(1)}, f32[48,24,128]{2,1,0:T(8,128)S(1)}, u32[]{:S(2)}, u32[]{:S(2)}) collective-permute-start(f32[48,24,128]{2,1,0:T(8,128)S(1)} %constant_dynamic-update-slice_fusion.middle), channel_id=1, source_target_pairs={{16,0},{32,16},{48,32},{64,48},{80,64},{96,80},{112,96},{128,112},... | collective-permute-start | bytes 1769480 | tf_op jit(solution)/shard_map/ppermute | solution.py:510
  76.5 17.4 %collective-permute-start.2 = (f32[48,24,128]{2,1,0:T(8,128)S(1)}, f32[48,24,128]{2,1,0:T(8,128)S(1)}, u32[]{:S(2)}, u32[]{:S(2)}) collective-permute-start(f32[48,24,128]{2,1,0:T(8,128)S(1)} %constant_dynamic-update-slice_fusion.middle), channel_id=1, source_target_pairs={{0,16},{16,32},{32,48},{48,64},{64,80},{80,96},{96,112},{112,128},... | collective-permute-start | bytes 1769480 | tf_op jit(solution)/shard_map/ppermute | solution.py:510

commit v2 on v1

--- a/solution.py
+++ b/solution.py
@@ -1,11 +1,10 @@
-import functools
-
 import jax
 import jax.numpy as jnp
 from jax import lax
 from jax.experimental import pallas as pl
 from jax.experimental.pallas import tpu as pltpu
 from jax.sharding import PartitionSpec as P
+
 
 aspect = 2.0
 face_weight = (1.0 / (aspect * aspect), 1.0, 1.0)
@@ -23,7 +22,6 @@
 f32 = jnp.float32
 TILE = 8
 ROWS = 3 * TILE
-GROUPS = 4
 DEPTH = 32
 
 
@@ -69,9 +67,6 @@
 def pack_body(residual, classes, edge_mask, class_weight, out):
     thick = classes.shape[0]
     slots = []
-    for part in range(2):
-        for comp in range(3):
-            slots += [residual[part, comp, i] for i in range(thick)]
     for i in range(thick):
         labels = classes[i]
         cells = jnp.zeros(labels.shape, f32)
@@ -80,6 +75,9 @@
         slots.append(cells)
     for comp in range(3):
         slots += [(1 - edge_mask[comp, i]).astype(f32) for i in range(thick)]
+    for part in range(2):
+        for comp in range(3):
+            slots += [residual[part, comp, i] for i in range(thick)]
     zero = jnp.zeros((TILE, 128), f32)
     while len(slots) % 16:
         slots.append(zero)
@@ -102,59 +100,24 @@
                 out[field // 3, field % 3, i] = moved[TILE * slot : TILE * slot + TILE]
 
 
-def line_body(
-    place,
-    middle,
-    shallow,
-    deep,
-    out,
-    W,
-    E,
-    M,
-    Dm,
-    Rm,
-    KW,
-    CW,
-    FI,
-    FB,
-    FQ,
-    CI,
-    CB,
-    CQ,
-    NS,
-    SM,
-    CS,
-    TY,
-    RH,
-    OUT,
-):
-    extent_y, extent_z = place[2], place[3]
-    shape = (ROWS, 128)
-    lane = lanes(shape)
-    row = lax.broadcasted_iota(jnp.int32, shape, 0)
-    at_y = lane % DEPTH + place[0]
-    at_z = row + place[1]
-    inside = jnp.where(
-        (at_y >= 0) & (at_y < extent_y) & (at_z >= 0) & (at_z < extent_z), 1.0, 0.0
-    ).astype(f32)
-    coarse_inside = jnp.where(row % 2 == 0, inside, row_back(inside))
-    not_first = jnp.where(lane < DEPTH, 0.0, 1.0).astype(f32)
-    not_last = jnp.where(lane >= 128 - DEPTH, 0.0, 1.0).astype(f32)
-    even_row = row % 2 == 0
-    even_lane = lane % 2 == 0
-
-    def pad_low(ref, field):
-        ref[field, 0] = pltpu.roll(ref[field, 16], DEPTH, 1) * not_first
-
-    def pad_high(ref, field):
-        ref[field, 17] = pltpu.roll(ref[field, 1], 128 - DEPTH, 1) * not_last
-
+def pad_low(ref, field):
+    lane = lanes((ROWS, 128))
+    ref[field, 0] = jnp.where(lane < DEPTH, 0.0, pltpu.roll(ref[field, 16], DEPTH, 1))
+
+
+def pad_high(ref, field):
+    lane = lanes((ROWS, 128))
+    ref[field, 17] = jnp.where(
+        lane >= 128 - DEPTH, 0.0, pltpu.roll(ref[field, 1], 128 - DEPTH, 1)
+    )
+
+
+def spread_out(windows, parts, put):
     zero8 = jnp.zeros((TILE, 128), f32)
-    windows = (shallow, middle, deep)
-
-    def spread_out(a, state):
+
+    def step(a, state):
         for y in range(3):
-            for part in range(3):
+            for part in range(parts):
                 pieces = []
                 for p in range(16):
                     g, t = divmod(p, 4)
@@ -167,18 +130,39 @@
                 moved = jnp.concatenate(pieces, axis=0).T
                 for slot in range(16):
                     field, i = divmod(16 * part + slot, 4)
-                    if field < 10:
-                        W[field, 4 * a + i + 1, TILE * y : TILE * y + TILE, :] = moved[
-                            TILE * slot : TILE * slot + TILE
-                        ]
-        return state
-
-    loop(4, spread_out, 0)
-    pad_low(W, 6)
+                    put(field, 4 * a + i, y, moved[TILE * slot : TILE * slot + TILE])
+        return state
+
+    loop(4, step, 0, unroll=2)
+
+
+def setup_body(
+    place, middle, shallow, deep, free_out, M, Dm, KW, CW, FI, FB, FQ, CI, CB, CQ, cells
+):
+    extent_y, extent_z = place[2], place[3]
+    shape = (ROWS, 128)
+    lane = lanes(shape)
+    row = lax.broadcasted_iota(jnp.int32, shape, 0)
+    at_y = lane % DEPTH + place[0]
+    at_z = row + place[1]
+    inside = jnp.where(
+        (at_y >= 0) & (at_y < extent_y) & (at_z >= 0) & (at_z < extent_z), 1.0, 0.0
+    ).astype(f32)
+    coarse_inside = jnp.where(row % 2 == 0, inside, row_back(inside))
+    even_row = row % 2 == 0
+
+    def put(field, level, y, values):
+        if field == 0:
+            cells[0, level + 1, TILE * y : TILE * y + TILE, :] = values
+        else:
+            free_out[field - 1, level, TILE * y : TILE * y + TILE, :] = values
+
+    spread_out((shallow, middle, deep), 1, put)
+    pad_low(cells, 0)
 
     def coefficients(l, state):
-        c = W[6, l + 1]
-        cx = W[6, l]
+        c = cells[0, l + 1]
+        cx = cells[0, l]
         cy = y_back(c)
         cz = z_back(c)
         averages = (
@@ -187,80 +171,20 @@
             0.25 * (((c + cx) + cy) + y_back(cx)),
         )
         for d in range(3):
-            free = W[7 + d, l + 1]
+            free = free_out[d, l]
             masses = mass_factor[d] * averages[d] * free
             diagonal = stiff_weight[d] + masses
-            damp = edge_damping * free / diagonal
             M[d, l] = masses
-            Dm[d, l] = damp
-            for part in range(2):
-                source = W[3 * part + d, l + 1] * free
-                W[3 * part + d, l + 1] = source
-                E[3 * part + d, l + 1] = source * damp
+            Dm[d, l] = edge_damping * free / diagonal
             stiff = diagonal * free
             for g, values in enumerate(turned([masses, stiff, stiff, stiff])):
                 KW[d, 16 * g + l + 1] = values
         return state
 
-    loop(16, coefficients, 0, unroll=2)
+    loop(16, coefficients, 0, unroll=8)
 
     for d in range(3):
         KW[d, 0] = jnp.zeros(shape, f32)
-
-    def side_fluxes(part, l):
-        e1, e2, e3 = (E[3 * part + d, l] for d in range(3))
-        b2 = face_weight[1] * ((z_next(e1) - e1) - (E[3 * part + 2, l + 1] - e3))
-        b3 = face_weight[2] * ((E[3 * part + 1, l + 1] - e2) - (y_next(e1) - e1))
-        return b2, b3
-
-    def curl(part, l, before):
-        e1, e2, e3 = (E[3 * part + d, l] for d in range(3))
-        b2, b3 = side_fluxes(part, l)
-        b1 = face_weight[0] * ((y_next(e3) - e3) - (z_next(e2) - e2))
-        b2_before, b3_before = before
-        results = (
-            (z_back(b2) - b2) - (y_back(b3) - b3) + M[0, l - 1] * e1,
-            (b3_before - b3) - (z_back(b1) - b1) + M[1, l - 1] * e2,
-            (y_back(b1) - b1) - (b2_before - b2) + M[2, l - 1] * e3,
-        )
-        return results, (b2, b3)
-
-    for field in range(6):
-        pad_low(E, field)
-        pad_high(E, field)
-
-    def first_remainder(l, state):
-        after = []
-        for part in range(2):
-            results, fluxes = curl(part, l + 1, state[part])
-            after.append(fluxes)
-            for d in range(3):
-                Rm[3 * part + d, l + 1] = (
-                    W[3 * part + d, l + 1] - results[d] * W[7 + d, l + 1]
-                )
-        return tuple(after)
-
-    loop(16, first_remainder, (side_fluxes(0, 0), side_fluxes(1, 0)), unroll=4)
-    pad_low(Rm, 0)
-    pad_low(Rm, 3)
-
-    def to_nodes(l, state):
-        for part in range(2):
-            r1, r2, r3 = (Rm[3 * part + d, l + 1] for d in range(3))
-            r1b = Rm[3 * part, l]
-            r2b = y_back(r2)
-            r3b = z_back(r3)
-            members = [
-                ((r1b - r1) + (r2b - r2)) + (r3b - r3),
-                0.5 * (r1 + r1b),
-                0.5 * (r2 + r2b),
-                0.5 * (r3 + r3b),
-            ]
-            for g, values in enumerate(turned(members)):
-                NS[part, 16 * g + l] = values
-        return state
-
-    loop(16, to_nodes, 0, unroll=4)
 
     def diagonals(x, cw1_before):
         w1b, w1, w2, w3 = KW[0, x], KW[0, x + 1], KW[1, x + 1], KW[2, x + 1]
@@ -280,7 +204,7 @@
 
     nothing = jnp.zeros(shape, f32)
     CW[0, 0] = nothing
-    loop(64, diagonals, nothing, unroll=4)
+    loop(64, diagonals, nothing, unroll=8)
 
     def factors(x, state):
         fine_before, coarse_before = state
@@ -299,6 +223,103 @@
 
     loop(64, factors, (nothing, nothing), unroll=2)
 
+
+def line_body(
+    middle,
+    shallow,
+    deep,
+    free,
+    M,
+    Dm,
+    KW,
+    CW,
+    FI,
+    FB,
+    FQ,
+    CI,
+    CB,
+    CQ,
+    out,
+    W,
+    E,
+    Rm,
+    NS,
+    SM,
+    CS,
+    TY,
+    RH,
+    OUT,
+):
+    shape = (ROWS, 128)
+    even_row = lax.broadcasted_iota(jnp.int32, shape, 0) % 2 == 0
+    even_lane = lanes(shape) % 2 == 0
+    nothing = jnp.zeros(shape, f32)
+    zero8 = jnp.zeros((TILE, 128), f32)
+
+    def put(field, level, y, values):
+        if field < 6:
+            rows = slice(TILE * y, TILE * y + TILE)
+            source = values * free[field % 3, level, rows, :]
+            W[field, level, rows, :] = source
+            E[field, level + 1, rows, :] = source * Dm[field % 3, level, rows, :]
+
+    spread_out((shallow, middle, deep), 2, put)
+
+    def side_fluxes(part, l):
+        e1, e2, e3 = (E[3 * part + d, l] for d in range(3))
+        b2 = face_weight[1] * ((z_next(e1) - e1) - (E[3 * part + 2, l + 1] - e3))
+        b3 = face_weight[2] * ((E[3 * part + 1, l + 1] - e2) - (y_next(e1) - e1))
+        return b2, b3
+
+    def curl(part, l, before):
+        e1, e2, e3 = (E[3 * part + d, l] for d in range(3))
+        b2, b3 = side_fluxes(part, l)
+        b1 = face_weight[0] * ((y_next(e3) - e3) - (z_next(e2) - e2))
+        b2_before, b3_before = before
+        results = (
+            (z_back(b2) - b2) - (y_back(b3) - b3) + M[0, l - 1] * e1,
+            (b3_before - b3) - (z_back(b1) - b1) + M[1, l - 1] * e2,
+            (y_back(b1) - b1) - (b2_before - b2) + M[2, l - 1] * e3,
+        )
+        return results, (b2, b3)
+
+    for field in range(6):
+        pad_low(E, field)
+        pad_high(E, field)
+
+    def first_remainder(l, state):
+        after = []
+        for part in range(2):
+            results, fluxes = curl(part, l + 1, state[part])
+            after.append(fluxes)
+            for d in range(3):
+                Rm[3 * part + d, l + 1] = (
+                    W[3 * part + d, l] - results[d] * free[d, l]
+                )
+        return tuple(after)
+
+    loop(16, first_remainder, (side_fluxes(0, 0), side_fluxes(1, 0)), unroll=4)
+    pad_low(Rm, 0)
+    pad_low(Rm, 3)
+
+    def to_nodes(l, state):
+        for part in range(2):
+            r1, r2, r3 = (Rm[3 * part + d, l + 1] for d in range(3))
+            r1b = Rm[3 * part, l]
+            r2b = y_back(r2)
+            r3b = z_back(r3)
+            members = [
+                ((r1b - r1) + (r2b - r2)) + (r3b - r3),
+                0.5 * (r1 + r1b),
+                0.5 * (r2 + r2b),
+                0.5 * (r3 + r3b),
+            ]
+            for g, values in enumerate(turned(members)):
+                NS[part, 16 * g + l] = values
+        return state
+
+    loop(16, to_nodes, 0, unroll=8)
+
     def eliminate(source, inverse, back, parts):
         def step(x, state):
             scale, couple = inverse[x], back[x]
@@ -355,7 +376,7 @@
     eliminate(NS, FI, FB, 2)
     substitute(FQ, 2, after_smoothing, 8)
     eliminate(CS, CI, CB, 1)
-    substitute(CQ, 1, after_coarse, 8)
+    substitute(CQ, 1, after_coarse, 16)
     eliminate(CS, CI, CB, 1)
     substitute(CQ, 1, after_correction, 8)
     eliminate(RH, FI, FB, 2)
@@ -371,11 +392,11 @@
                 (2, (z_next(p0) - p0, 0.5 * (p3 + z_next(p3)))),
             ):
                 E[3 * part + d, l + 1] = (
-                    E[3 * part + d, l + 1] + (g_part + h_part) * W[7 + d, l + 1]
+                    E[3 * part + d, l + 1] + (g_part + h_part) * free[d, l]
                 )
         return state
 
-    loop(16, from_nodes, 0, unroll=4)
+    loop(16, from_nodes, 0, unroll=8)
     for part in range(2):
         pad_high(Rm, 3 * part)
         pad_high(Rm, 3 * part + 1)
@@ -385,7 +406,7 @@
             p0, p1 = Rm[3 * part, l + 1], Rm[3 * part + 1, l + 1]
             g_part = Rm[3 * part, l + 2] - p0
             h_part = 0.5 * (p1 + Rm[3 * part + 1, l + 2])
-            E[3 * part, l + 1] = E[3 * part, l + 1] + (g_part + h_part) * W[7, l + 1]
+            E[3 * part, l + 1] = E[3 * part, l + 1] + (g_part + h_part) * free[0, l]
         return state
 
     loop(16, second_first, 0, unroll=4)
@@ -400,12 +421,12 @@
             after.append(fluxes)
             for d in range(3):
                 field = 3 * part + d
-                remainder = W[field, l + 1] - results[d] * W[7 + d, l + 1]
+                remainder = W[field, l] - results[d] * free[d, l]
                 value = E[field, l + 1] + Dm[d, l] * remainder
                 OUT[field, l] = value[TILE : 2 * TILE]
         return tuple(after)
 
-    loop(16, last_step, (side_fluxes(0, 0), side_fluxes(1, 0)), unroll=4)
+    loop(16, last_step, (side_fluxes(0, 0), side_fluxes(1, 0)), unroll=8)
 
     def gather_up(a, state):
         for part in range(2):
@@ -452,39 +473,47 @@
     )(packed)
 
 
-def lines(place, middle, shallow, deep, **options):
-    edge = lambda count, levels: pltpu.VMEM((count, levels, ROWS, 128), f32)
-    line = pltpu.VMEM((64, ROWS, 128), f32)
-    pair = pltpu.VMEM((2, 64, ROWS, 128), f32)
+def resident(*shape):
+    return pltpu.VMEM(shape, f32)
+
+
+def setup(place, middle, shallow, deep, **options):
+    line = resident(64, ROWS, 128)
+    edge = resident(3, 16, ROWS, 128)
+    weights = resident(3, 65, ROWS, 128)
+    return pl.pallas_call(
+        setup_body,
+        out_shape=[edge, edge, edge, weights, weights] + [line] * 6,
+        in_specs=[smem(), vmem(), vmem(), vmem()],
+        out_specs=[vmem()] * 11,
+        scratch_shapes=[resident(1, 18, ROWS, 128)],
+        name="setup",
+        **options,
+    )(place, middle, shallow, deep)
+
+
+def lines(middle, shallow, deep, ready, **options):
+    edge = lambda count, levels: resident(count, levels, ROWS, 128)
+    pair = resident(2, 64, ROWS, 128)
     return pl.pallas_call(
         line_body,
         out_shape=jax.ShapeDtypeStruct((16, 2 * TILE, 128), f32),
-        in_specs=[smem(), vmem(), vmem(), vmem()],
+        in_specs=[vmem()] * (3 + len(ready)),
         out_specs=vmem(),
         scratch_shapes=[
-            edge(10, 18),
+            edge(6, 16),
             edge(6, 18),
-            edge(3, 16),
-            edge(3, 16),
             edge(6, 18),
-            pltpu.VMEM((3, 65, ROWS, 128), f32),
-            pltpu.VMEM((3, 65, ROWS, 128), f32),
-            line,
-            line,
-            line,
-            line,
-            line,
-            line,
             pair,
             pair,
-            pltpu.VMEM((1, 64, ROWS, 128), f32),
+            resident(1, 64, ROWS, 128),
             pair,
             pair,
-            pltpu.VMEM((6, 16, TILE, 128), f32),
+            resident(6, 16, TILE, 128),
         ],
         name="lines",
         **options,
-    )(place, middle, shallow, deep)
+    )(middle, shallow, deep, *ready)
 
 
 def swap(values):
@@ -518,8 +547,11 @@
         )
     )
     middle = jnp.concatenate([from_side(own, 1, 0), own, from_side(own, -1, 0)], axis=0)
-    shallow = from_side(middle, 0, 1)
-    deep = from_side(middle, 0, -1)
+    material, source = middle[:, :TILE], middle[:, TILE:]
+    shallow_material = from_side(material, 0, 1)
+    deep_material = from_side(material, 0, -1)
+    shallow_source = from_side(source, 0, 1)
+    deep_source = from_side(source, 0, -1)
     tile = lax.axis_index("gz") * size_x + lax.axis_index("gx")
     place = jnp.stack(
         [
@@ -529,8 +561,14 @@
             jnp.int32(tiles * TILE),
         ]
     ).astype(jnp.int32)
-    options = dict(compiler_params=pltpu.CompilerParams(vmem_limit_bytes=50 * 2**20))
-    result = swap(lines(place, middle, shallow, deep, **options))
+    options = lambda size, cost: dict(
+        compiler_params=pltpu.CompilerParams(vmem_limit_bytes=size * 2**20),
+        cost_estimate=pl.CostEstimate(flops=cost, bytes_accessed=0, transcendentals=0),
+    )
+    ready = setup(
+        place, material, shallow_material, deep_material, **options(20, 2**27)
+    )
+    result = swap(lines(source, shallow_source, deep_source, ready, **options(32, 2**27)))
     return unpack(result, residual.shape)
 
 

time: 136 us -> 132 us (0.971)
  waiting for transfers between devices: 19.5 us -> 14.4 us
  starting transfers between devices: 12.7 us -> 17.7 us
  Pallas kernels: 22.1 us -> 19.7 us
  blocking collectives: 81.5 us -> 79.4 us
    pallas_call x1, Pallas kernels: 18.7 us -> 11.5 us  [lines(): pl.pallas_call(line_body, out_shape=jax.ShapeDtypeStruct((16, 2 * TILE, 1...]
    ppermute x4 -> x6, starting transfers between devices: 12.7 us -> 17.7 us  [from_side(): return lax.ppermute(values, axes, pairs)]
    ppermute x4 -> x6, waiting for transfers between devices: 19.5 us -> 14.4 us  [from_side(): return lax.ppermute(values, axes, pairs)]
    pallas_call x0 -> x1, Pallas kernels: none -> 4.87 us  [setup(): pl.pallas_call(setup_body, out_shape=[edge, edge, edge, weights, weights]...]
    all_to_all x2, blocking collectives: 81.5 us -> 79.4 us  [swap(): return lax.all_to_all(values, 'gx', 0, 0, tiled=True)]
  transfers between devices with their start and end apart: 4 -> 6, of which waited for: 4 -> 4; matrix products, arithmetic and copies ran while one was open for 0% -> 0% of each run, Pallas kernels for 0% -> 4%
where the time goes in v2:
time: 132 us
  blocking collectives  79.4 us (60%)
  Pallas kernels  19.7 us (15%)
  starting transfers between devices  17.7 us (13%)
  waiting for transfers between devices  14.4 us (11%)
    all_to_all x2, blocking collectives, swap(): return lax.all_to_all(values, 'gx', 0, 0, tiled=True)  79.4 us
    ppermute x6, starting transfers between devices, from_side(): return lax.ppermute(values, axes, pairs)  17.7 us
    ppermute x6, waiting for transfers between devices, from_side(): return lax.ppermute(values, axes, pairs)  14.4 us
    pallas_call x1, Pallas kernels, lines(): pl.pallas_call(line_body, out_shape=jax.ShapeDtypeStruct((16, 2 * TILE, 1...  11.5 us
    pallas_call x1, Pallas kernels, setup(): pl.pallas_call(setup_body, out_shape=[edge, edge, edge, weights, weights]...  4.87 us
  transfers between devices with their start and end apart: 6, of which 4 were waited for; matrix products, arithmetic and copies ran while one was open for 0% of the time, Pallas kernels for 4%

profile of v2, /device:TPU:86, one launch (start us, length us, event | category | flops | bytes accessed | tf_op | source)
XLA Modules:
  0.0 131.5 jit_solution(6705995545204878568)
XLA Ops:
  0.0 1.7 %pack.1 = f32[16,24,128]{2,1,0:T(8,128)} custom-call(f32[2,3,4,8,128]{4,3,2,1,0:T(8,128)} %residual.1, s32[4,8,128]{2,1,0:T(8,128)} %classes.1, s32[3,4,8,128]{3,2,1,0:T(8,128)} %edge_mask.1, f32[16]{0:T(128)} %class_weight.1), custom_call_target="tpu_custom_call" | custom-call | tf_op jit(solution)/shard_map/pack/pallas_call | solution.py:455
  1.7 59.9 %all_to_all.10 = f32[16,24,128]{2,1,0:T(8,128)S(1)} all-to-all(f32[16,24,128]{2,1,0:T(8,128)} %pack.1), channel_id=1, replica_groups=mesh['period'=2,'gx'=16,'gy'=8,'gz'=2] {'gx'}, dimensions={0} | all-to-all | bytes 393216 | tf_op jit(solution)/shard_map/all_to_all | solution.py:520
  61.6 4.8 %collective-permute-start = (f32[16,24,128]{2,1,0:T(8,128)S(1)}, f32[16,24,128]{2,1,0:T(8,128)S(1)}, u32[]{:S(2)}, u32[]{:S(2)}) collective-permute-start(f32[16,24,128]{2,1,0:T(8,128)S(1)} %all_to_all.10), channel_id=1, source_target_pairs={{0,2},{16,18},{32,34},{48,50},{64,66},{80,82},{96,98},{112,114},{1... | collective-permute-start | bytes 589832 | tf_op jit(solution)/shard_map/ppermute | solution.py:539
  66.4 2.0 %collective-permute-start.1 = (f32[16,24,128]{2,1,0:T(8,128)S(1)}, f32[16,24,128]{2,1,0:T(8,128)S(1)}, u32[]{:S(2)}, u32[]{:S(2)}) collective-permute-start(f32[16,24,128]{2,1,0:T(8,128)S(1)} %all_to_all.10), channel_id=1, source_target_pairs={{2,0},{18,16},{34,32},{50,48},{66,64},{82,80},{98,96},{114,112},{1... | collective-permute-start | bytes 589832 | tf_op jit(solution)/shard_map/ppermute | solution.py:539
  68.3 1.2 collective-permute-done
  69.6 5.6 %collective-permute-done.1 = f32[16,24,128]{2,1,0:T(8,128)S(1)} collective-permute-done((f32[16,24,128]{2,1,0:T(8,128)S(1)}, f32[16,24,128]{2,1,0:T(8,128)S(1)}, u32[]{:S(2)}, u32[]{:S(2)}) %collective-permute-start.1) | collective-permute-done | bytes 196640 | tf_op jit(solution)/shard_map/ppermute | solution.py:539
  75.2 3.8 %collective-permute-start.2 = (f32[48,16,128]{2,1,0:T(8,128)S(1)}, f32[48,16,128]{2,1,0:T(8,128)S(1)}, u32[]{:S(2)}, u32[]{:S(2)}) collective-permute-start(f32[48,16,128]{2,1,0:T(8,128)S(1)} %slice.8.middle), channel_id=1, source_target_pairs={{0,16},{16,32},{32,48},{48,64},{64,80},{80,96},{96,112},{112,128},... | collective-permute-start | bytes 1179656 | tf_op jit(solution)/shard_map/ppermute | solution.py:539
  79.0 1.3 collective-permute-start.3
  80.3 4.6 %collective-permute-start.4 = (f32[48,8,128]{2,1,0:T(8,128)S(1)}, f32[48,8,128]{2,1,0:T(8,128)S(1)}, u32[]{:S(2)}, u32[]{:S(2)}) collective-permute-start(f32[48,8,128]{2,1,0:T(8,128)S(1)} %slice.9.middle), channel_id=1, source_target_pairs={{0,16},{16,32},{32,48},{48,64},{64,80},{80,96},{96,112},{112,128},... | collective-permute-start | bytes 589832 | tf_op jit(solution)/shard_map/ppermute | solution.py:539
  85.0 1.3 collective-permute-start.5
  86.3 0.1 pad_add_fusion.place
  86.4 3.5 %collective-permute-done.4.shallow = f32[48,8,128]{2,1,0:T(8,128)S(1)} collective-permute-done((f32[48,8,128]{2,1,0:T(8,128)S(1)}, f32[48,8,128]{2,1,0:T(8,128)S(1)}, u32[]{:S(2)}, u32[]{:S(2)}) %collective-permute-start.4) | collective-permute-done | bytes 196640 | tf_op jit(solution)/shard_map/ppermute | solution.py:539
  89.8 4.1 %collective-permute-done.5.deep = f32[48,8,128]{2,1,0:T(8,128)S(1)} collective-permute-done((f32[48,8,128]{2,1,0:T(8,128)S(1)}, f32[48,8,128]{2,1,0:T(8,128)S(1)}, u32[]{:S(2)}, u32[]{:S(2)}) %collective-permute-start.5) | collective-permute-done | bytes 196640 | tf_op jit(solution)/shard_map/ppermute | solution.py:539
  94.0 4.9 %setup.1 = (f32[3,16,24,128]{3,2,1,0:T(8,128)S(1)}, f32[3,16,24,128]{3,2,1,0:T(8,128)S(1)}, f32[3,16,24,128]{3,2,1,0:T(8,128)S(1)}, f32[3,65,24,128]{3,2,1,0:T(8...) custom-call(s32[4]{0:T(128)S(1)} %pad_add_fusion.place, ...), custom_call_target="tpu_custom_call" | custom-call | flops 134217728 | tf_op jit(solution)/shard_map/setup/pallas_call | solution.py:484
  98.9 0.0 collective-permute-done.2.shallow
  98.9 0.0 collective-permute-done.3.deep
  98.9 11.5 %lines.1 = f32[16,16,128]{2,1,0:T(8,128)S(1)} custom-call(f32[48,16,128]{2,1,0:T(8,128)S(1)} %slice.8.middle, f32[48,16,128]{2,1,0:T(8,128)S(1)} %collective-permute-done.2.shallow, f32[48,16,128]{2,1,0:T(8,128)S(1)} %collective-permute-done.3.deep, f32[3,16,24,128]{3,2,1,0:T(8,128)S(1)} %get-tuple-element.16.free, ...), custom_call_target="tpu_custom_call" | custom-call | flops 134217728 | tf_op jit(solution)/shard_map/lines/pallas_call | solution.py:498
  110.4 19.5 %all_to_all.11.packed = f32[16,16,128]{2,1,0:T(8,128)} all-to-all(f32[16,16,128]{2,1,0:T(8,128)S(1)} %lines.1), channel_id=1, replica_groups=mesh['period'=2,'gx'=16,'gy'=8,'gz'=2] {'gx'}, dimensions={0} | all-to-all | bytes 262144 | tf_op jit(solution)/shard_map/all_to_all | solution.py:520
  129.9 1.6 %unpack.1 = f32[2,3,4,8,128]{4,3,2,1,0:T(8,128)} custom-call(f32[16,16,128]{2,1,0:T(8,128)} %all_to_all.11.packed), custom_call_target="tpu_custom_call" | custom-call | tf_op jit(solution)/shard_map/unpack/pallas_call | solution.py:466
  (5 shorter events, 0.1 us)
Async XLA Ops:
  61.6 7.9 %collective-permute-start = (f32[16,24,128]{2,1,0:T(8,128)S(1)}, f32[16,24,128]{2,1,0:T(8,128)S(1)}, u32[]{:S(2)}, u32[]{:S(2)}) collective-permute-start(f32[16,24,128]{2,1,0:T(8,128)S(1)} %all_to_all.10), channel_id=1, source_target_pairs={{0,2},{16,18},{32,34},{48,50},{64,66},{80,82},{96,98},{112,114},{1... | collective-permute-start | bytes 589832 | tf_op jit(solution)/shard_map/ppermute | solution.py:539
  66.4 8.8 %collective-permute-start.1 = (f32[16,24,128]{2,1,0:T(8,128)S(1)}, f32[16,24,128]{2,1,0:T(8,128)S(1)}, u32[]{:S(2)}, u32[]{:S(2)}) collective-permute-start(f32[16,24,128]{2,1,0:T(8,128)S(1)} %all_to_all.10), channel_id=1, source_target_pairs={{2,0},{18,16},{34,32},{50,48},{66,64},{82,80},{98,96},{114,112},{1... | collective-permute-start | bytes 589832 | tf_op jit(solution)/shard_map/ppermute | solution.py:539
  75.2 23.6 %collective-permute-start.2 = (f32[48,16,128]{2,1,0:T(8,128)S(1)}, f32[48,16,128]{2,1,0:T(8,128)S(1)}, u32[]{:S(2)}, u32[]{:S(2)}) collective-permute-start(f32[48,16,128]{2,1,0:T(8,128)S(1)} %slice.8.middle), channel_id=1, source_target_pairs={{0,16},{16,32},{32,48},{48,64},{64,80},{80,96},{96,112},{112,128},... | collective-permute-start | bytes 1179656 | tf_op jit(solution)/shard_map/ppermute | solution.py:539
  79.0 19.9 %collective-permute-start.3 = (f32[48,16,128]{2,1,0:T(8,128)S(1)}, f32[48,16,128]{2,1,0:T(8,128)S(1)}, u32[]{:S(2)}, u32[]{:S(2)}) collective-permute-start(f32[48,16,128]{2,1,0:T(8,128)S(1)} %slice.8.middle), channel_id=1, source_target_pairs={{16,0},{32,16},{48,32},{64,48},{80,64},{96,80},{112,96},{128,112},... | collective-permute-start | bytes 1179656 | tf_op jit(solution)/shard_map/ppermute | solution.py:539
  80.3 9.5 %collective-permute-start.4 = (f32[48,8,128]{2,1,0:T(8,128)S(1)}, f32[48,8,128]{2,1,0:T(8,128)S(1)}, u32[]{:S(2)}, u32[]{:S(2)}) collective-permute-start(f32[48,8,128]{2,1,0:T(8,128)S(1)} %slice.9.middle), channel_id=1, source_target_pairs={{0,16},{16,32},{32,48},{48,64},{64,80},{80,96},{96,112},{112,128},... | collective-permute-start | bytes 589832 | tf_op jit(solution)/shard_map/ppermute | solution.py:539
  85.0 9.0 %collective-permute-start.5 = (f32[48,8,128]{2,1,0:T(8,128)S(1)}, f32[48,8,128]{2,1,0:T(8,128)S(1)}, u32[]{:S(2)}, u32[]{:S(2)}) collective-permute-start(f32[48,8,128]{2,1,0:T(8,128)S(1)} %slice.9.middle), channel_id=1, source_target_pairs={{16,0},{32,16},{48,32},{64,48},{80,64},{96,80},{112,96},{128,112},... | collective-permute-start | bytes 589832 | tf_op jit(solution)/shard_map/ppermute | solution.py:539

commit v3 on v2

--- a/solution.py
+++ b/solution.py
@@ -23,6 +23,7 @@
 TILE = 8
 ROWS = 3 * TILE
 DEPTH = 32
+HALF = TILE // 2
 
 
 def lanes(shape):
@@ -78,26 +79,49 @@
     for part in range(2):
         for comp in range(3):
             slots += [residual[part, comp, i] for i in range(thick)]
-    zero = jnp.zeros((TILE, 128), f32)
-    while len(slots) % 16:
-        slots.append(zero)
-    for part in range(len(slots) // 16):
-        moved = jnp.concatenate(slots[16 * part : 16 * part + 16], axis=0).T
-        for target in range(16):
-            out[target, TILE * part : TILE * part + TILE, :] = moved[
-                TILE * target : TILE * target + TILE
-            ]
+    block = 0
+    for start in range(0, len(slots), 16):
+        group = jnp.concatenate(slots[start : start + 16], axis=0)
+        block = send_group(group, lambda target: target, out, block)
+
+
+def send_group(group, device, out, block):
+    half = HALF
+    if group.shape[0] == 128:
+        moved = group.T
+        parts = 2
+    else:
+        moved = jnp.concatenate([group, pltpu.roll(group, 128 - half, 1)], axis=0).T
+        parts = 1
+    for target in range(16):
+        place = device(target)
+        if place is not None:
+            for part in range(parts):
+                row = TILE * target + half * part
+                out[place, block + part] = moved[row : row + half]
+    return block + parts
+
+
+def receive_group(blocks, block, full):
+    half = HALF
+    gap = jnp.zeros((half, 128), f32)
+    rows = []
+    for source in range(16):
+        rows.append(blocks(source, block))
+        rows.append(blocks(source, block + 1) if full else gap)
+    moved = jnp.concatenate(rows, axis=0).T
+    if full:
+        return moved
+    upper = pltpu.roll(moved[64:], half, 1)
+    return jnp.where(lanes((64, 128)) % TILE < half, moved[:64], upper)
 
 
 def unpack_body(packed, out):
     for part in range(2):
-        moved = jnp.concatenate(
-            [packed[source, TILE * part : TILE * part + TILE, :] for source in range(16)], axis=0
-        ).T
-        for slot in range(16):
+        moved = receive_group(lambda source, block: packed[source, block], 2 * part, part == 0)
+        for slot in range(moved.shape[0] // TILE):
             field, i = divmod(16 * part + slot, 4)
-            if field < 6:
-                out[field // 3, field % 3, i] = moved[TILE * slot : TILE * slot + TILE]
+            out[field // 3, field % 3, i] = moved[TILE * slot : TILE * slot + TILE]
 
 
 def pad_low(ref, field):
@@ -112,23 +136,22 @@
     )
 
 
-def spread_out(windows, parts, put):
-    zero8 = jnp.zeros((TILE, 128), f32)
+def spread_out(windows, groups, put):
+    gap = jnp.zeros((HALF, 128), f32)
 
     def step(a, state):
         for y in range(3):
-            for part in range(parts):
-                pieces = []
-                for p in range(16):
+            for part, full in enumerate(groups):
+
+                def blocks(p, block):
                     g, t = divmod(p, 4)
                     if t == 3:
-                        pieces.append(zero8)
-                    else:
-                        pieces.append(
-                            windows[t][y * 16 + 4 * g + a, TILE * part : TILE * part + TILE, :]
-                        )
-                moved = jnp.concatenate(pieces, axis=0).T
-                for slot in range(16):
+                        return gap
+                    ref, first = windows[t]
+                    return ref[y * 16 + 4 * g + a, first + block]
+
+                moved = receive_group(blocks, 2 * part, full)
+                for slot in range(moved.shape[0] // TILE):
                     field, i = divmod(16 * part + slot, 4)
                     put(field, 4 * a + i, y, moved[TILE * slot : TILE * slot + TILE])
         return state
@@ -157,7 +180,7 @@
         else:
             free_out[field - 1, level, TILE * y : TILE * y + TILE, :] = values
 
-    spread_out((shallow, middle, deep), 1, put)
+    spread_out(((shallow, 0), (middle, 0), (deep, 0)), (True,), put)
     pad_low(cells, 0)
 
     def coefficients(l, state):
@@ -254,16 +277,14 @@
     even_row = lax.broadcasted_iota(jnp.int32, shape, 0) % 2 == 0
     even_lane = lanes(shape) % 2 == 0
     nothing = jnp.zeros(shape, f32)
-    zero8 = jnp.zeros((TILE, 128), f32)
 
     def put(field, level, y, values):
-        if field < 6:
-            rows = slice(TILE * y, TILE * y + TILE)
-            source = values * free[field % 3, level, rows, :]
-            W[field, level, rows, :] = source
-            E[field, level + 1, rows, :] = source * Dm[field % 3, level, rows, :]
-
-    spread_out((shallow, middle, deep), 2, put)
+        rows = slice(TILE * y, TILE * y + TILE)
+        source = values * free[field % 3, level, rows, :]
+        W[field, level, rows, :] = source
+        E[field, level + 1, rows, :] = source * Dm[field % 3, level, rows, :]
+
+    spread_out(((shallow, 0), (middle, 2), (deep, 0)), (True, False), put)
 
     def side_fluxes(part, l):
         e1, e2, e3 = (E[3 * part + d, l] for d in range(3))
@@ -429,15 +450,13 @@
     loop(16, last_step, (side_fluxes(0, 0), side_fluxes(1, 0)), unroll=8)
 
     def gather_up(a, state):
-        for part in range(2):
-            pieces = []
-            for slot in range(16):
-                field, i = divmod(16 * part + slot, 4)
-                pieces.append(OUT[field, 4 * a + i] if field < 6 else zero8)
-            moved = jnp.concatenate(pieces, axis=0).T
-            for g in range(4):
-                start = TILE * (4 * g + 1)
-                out[4 * g + a, TILE * part : TILE * part + TILE, :] = moved[start : start + TILE]
+        slots = [OUT[field, 4 * a + i] for field in range(6) for i in range(4)]
+        block = 0
+        for start in (0, 16):
+            group = jnp.concatenate(slots[start : start + 16], axis=0)
+            block = send_group(
+                group, lambda p: p // 4 * 4 + a if p % 4 == 1 else None, out, block
+            )
         return state
 
     loop(4, gather_up, 0)
@@ -454,7 +473,7 @@
 def pack(residual, classes, edge_mask, class_weight, **options):
     return pl.pallas_call(
         pack_body,
-        out_shape=jax.ShapeDtypeStruct((16, ROWS, 128), f32),
+        out_shape=resident(16, 5, HALF, 128),
         in_specs=[vmem(), vmem(), vmem(), smem()],
         out_specs=vmem(),
         name="pack",
@@ -497,7 +516,7 @@
     pair = resident(2, 64, ROWS, 128)
     return pl.pallas_call(
         line_body,
-        out_shape=jax.ShapeDtypeStruct((16, 2 * TILE, 128), f32),
+        out_shape=resident(16, 3, HALF, 128),
         in_specs=[vmem()] * (3 + len(ready)),
         out_specs=vmem(),
         scratch_shapes=[
@@ -547,7 +566,7 @@
         )
     )
     middle = jnp.concatenate([from_side(own, 1, 0), own, from_side(own, -1, 0)], axis=0)
-    material, source = middle[:, :TILE], middle[:, TILE:]
+    material, source = middle[:, :2], middle[:, 2:]
     shallow_material = from_side(material, 0, 1)
     deep_material = from_side(material, 0, -1)
     shallow_source = from_side(source, 0, 1)
@@ -565,10 +584,8 @@
         compiler_params=pltpu.CompilerParams(vmem_limit_bytes=size * 2**20),
         cost_estimate=pl.CostEstimate(flops=cost, bytes_accessed=0, transcendentals=0),
     )
-    ready = setup(
-        place, material, shallow_material, deep_material, **options(20, 2**27)
-    )
-    result = swap(lines(source, shallow_source, deep_source, ready, **options(32, 2**27)))
+    ready = setup(place, middle, shallow_material, deep_material, **options(20, 2**27))
+    result = swap(lines(middle, shallow_source, deep_source, ready, **options(32, 2**27)))
     return unpack(result, residual.shape)
 
 

time: 132 us -> 129 us (0.977)
  the two profiles are of different devices: /device:TPU:86 before, /device:TPU:70 now
where the time goes in v3:
time: 129 us
  blocking collectives  78.2 us (61%)
  Pallas kernels  19.6 us (15%)
  starting transfers between devices  17.3 us (13%)
  waiting for transfers between devices  13.5 us (10%)
    all_to_all x2, blocking collectives, swap(): return lax.all_to_all(values, 'gx', 0, 0, tiled=True)  78.2 us
    ppermute x6, starting transfers between devices, from_side(): return lax.ppermute(values, axes, pairs)  17.3 us
    ppermute x6, waiting for transfers between devices, from_side(): return lax.ppermute(values, axes, pairs)  13.5 us
    pallas_call x1, Pallas kernels, lines(): pl.pallas_call(line_body, out_shape=resident(16, 3, HALF, 128), in_specs=...  11.9 us
    pallas_call x1, Pallas kernels, setup(): pl.pallas_call(setup_body, out_shape=[edge, edge, edge, weights, weights]...  4.87 us
  transfers between devices with their start and end apart: 6, of which 4 were waited for; matrix products, arithmetic and copies ran while one was open for 0% of the time, Pallas kernels for 4%

profile of v3, /device:TPU:70, one launch (start us, length us, event | category | flops | bytes accessed | tf_op | source)
XLA Modules:
  0.0 128.8 jit_solution(14523704589936726176)
XLA Ops:
  0.0 1.1 pack.1
  1.1 58.8 %all_to_all.10 = f32[16,5,4,128]{3,2,1,0:T(4,128)S(1)} all-to-all(f32[16,5,4,128]{3,2,1,0:T(4,128)S(1)} %pack.1), channel_id=1, replica_groups=mesh['period'=2,'gx'=16,'gy'=8,'gz'=2] {'gx'}, dimensions={0} | all-to-all | bytes 327680 | tf_op jit(solution)/shard_map/all_to_all | solution.py:539
  59.9 4.8 %collective-permute-start = (f32[16,5,4,128]{3,2,1,0:T(4,128)S(1)}, f32[16,5,4,128]{3,2,1,0:T(4,128)S(1)}, u32[]{:S(2)}, u32[]{:S(2)}) collective-permute-start(f32[16,5,4,128]{3,2,1,0:T(4,128)S(1)} %all_to_all.10), channel_id=1, source_target_pairs={{0,2},{16,18},{32,34},{48,50},{64,66},{80,82},{96,98},{112,114},{1... | collective-permute-start | bytes 491528 | tf_op jit(solution)/shard_map/ppermute | solution.py:558
  64.6 2.0 %collective-permute-start.1 = (f32[16,5,4,128]{3,2,1,0:T(4,128)S(1)}, f32[16,5,4,128]{3,2,1,0:T(4,128)S(1)}, u32[]{:S(2)}, u32[]{:S(2)}) collective-permute-start(f32[16,5,4,128]{3,2,1,0:T(4,128)S(1)} %all_to_all.10), channel_id=1, source_target_pairs={{2,0},{18,16},{34,32},{50,48},{66,64},{82,80},{98,96},{114,112},{1... | collective-permute-start | bytes 491528 | tf_op jit(solution)/shard_map/ppermute | solution.py:558
  66.6 0.9 collective-permute-done
  67.5 5.6 %collective-permute-done.1 = f32[16,5,4,128]{3,2,1,0:T(4,128)S(1)} collective-permute-done((f32[16,5,4,128]{3,2,1,0:T(4,128)S(1)}, f32[16,5,4,128]{3,2,1,0:T(4,128)S(1)}, u32[]{:S(2)}, u32[]{:S(2)}) %collective-permute-start.1) | collective-permute-done | bytes 163872 | tf_op jit(solution)/shard_map/ppermute | solution.py:558
  73.2 3.4 %collective-permute-start.2 = (f32[48,3,4,128]{3,2,1,0:T(4,128)S(1)}, f32[48,3,4,128]{3,2,1,0:T(4,128)S(1)}, u32[]{:S(2)}, u32[]{:S(2)}) collective-permute-start(f32[48,3,4,128]{3,2,1,0:T(4,128)S(1)} %slice.8), channel_id=1, source_target_pairs={{0,16},{16,32},{32,48},{48,64},{64,80},{80,96},{96,112},{112,128},... | collective-permute-start | bytes 884744 | tf_op jit(solution)/shard_map/ppermute | solution.py:558
  76.5 1.3 %collective-permute-start.3 = (f32[48,3,4,128]{3,2,1,0:T(4,128)S(1)}, f32[48,3,4,128]{3,2,1,0:T(4,128)S(1)}, u32[]{:S(2)}, u32[]{:S(2)}) collective-permute-start(f32[48,3,4,128]{3,2,1,0:T(4,128)S(1)} %slice.8), channel_id=1, source_target_pairs={{16,0},{32,16},{48,32},{64,48},{80,64},{96,80},{112,96},{128,112},... | collective-permute-start | bytes 884744 | tf_op jit(solution)/shard_map/ppermute | solution.py:558
  77.9 4.6 %collective-permute-start.4 = (f32[48,2,4,128]{3,2,1,0:T(4,128)S(1)}, f32[48,2,4,128]{3,2,1,0:T(4,128)S(1)}, u32[]{:S(2)}, u32[]{:S(2)}) collective-permute-start(f32[48,2,4,128]{3,2,1,0:T(4,128)S(1)} %slice.9), channel_id=1, source_target_pairs={{0,16},{16,32},{32,48},{48,64},{64,80},{80,96},{96,112},{112,128},... | collective-permute-start | bytes 589832 | tf_op jit(solution)/shard_map/ppermute | solution.py:558
  82.5 1.3 %collective-permute-start.5 = (f32[48,2,4,128]{3,2,1,0:T(4,128)S(1)}, f32[48,2,4,128]{3,2,1,0:T(4,128)S(1)}, u32[]{:S(2)}, u32[]{:S(2)}) collective-permute-start(f32[48,2,4,128]{3,2,1,0:T(4,128)S(1)} %slice.9), channel_id=1, source_target_pairs={{16,0},{32,16},{48,32},{64,48},{80,64},{96,80},{112,96},{128,112},... | collective-permute-start | bytes 589832 | tf_op jit(solution)/shard_map/ppermute | solution.py:558
  83.8 0.1 pad_add_fusion.place
  83.9 2.9 %collective-permute-done.4.shallow = f32[48,2,4,128]{3,2,1,0:T(4,128)S(1)} collective-permute-done((f32[48,2,4,128]{3,2,1,0:T(4,128)S(1)}, f32[48,2,4,128]{3,2,1,0:T(4,128)S(1)}, u32[]{:S(2)}, u32[]{:S(2)}) %collective-permute-start.4) | collective-permute-done | bytes 196640 | tf_op jit(solution)/shard_map/ppermute | solution.py:558
  86.7 4.1 %collective-permute-done.5.deep = f32[48,2,4,128]{3,2,1,0:T(4,128)S(1)} collective-permute-done((f32[48,2,4,128]{3,2,1,0:T(4,128)S(1)}, f32[48,2,4,128]{3,2,1,0:T(4,128)S(1)}, u32[]{:S(2)}, u32[]{:S(2)}) %collective-permute-start.5) | collective-permute-done | bytes 196640 | tf_op jit(solution)/shard_map/ppermute | solution.py:558
  90.9 4.9 %setup.1 = (f32[3,16,24,128]{3,2,1,0:T(8,128)S(1)}, f32[3,16,24,128]{3,2,1,0:T(8,128)S(1)}, f32[3,16,24,128]{3,2,1,0:T(8,128)S(1)}, f32[3,65,24,128]{3,2,1,0:T(8...) custom-call(s32[4]{0:T(128)S(1)} %pad_add_fusion.place, ...), custom_call_target="tpu_custom_call" | custom-call | flops 134217728 | tf_op jit(solution)/shard_map/setup/pallas_call | solution.py:503
  95.8 0.0 collective-permute-done.2.shallow
  95.8 0.0 collective-permute-done.3.deep
  95.8 11.9 %lines.1 = f32[16,3,4,128]{3,2,1,0:T(4,128)S(1)} custom-call(f32[48,5,4,128]{3,2,1,0:T(4,128)S(1)} %constant_dynamic-update-slice_fusion.middle, f32[48,3,4,128]{3,2,1,0:T(4,128)S(1)} %collective-permute-done.2.shallow, f32[48,3,4,128]{3,2,1,0:T(4,128)S(1)} %collective-permute-done.3.deep, f32[3,16,24,128]{3,2,1,0:T(8,128)S(1)} %get-tuple-element.16.free, ...), custom_call_target="tpu_custom_call" | custom-call | flops 134217728 | tf_op jit(solution)/shard_map/lines/pallas_call | solution.py:517
  107.7 19.4 %all_to_all.11.packed = f32[16,3,4,128]{3,2,1,0:T(4,128)} all-to-all(f32[16,3,4,128]{3,2,1,0:T(4,128)S(1)} %lines.1), channel_id=1, replica_groups=mesh['period'=2,'gx'=16,'gy'=8,'gz'=2] {'gx'}, dimensions={0} | all-to-all | bytes 196608 | tf_op jit(solution)/shard_map/all_to_all | solution.py:539
  127.1 1.8 %unpack.1 = f32[2,3,4,8,128]{4,3,2,1,0:T(8,128)} custom-call(f32[16,3,4,128]{3,2,1,0:T(4,128)} %all_to_all.11.packed), custom_call_target="tpu_custom_call" | custom-call | tf_op jit(solution)/shard_map/unpack/pallas_call | solution.py:485
  (5 shorter events, 0.1 us)
Async XLA Ops:
  59.9 7.6 %collective-permute-start = (f32[16,5,4,128]{3,2,1,0:T(4,128)S(1)}, f32[16,5,4,128]{3,2,1,0:T(4,128)S(1)}, u32[]{:S(2)}, u32[]{:S(2)}) collective-permute-start(f32[16,5,4,128]{3,2,1,0:T(4,128)S(1)} %all_to_all.10), channel_id=1, source_target_pairs={{0,2},{16,18},{32,34},{48,50},{64,66},{80,82},{96,98},{112,114},{1... | collective-permute-start | bytes 491528 | tf_op jit(solution)/shard_map/ppermute | solution.py:558
  64.6 8.5 %collective-permute-start.1 = (f32[16,5,4,128]{3,2,1,0:T(4,128)S(1)}, f32[16,5,4,128]{3,2,1,0:T(4,128)S(1)}, u32[]{:S(2)}, u32[]{:S(2)}) collective-permute-start(f32[16,5,4,128]{3,2,1,0:T(4,128)S(1)} %all_to_all.10), channel_id=1, source_target_pairs={{2,0},{18,16},{34,32},{50,48},{66,64},{82,80},{98,96},{114,112},{1... | collective-permute-start | bytes 491528 | tf_op jit(solution)/shard_map/ppermute | solution.py:558
  73.2 22.6 %collective-permute-start.2 = (f32[48,3,4,128]{3,2,1,0:T(4,128)S(1)}, f32[48,3,4,128]{3,2,1,0:T(4,128)S(1)}, u32[]{:S(2)}, u32[]{:S(2)}) collective-permute-start(f32[48,3,4,128]{3,2,1,0:T(4,128)S(1)} %slice.8), channel_id=1, source_target_pairs={{0,16},{16,32},{32,48},{48,64},{64,80},{80,96},{96,112},{112,128},... | collective-permute-start | bytes 884744 | tf_op jit(solution)/shard_map/ppermute | solution.py:558
  76.5 19.3 %collective-permute-start.3 = (f32[48,3,4,128]{3,2,1,0:T(4,128)S(1)}, f32[48,3,4,128]{3,2,1,0:T(4,128)S(1)}, u32[]{:S(2)}, u32[]{:S(2)}) collective-permute-start(f32[48,3,4,128]{3,2,1,0:T(4,128)S(1)} %slice.8), channel_id=1, source_target_pairs={{16,0},{32,16},{48,32},{64,48},{80,64},{96,80},{112,96},{128,112},... | collective-permute-start | bytes 884744 | tf_op jit(solution)/shard_map/ppermute | solution.py:558
  77.9 8.9 %collective-permute-start.4 = (f32[48,2,4,128]{3,2,1,0:T(4,128)S(1)}, f32[48,2,4,128]{3,2,1,0:T(4,128)S(1)}, u32[]{:S(2)}, u32[]{:S(2)}) collective-permute-start(f32[48,2,4,128]{3,2,1,0:T(4,128)S(1)} %slice.9), channel_id=1, source_target_pairs={{0,16},{16,32},{32,48},{48,64},{64,80},{80,96},{96,112},{112,128},... | collective-permute-start | bytes 589832 | tf_op jit(solution)/shard_map/ppermute | solution.py:558
  82.5 8.4 %collective-permute-start.5 = (f32[48,2,4,128]{3,2,1,0:T(4,128)S(1)}, f32[48,2,4,128]{3,2,1,0:T(4,128)S(1)}, u32[]{:S(2)}, u32[]{:S(2)}) collective-permute-start(f32[48,2,4,128]{3,2,1,0:T(4,128)S(1)} %slice.9), channel_id=1, source_target_pairs={{16,0},{32,16},{48,32},{64,48},{80,64},{96,80},{112,96},{128,112},... | collective-permute-start | bytes 589832 | tf_op jit(solution)/shard_map/ppermute | solution.py:558

commit v4 on v3

--- a/solution.py
+++ b/solution.py
@@ -209,25 +209,27 @@
     for d in range(3):
         KW[d, 0] = jnp.zeros(shape, f32)
 
-    def diagonals(x, cw1_before):
+    nothing = jnp.zeros(shape, f32)
+    CW[0, 0] = nothing
+
+    def diagonals(x, state):
         w1b, w1, w2, w3 = KW[0, x], KW[0, x + 1], KW[1, x + 1], KW[2, x + 1]
         total = ((((w1 + w1b) + w3) + row_back(w3)) + w2) + lane_back(w2)
         FI[x] = (1.0 + shift_ratio) * total + shift_added
-        cw = []
         for d, w in enumerate((w1, w2, w3)):
             pair = w + row_next(w)
             pair = jnp.where(even_row, pair, row_back(pair))
-            cw.append(coarse_scale[d] * (pair + lane_next(pair)))
-            CW[d, x + 1] = cw[d]
-        total = (
-            (((cw[0] + cw1_before) + cw[2]) + row_back(cw[2], 2)) + cw[1]
-        ) + lane_back(cw[1], 2)
+            CW[d, x + 1] = coarse_scale[d] * (pair + lane_next(pair))
+        return state
+
+    def coarse_diagonals(x, state):
+        w1b, w1, w2, w3 = CW[0, x], CW[0, x + 1], CW[1, x + 1], CW[2, x + 1]
+        total = ((((w1 + w1b) + w3) + row_back(w3, 2)) + w2) + lane_back(w2, 2)
         CI[x] = (1.0 + shift_ratio) * total + shift_added
-        return cw[0]
-
-    nothing = jnp.zeros(shape, f32)
-    CW[0, 0] = nothing
-    loop(64, diagonals, nothing, unroll=8)
+        return state
+
+    loop(64, diagonals, 0, unroll=16)
+    loop(64, coarse_diagonals, 0, unroll=16)
 
     def factors(x, state):
         fine_before, coarse_before = state
@@ -270,7 +272,7 @@
     SM,
     CS,
     TY,
-    RH,
+    CM,
     OUT,
 ):
     shape = (ROWS, 128)
@@ -341,17 +343,18 @@
 
     loop(16, to_nodes, 0, unroll=8)
 
-    def eliminate(source, inverse, back, parts):
+    def eliminate(source, inverse, back, parts, unroll=4):
         def step(x, state):
             scale, couple = inverse[x], back[x]
+            sources = source(x)
             after = []
             for part in range(parts):
-                value = source[part, x] * scale + couple * state[part]
+                value = sources[part] * scale + couple * state[part]
                 TY[part, x] = value
                 after.append(value)
             return tuple(after)
 
-        loop(64, step, (nothing,) * parts, unroll=4)
+        loop(64, step, (nothing,) * parts, unroll=unroll)
 
     def substitute(quotient, parts, then, unroll):
         def step(x, state):
@@ -373,34 +376,43 @@
             SM[part, x] = value
             residue = sides(value, KW[1, x + 1], KW[2, x + 1], 1)
             halved.append(residue + 0.5 * (row_back(residue) + row_next(residue)))
-        merged = jnp.where(even_row, halved[0], row_back(halved[1]))
-        CS[0, x] = merged + 0.5 * (lane_back(merged) + lane_next(merged))
+        CM[0, x] = jnp.where(even_row, halved[0], row_back(halved[1]))
+
+    def coarse_source(x):
+        merged = CM[0, x]
+        value = merged + 0.5 * (lane_back(merged) + lane_next(merged))
+        CS[0, x] = value
+        return (value,)
 
     def after_coarse(x, value):
-        CS[0, x] = CS[0, x] + sides(value, CW[1, x + 1], CW[2, x + 1], 2)
+        CM[0, x] = CS[0, x] + sides(value, CW[1, x + 1], CW[2, x + 1], 2)
 
     def after_correction(x, value):
-        wide = jnp.where(even_lane, value, 0.5 * (lane_back(value) + lane_next(value)))
+        CS[0, x] = jnp.where(even_lane, value, 0.5 * (lane_back(value) + lane_next(value)))
+
+    def corrected_source(x):
+        wide = CS[0, x]
         above = row_next(wide)
         corrections = (
             jnp.where(even_row, wide, 0.5 * (row_back(wide) + above)),
             jnp.where(even_row, above, 0.5 * (wide + row_next(wide, 2))),
         )
-        for part in range(2):
-            smoothed = SM[part, x] + corrections[part]
-            RH[part, x] = NS[part, x] + sides(smoothed, KW[1, x + 1], KW[2, x + 1], 1)
+        return tuple(
+            NS[part, x] + sides(SM[part, x] + corrections[part], KW[1, x + 1], KW[2, x + 1], 1)
+            for part in range(2)
+        )
 
     def after_potential(x, *values):
         for part in range(2):
             NS[part, x] = values[part]
 
-    eliminate(NS, FI, FB, 2)
-    substitute(FQ, 2, after_smoothing, 8)
-    eliminate(CS, CI, CB, 1)
+    eliminate(lambda x: (NS[0, x], NS[1, x]), FI, FB, 2)
+    substitute(FQ, 2, after_smoothing, 16)
+    eliminate(coarse_source, CI, CB, 1, 16)
     substitute(CQ, 1, after_coarse, 16)
-    eliminate(CS, CI, CB, 1)
-    substitute(CQ, 1, after_correction, 8)
-    eliminate(RH, FI, FB, 2)
+    eliminate(lambda x: (CM[0, x],), CI, CB, 1)
+    substitute(CQ, 1, after_correction, 16)
+    eliminate(corrected_source, FI, FB, 2, 16)
     substitute(FQ, 2, after_potential, 4)
 
     def from_nodes(l, state):
@@ -459,7 +471,7 @@
             )
         return state
 
-    loop(4, gather_up, 0)
+    loop(4, gather_up, 0, unroll=4)
 
 
 def vmem():
@@ -527,7 +539,7 @@
             pair,
             resident(1, 64, ROWS, 128),
             pair,
-            pair,
+            resident(1, 64, ROWS, 128),
             resident(6, 16, TILE, 128),
         ],
         name="lines",
@@ -586,6 +598,7 @@
     )
     ready = setup(place, middle, shallow_material, deep_material, **options(20, 2**27))
     result = swap(lines(middle, shallow_source, deep_source, ready, **options(32, 2**27)))
+    result = pltpu.with_memory_space_constraint(result, pltpu.VMEM)
     return unpack(result, residual.shape)
 
 

time: 129 us -> 126 us (0.977)
  Pallas kernels: 19.6 us -> 16.4 us
    pallas_call x1, Pallas kernels: 11.9 us -> 10 us  [lines(): pl.pallas_call(line_body, out_shape=resident(16, 3, HALF, 128), in_specs=...]
where the time goes in v4:
time: 126 us
  blocking collectives  78.1 us (62%)
  starting transfers between devices  17.3 us (14%)
  Pallas kernels  16.4 us (13%)
  waiting for transfers between devices  13.5 us (11%)
    all_to_all x2, blocking collectives, swap(): return lax.all_to_all(values, 'gx', 0, 0, tiled=True)  78.1 us
    ppermute x6, starting transfers between devices, from_side(): return lax.ppermute(values, axes, pairs)  17.3 us
    ppermute x6, waiting for transfers between devices, from_side(): return lax.ppermute(values, axes, pairs)  13.5 us
    pallas_call x1, Pallas kernels, lines(): pl.pallas_call(line_body, out_shape=resident(16, 3, HALF, 128), in_specs=...  10 us
    pallas_call x1, Pallas kernels, setup(): pl.pallas_call(setup_body, out_shape=[edge, edge, edge, weights, weights]...  4.5 us
  transfers between devices with their start and end apart: 6, of which 4 were waited for; matrix products, arithmetic and copies ran while one was open for 0% of the time, Pallas kernels for 4%

profile of v4, /device:TPU:70, one launch (start us, length us, event | category | flops | bytes accessed | tf_op | source)
XLA Modules:
  0.0 125.7 jit_solution(14793582190160195230)
XLA Ops:
  0.0 1.1 pack.1
  1.1 58.8 %all_to_all.10 = f32[16,5,4,128]{3,2,1,0:T(4,128)S(1)} all-to-all(f32[16,5,4,128]{3,2,1,0:T(4,128)S(1)} %pack.1), channel_id=1, replica_groups=mesh['period'=2,'gx'=16,'gy'=8,'gz'=2] {'gx'}, dimensions={0} | all-to-all | bytes 327680 | tf_op jit(solution)/shard_map/all_to_all | solution.py:551
  59.9 4.8 %collective-permute-start = (f32[16,5,4,128]{3,2,1,0:T(4,128)S(1)}, f32[16,5,4,128]{3,2,1,0:T(4,128)S(1)}, u32[]{:S(2)}, u32[]{:S(2)}) collective-permute-start(f32[16,5,4,128]{3,2,1,0:T(4,128)S(1)} %all_to_all.10), channel_id=1, source_target_pairs={{0,2},{16,18},{32,34},{48,50},{64,66},{80,82},{96,98},{112,114},{1... | collective-permute-start | bytes 491528 | tf_op jit(solution)/shard_map/ppermute | solution.py:570
  64.6 2.0 %collective-permute-start.1 = (f32[16,5,4,128]{3,2,1,0:T(4,128)S(1)}, f32[16,5,4,128]{3,2,1,0:T(4,128)S(1)}, u32[]{:S(2)}, u32[]{:S(2)}) collective-permute-start(f32[16,5,4,128]{3,2,1,0:T(4,128)S(1)} %all_to_all.10), channel_id=1, source_target_pairs={{2,0},{18,16},{34,32},{50,48},{66,64},{82,80},{98,96},{114,112},{1... | collective-permute-start | bytes 491528 | tf_op jit(solution)/shard_map/ppermute | solution.py:570
  66.6 0.9 collective-permute-done
  67.5 5.6 %collective-permute-done.1 = f32[16,5,4,128]{3,2,1,0:T(4,128)S(1)} collective-permute-done((f32[16,5,4,128]{3,2,1,0:T(4,128)S(1)}, f32[16,5,4,128]{3,2,1,0:T(4,128)S(1)}, u32[]{:S(2)}, u32[]{:S(2)}) %collective-permute-start.1) | collective-permute-done | bytes 163872 | tf_op jit(solution)/shard_map/ppermute | solution.py:570
  73.2 3.4 %collective-permute-start.2 = (f32[48,3,4,128]{3,2,1,0:T(4,128)S(1)}, f32[48,3,4,128]{3,2,1,0:T(4,128)S(1)}, u32[]{:S(2)}, u32[]{:S(2)}) collective-permute-start(f32[48,3,4,128]{3,2,1,0:T(4,128)S(1)} %slice.8), channel_id=1, source_target_pairs={{0,16},{16,32},{32,48},{48,64},{64,80},{80,96},{96,112},{112,128},... | collective-permute-start | bytes 884744 | tf_op jit(solution)/shard_map/ppermute | solution.py:570
  76.5 1.3 %collective-permute-start.3 = (f32[48,3,4,128]{3,2,1,0:T(4,128)S(1)}, f32[48,3,4,128]{3,2,1,0:T(4,128)S(1)}, u32[]{:S(2)}, u32[]{:S(2)}) collective-permute-start(f32[48,3,4,128]{3,2,1,0:T(4,128)S(1)} %slice.8), channel_id=1, source_target_pairs={{16,0},{32,16},{48,32},{64,48},{80,64},{96,80},{112,96},{128,112},... | collective-permute-start | bytes 884744 | tf_op jit(solution)/shard_map/ppermute | solution.py:570
  77.9 4.6 %collective-permute-start.4 = (f32[48,2,4,128]{3,2,1,0:T(4,128)S(1)}, f32[48,2,4,128]{3,2,1,0:T(4,128)S(1)}, u32[]{:S(2)}, u32[]{:S(2)}) collective-permute-start(f32[48,2,4,128]{3,2,1,0:T(4,128)S(1)} %slice.9), channel_id=1, source_target_pairs={{0,16},{16,32},{32,48},{48,64},{64,80},{80,96},{96,112},{112,128},... | collective-permute-start | bytes 589832 | tf_op jit(solution)/shard_map/ppermute | solution.py:570
  82.5 1.3 %collective-permute-start.5 = (f32[48,2,4,128]{3,2,1,0:T(4,128)S(1)}, f32[48,2,4,128]{3,2,1,0:T(4,128)S(1)}, u32[]{:S(2)}, u32[]{:S(2)}) collective-permute-start(f32[48,2,4,128]{3,2,1,0:T(4,128)S(1)} %slice.9), channel_id=1, source_target_pairs={{16,0},{32,16},{48,32},{64,48},{80,64},{96,80},{112,96},{128,112},... | collective-permute-start | bytes 589832 | tf_op jit(solution)/shard_map/ppermute | solution.py:570
  83.8 0.1 pad_add_fusion.place
  83.9 2.9 %collective-permute-done.4.shallow = f32[48,2,4,128]{3,2,1,0:T(4,128)S(1)} collective-permute-done((f32[48,2,4,128]{3,2,1,0:T(4,128)S(1)}, f32[48,2,4,128]{3,2,1,0:T(4,128)S(1)}, u32[]{:S(2)}, u32[]{:S(2)}) %collective-permute-start.4) | collective-permute-done | bytes 196640 | tf_op jit(solution)/shard_map/ppermute | solution.py:570
  86.7 4.1 %collective-permute-done.5.deep = f32[48,2,4,128]{3,2,1,0:T(4,128)S(1)} collective-permute-done((f32[48,2,4,128]{3,2,1,0:T(4,128)S(1)}, f32[48,2,4,128]{3,2,1,0:T(4,128)S(1)}, u32[]{:S(2)}, u32[]{:S(2)}) %collective-permute-start.5) | collective-permute-done | bytes 196640 | tf_op jit(solution)/shard_map/ppermute | solution.py:570
  90.9 4.5 %setup.1 = (f32[3,16,24,128]{3,2,1,0:T(8,128)S(1)}, f32[3,16,24,128]{3,2,1,0:T(8,128)S(1)}, f32[3,16,24,128]{3,2,1,0:T(8,128)S(1)}, f32[3,65,24,128]{3,2,1,0:T(8...) custom-call(s32[4]{0:T(128)S(1)} %pad_add_fusion.place, ...), custom_call_target="tpu_custom_call" | custom-call | flops 134217728 | tf_op jit(solution)/shard_map/setup/pallas_call | solution.py:515
  95.4 0.0 collective-permute-done.2.shallow
  95.4 0.0 collective-permute-done.3.deep
  95.4 10.0 %lines.1 = f32[16,3,4,128]{3,2,1,0:T(4,128)S(1)} custom-call(f32[48,5,4,128]{3,2,1,0:T(4,128)S(1)} %constant_dynamic-update-slice_fusion.middle, f32[48,3,4,128]{3,2,1,0:T(4,128)S(1)} %collective-permute-done.2.shallow, f32[48,3,4,128]{3,2,1,0:T(4,128)S(1)} %collective-permute-done.3.deep, f32[3,16,24,128]{3,2,1,0:T(8,128)S(1)} %get-tuple-element.16.free, ...), custom_call_target="tpu_custom_call" | custom-call | flops 134217728 | tf_op jit(solution)/shard_map/lines/pallas_call | solution.py:529
  105.4 19.3 %all_to_all.11.packed = f32[16,3,4,128]{3,2,1,0:T(4,128)S(1)} all-to-all(f32[16,3,4,128]{3,2,1,0:T(4,128)S(1)} %lines.1), channel_id=1, replica_groups=mesh['period'=2,'gx'=16,'gy'=8,'gz'=2] {'gx'}, dimensions={0} | all-to-all | bytes 196608 | tf_op jit(solution)/shard_map/all_to_all | solution.py:551
  124.8 0.9 unpack.1
  (5 shorter events, 0.1 us)
Async XLA Ops:
  59.9 7.6 %collective-permute-start = (f32[16,5,4,128]{3,2,1,0:T(4,128)S(1)}, f32[16,5,4,128]{3,2,1,0:T(4,128)S(1)}, u32[]{:S(2)}, u32[]{:S(2)}) collective-permute-start(f32[16,5,4,128]{3,2,1,0:T(4,128)S(1)} %all_to_all.10), channel_id=1, source_target_pairs={{0,2},{16,18},{32,34},{48,50},{64,66},{80,82},{96,98},{112,114},{1... | collective-permute-start | bytes 491528 | tf_op jit(solution)/shard_map/ppermute | solution.py:570
  64.6 8.5 %collective-permute-start.1 = (f32[16,5,4,128]{3,2,1,0:T(4,128)S(1)}, f32[16,5,4,128]{3,2,1,0:T(4,128)S(1)}, u32[]{:S(2)}, u32[]{:S(2)}) collective-permute-start(f32[16,5,4,128]{3,2,1,0:T(4,128)S(1)} %all_to_all.10), channel_id=1, source_target_pairs={{2,0},{18,16},{34,32},{50,48},{66,64},{82,80},{98,96},{114,112},{1... | collective-permute-start | bytes 491528 | tf_op jit(solution)/shard_map/ppermute | solution.py:570
  73.2 22.2 %collective-permute-start.2 = (f32[48,3,4,128]{3,2,1,0:T(4,128)S(1)}, f32[48,3,4,128]{3,2,1,0:T(4,128)S(1)}, u32[]{:S(2)}, u32[]{:S(2)}) collective-permute-start(f32[48,3,4,128]{3,2,1,0:T(4,128)S(1)} %slice.8), channel_id=1, source_target_pairs={{0,16},{16,32},{32,48},{48,64},{64,80},{80,96},{96,112},{112,128},... | collective-permute-start | bytes 884744 | tf_op jit(solution)/shard_map/ppermute | solution.py:570
  76.5 18.9 %collective-permute-start.3 = (f32[48,3,4,128]{3,2,1,0:T(4,128)S(1)}, f32[48,3,4,128]{3,2,1,0:T(4,128)S(1)}, u32[]{:S(2)}, u32[]{:S(2)}) collective-permute-start(f32[48,3,4,128]{3,2,1,0:T(4,128)S(1)} %slice.8), channel_id=1, source_target_pairs={{16,0},{32,16},{48,32},{64,48},{80,64},{96,80},{112,96},{128,112},... | collective-permute-start | bytes 884744 | tf_op jit(solution)/shard_map/ppermute | solution.py:570
  77.9 8.9 %collective-permute-start.4 = (f32[48,2,4,128]{3,2,1,0:T(4,128)S(1)}, f32[48,2,4,128]{3,2,1,0:T(4,128)S(1)}, u32[]{:S(2)}, u32[]{:S(2)}) collective-permute-start(f32[48,2,4,128]{3,2,1,0:T(4,128)S(1)} %slice.9), channel_id=1, source_target_pairs={{0,16},{16,32},{32,48},{48,64},{64,80},{80,96},{96,112},{112,128},... | collective-permute-start | bytes 589832 | tf_op jit(solution)/shard_map/ppermute | solution.py:570
  82.5 8.4 %collective-permute-start.5 = (f32[48,2,4,128]{3,2,1,0:T(4,128)S(1)}, f32[48,2,4,128]{3,2,1,0:T(4,128)S(1)}, u32[]{:S(2)}, u32[]{:S(2)}) collective-permute-start(f32[48,2,4,128]{3,2,1,0:T(4,128)S(1)} %slice.9), channel_id=1, source_target_pairs={{16,0},{32,16},{48,32},{64,48},{80,64},{96,80},{112,96},{128,112},... | collective-permute-start | bytes 589832 | tf_op jit(solution)/shard_map/ppermute | solution.py:570

commit v5 on v4

--- a/solution.py
+++ b/solution.py
@@ -1,3 +1,5 @@
+import functools
+
 import jax
 import jax.numpy as jnp
 from jax import lax
@@ -65,7 +67,22 @@
 row_next, row_back, lane_next, lane_back = y_next, y_back, z_next, z_back
 
 
-def pack_body(residual, classes, edge_mask, class_weight, out):
+def position_facts(place, sizes):
+    x, y, z = place[0], place[1], place[2]
+    flip = z % 2
+    along = x + flip * (sizes[0] - 1 - 2 * x)
+    before = jnp.where(along == 0, 1 - flip, flip)
+    after = jnp.where(along == sizes[0] - 1, 1 - flip, flip)
+    corner_y = y * TILE - TILE
+    corner_z = (z * sizes[0] + along) * TILE - TILE
+    return corner_y, corner_z, (before, flip, after)
+
+
+def mirrored(place, index, count):
+    return index + place[2] % 2 * (count - 1 - 2 * index)
+
+
+def pack_body(place, residual, classes, edge_mask, class_weight, out):
     thick = classes.shape[0]
     slots = []
     for i in range(thick):
@@ -82,7 +99,7 @@
     block = 0
     for start in range(0, len(slots), 16):
         group = jnp.concatenate(slots[start : start + 16], axis=0)
-        block = send_group(group, lambda target: target, out, block)
+        block = send_group(group, lambda target: mirrored(place, target, 16), out, block)
 
 
 def send_group(group, device, out, block):
@@ -94,11 +111,11 @@
         moved = jnp.concatenate([group, pltpu.roll(group, 128 - half, 1)], axis=0).T
         parts = 1
     for target in range(16):
-        place = device(target)
-        if place is not None:
+        where = device(target)
+        if where is not None:
             for part in range(parts):
                 row = TILE * target + half * part
-                out[place, block + part] = moved[row : row + half]
+                out[where, block + part] = moved[row : row + half]
     return block + parts
 
 
@@ -116,9 +133,11 @@
     return jnp.where(lanes((64, 128)) % TILE < half, moved[:64], upper)
 
 
-def unpack_body(packed, out):
+def unpack_body(place, packed, out):
     for part in range(2):
-        moved = receive_group(lambda source, block: packed[source, block], 2 * part, part == 0)
+        moved = receive_group(
+            lambda window, block: packed[mirrored(place, window, 16), block], 2 * part, part == 0
+        )
         for slot in range(moved.shape[0] // TILE):
             field, i = divmod(16 * part + slot, 4)
             out[field // 3, field % 3, i] = moved[TILE * slot : TILE * slot + TILE]
@@ -147,8 +166,9 @@
                     g, t = divmod(p, 4)
                     if t == 3:
                         return gap
-                    ref, first = windows[t]
-                    return ref[y * 16 + 4 * g + a, first + block]
+                    ref, first, flag = windows[t]
+                    turn = y + flag * (2 - 2 * y)
+                    return ref[turn * 16 + 4 * g + a, first + block]
 
                 moved = receive_group(blocks, 2 * part, full)
                 for slot in range(moved.shape[0] // TILE):
@@ -160,14 +180,31 @@
 
 
 def setup_body(
-    place, middle, shallow, deep, free_out, M, Dm, KW, CW, FI, FB, FQ, CI, CB, CQ, cells
+    sizes,
+    place,
+    middle,
+    shallow,
+    deep,
+    free_out,
+    M,
+    Dm,
+    KW,
+    CW,
+    FI,
+    FB,
+    FQ,
+    CI,
+    CB,
+    CQ,
+    cells,
 ):
-    extent_y, extent_z = place[2], place[3]
+    corner_y, corner_z, orders = position_facts(place, sizes)
+    extent_y, extent_z = sizes[1] * TILE, sizes[0] * sizes[2] * TILE
     shape = (ROWS, 128)
     lane = lanes(shape)
     row = lax.broadcasted_iota(jnp.int32, shape, 0)
-    at_y = lane % DEPTH + place[0]
-    at_z = row + place[1]
+    at_y = lane % DEPTH + corner_y
+    at_z = row + corner_z
     inside = jnp.where(
         (at_y >= 0) & (at_y < extent_y) & (at_z >= 0) & (at_z < extent_z), 1.0, 0.0
     ).astype(f32)
@@ -180,7 +217,9 @@
         else:
             free_out[field - 1, level, TILE * y : TILE * y + TILE, :] = values
 
-    spread_out(((shallow, 0), (middle, 0), (deep, 0)), (True,), put)
+    spread_out(
+        ((shallow, 0, orders[0]), (middle, 0, orders[1]), (deep, 0, orders[2])), (True,), put
+    )
     pad_low(cells, 0)
 
     def coefficients(l, state):
@@ -250,6 +289,8 @@
 
 
 def line_body(
+    sizes,
+    place,
     middle,
     shallow,
     deep,
@@ -276,6 +317,7 @@
     OUT,
 ):
     shape = (ROWS, 128)
+    orders = position_facts(place, sizes)[2]
     even_row = lax.broadcasted_iota(jnp.int32, shape, 0) % 2 == 0
     even_lane = lanes(shape) % 2 == 0
     nothing = jnp.zeros(shape, f32)
@@ -286,7 +328,11 @@
         W[field, level, rows, :] = source
         E[field, level + 1, rows, :] = source * Dm[field % 3, level, rows, :]
 
-    spread_out(((shallow, 0), (middle, 2), (deep, 0)), (True, False), put)
+    spread_out(
+        ((shallow, 0, orders[0]), (middle, 2, orders[1]), (deep, 0, orders[2])),
+        (True, False),
+        put,
+    )
 
     def side_fluxes(part, l):
         e1, e2, e3 = (E[3 * part + d, l] for d in range(3))
@@ -482,38 +528,38 @@
     return pl.BlockSpec(memory_space=pltpu.SMEM)
 
 
-def pack(residual, classes, edge_mask, class_weight, **options):
+def pack(place, residual, classes, edge_mask, class_weight, **options):
     return pl.pallas_call(
         pack_body,
         out_shape=resident(16, 5, HALF, 128),
-        in_specs=[vmem(), vmem(), vmem(), smem()],
+        in_specs=[smem(), vmem(), vmem(), vmem(), smem()],
         out_specs=vmem(),
         name="pack",
         **options,
-    )(residual, classes, edge_mask, class_weight)
-
-
-def unpack(packed, shape, **options):
+    )(place, residual, classes, edge_mask, class_weight)
+
+
+def unpack(place, packed, shape, **options):
     return pl.pallas_call(
         unpack_body,
         out_shape=jax.ShapeDtypeStruct(shape, f32),
-        in_specs=[vmem()],
+        in_specs=[smem(), vmem()],
         out_specs=vmem(),
         name="unpack",
         **options,
-    )(packed)
+    )(place, packed)
 
 
 def resident(*shape):
     return pltpu.VMEM(shape, f32)
 
 
-def setup(place, middle, shallow, deep, **options):
+def setup(sizes, place, middle, shallow, deep, **options):
     line = resident(64, ROWS, 128)
     edge = resident(3, 16, ROWS, 128)
     weights = resident(3, 65, ROWS, 128)
     return pl.pallas_call(
-        setup_body,
+        functools.partial(setup_body, sizes),
         out_shape=[edge, edge, edge, weights, weights] + [line] * 6,
         in_specs=[smem(), vmem(), vmem(), vmem()],
         out_specs=[vmem()] * 11,
@@ -523,13 +569,13 @@
     )(place, middle, shallow, deep)
 
 
-def lines(middle, shallow, deep, ready, **options):
+def lines(sizes, place, middle, shallow, deep, ready, **options):
     edge = lambda count, levels: resident(count, levels, ROWS, 128)
     pair = resident(2, 64, ROWS, 128)
     return pl.pallas_call(
-        line_body,
+        functools.partial(line_body, sizes),
         out_shape=resident(16, 3, HALF, 128),
-        in_specs=[vmem()] * (3 + len(ready)),
+        in_specs=[smem()] + [vmem()] * (3 + len(ready)),
         out_specs=vmem(),
         scratch_shapes=[
             edge(6, 16),
@@ -544,7 +590,7 @@
         ],
         name="lines",
         **options,
-    )(middle, shallow, deep, *ready)
+    )(place, middle, shallow, deep, *ready)
 
 
 def swap(values):
@@ -558,48 +604,36 @@
 
     def position(y, tile):
         z, x = divmod(tile, size_x)
+        if z % 2:
+            x = size_x - 1 - x
         return (x * size_y + y) * size_z + z
 
     def from_side(values, step_y, step_tile):
-        pairs = [
-            (position(y, tile), position(y + step_y, tile + step_tile))
-            for y in range(size_y)
-            for tile in range(tiles)
-            if 0 <= y + step_y < size_y and 0 <= tile + step_tile < tiles
-        ]
+        pairs = []
+        for y in range(size_y):
+            for tile in range(tiles):
+                next_y = y - step_y if tile // size_x % 2 else y + step_y
+                if 0 <= next_y < size_y and 0 <= tile + step_tile < tiles:
+                    pairs.append((position(y, tile), position(next_y, tile + step_tile)))
         return lax.ppermute(values, axes, pairs)
 
-    own = swap(
-        pack(
-            residual,
-            classes,
-            edge_mask,
-            class_weight,
-        )
-    )
+    sizes = (size_x, size_y, size_z)
+    place = jnp.stack([lax.axis_index(name) for name in axes]).astype(jnp.int32)
+    own = swap(pack(place, residual, classes, edge_mask, class_weight))
     middle = jnp.concatenate([from_side(own, 1, 0), own, from_side(own, -1, 0)], axis=0)
     material, source = middle[:, :2], middle[:, 2:]
     shallow_material = from_side(material, 0, 1)
     deep_material = from_side(material, 0, -1)
     shallow_source = from_side(source, 0, 1)
     deep_source = from_side(source, 0, -1)
-    tile = lax.axis_index("gz") * size_x + lax.axis_index("gx")
-    place = jnp.stack(
-        [
-            lax.axis_index("gy") * TILE - TILE,
-            tile * TILE - TILE,
-            jnp.int32(size_y * TILE),
-            jnp.int32(tiles * TILE),
-        ]
-    ).astype(jnp.int32)
     options = lambda size, cost: dict(
         compiler_params=pltpu.CompilerParams(vmem_limit_bytes=size * 2**20),
         cost_estimate=pl.CostEstimate(flops=cost, bytes_accessed=0, transcendentals=0),
     )
-    ready = setup(place, middle, shallow_material, deep_material, **options(20, 2**27))
-    result = swap(lines(middle, shallow_source, deep_source, ready, **options(32, 2**27)))
+    ready = setup(sizes, place, middle, shallow_material, deep_material, **options(20, 2**27))
+    result = swap(lines(sizes, place, middle, shallow_source, deep_source, ready, **options(32, 2**27)))
     result = pltpu.with_memory_space_constraint(result, pltpu.VMEM)
-    return unpack(result, residual.shape)
+    return unpack(place, result, residual.shape)
 
 
 def solution(mesh):

time: 126 us -> 128 us (1.016)
  the two profiles are of different devices: /device:TPU:70 before, /device:TPU:86 now
where the time goes in v5:
time: 128 us
  blocking collectives  79.1 us (62%)
  Pallas kernels  17.9 us (14%)
  starting transfers between devices  17.3 us (14%)
  waiting for transfers between devices  12.7 us (10%)
    all_to_all x2, blocking collectives, swap(): return lax.all_to_all(values, 'gx', 0, 0, tiled=True)  79.1 us
    ppermute x6, starting transfers between devices, from_side(): return lax.ppermute(values, axes, pairs)  17.3 us
    ppermute x6, waiting for transfers between devices, from_side(): return lax.ppermute(values, axes, pairs)  12.7 us
    pallas_call x1, Pallas kernels, lines(): pl.pallas_call(functools.partial(line_body, sizes), out_shape=resident(16...  10.7 us
    pallas_call x1, Pallas kernels, setup(): pl.pallas_call(functools.partial(setup_body, sizes), out_shape=[edge, edg...  4.58 us
  transfers between devices with their start and end apart: 6, of which 4 were waited for; matrix products, arithmetic and copies ran while one was open for 0% of the time, Pallas kernels for 4%

profile of v5, /device:TPU:86, one launch (start us, length us, event | category | flops | bytes accessed | tf_op | source)
XLA Modules:
  0.0 127.8 jit_solution(10925477243678881595)
XLA Ops:
  0.0 0.6 pad_add_fusion.place
  0.6 0.0 copy-start
  0.6 1.1 pack.1
  1.7 58.8 %all_to_all.10 = f32[16,5,4,128]{3,2,1,0:T(4,128)S(1)} all-to-all(f32[16,5,4,128]{3,2,1,0:T(4,128)S(1)} %pack.1), channel_id=1, replica_groups=mesh['period'=2,'gx'=16,'gy'=8,'gz'=2] {'gx'}, dimensions={0} | all-to-all | bytes 327680 | tf_op jit(solution)/shard_map/all_to_all | solution.py:597
  60.5 4.8 %collective-permute-start = (f32[16,5,4,128]{3,2,1,0:T(4,128)S(1)}, f32[16,5,4,128]{3,2,1,0:T(4,128)S(1)}, u32[]{:S(2)}, u32[]{:S(2)}) collective-permute-start(f32[16,5,4,128]{3,2,1,0:T(4,128)S(1)} %all_to_all.10), channel_id=1, source_target_pairs={{0,2},{16,18},{32,34},{48,50},{64,66},{80,82},{96,98},{112,114},{1... | collective-permute-start | bytes 491528 | tf_op jit(solution)/shard_map/ppermute | solution.py:618
  65.3 2.0 %collective-permute-start.1 = (f32[16,5,4,128]{3,2,1,0:T(4,128)S(1)}, f32[16,5,4,128]{3,2,1,0:T(4,128)S(1)}, u32[]{:S(2)}, u32[]{:S(2)}) collective-permute-start(f32[16,5,4,128]{3,2,1,0:T(4,128)S(1)} %all_to_all.10), channel_id=1, source_target_pairs={{241,243},{225,227},{209,211},{193,195},{177,179},{161,163},{145,1... | collective-permute-start | bytes 491528 | tf_op jit(solution)/shard_map/ppermute | solution.py:618
  67.2 0.9 collective-permute-done
  68.2 5.6 %collective-permute-done.1 = f32[16,5,4,128]{3,2,1,0:T(4,128)S(1)} collective-permute-done((f32[16,5,4,128]{3,2,1,0:T(4,128)S(1)}, f32[16,5,4,128]{3,2,1,0:T(4,128)S(1)}, u32[]{:S(2)}, u32[]{:S(2)}) %collective-permute-start.1) | collective-permute-done | bytes 163872 | tf_op jit(solution)/shard_map/ppermute | solution.py:618
  73.8 3.4 %collective-permute-start.2 = (f32[48,3,4,128]{3,2,1,0:T(4,128)S(1)}, f32[48,3,4,128]{3,2,1,0:T(4,128)S(1)}, u32[]{:S(2)}, u32[]{:S(2)}) collective-permute-start(f32[48,3,4,128]{3,2,1,0:T(4,128)S(1)} %slice.8), channel_id=1, source_target_pairs={{0,16},{16,32},{32,48},{48,64},{64,80},{80,96},{96,112},{112,128},... | collective-permute-start | bytes 884744 | tf_op jit(solution)/shard_map/ppermute | solution.py:618
  77.2 1.3 %collective-permute-start.3 = (f32[48,3,4,128]{3,2,1,0:T(4,128)S(1)}, f32[48,3,4,128]{3,2,1,0:T(4,128)S(1)}, u32[]{:S(2)}, u32[]{:S(2)}) collective-permute-start(f32[48,3,4,128]{3,2,1,0:T(4,128)S(1)} %slice.8), channel_id=1, source_target_pairs={{16,0},{32,16},{48,32},{64,48},{80,64},{96,80},{112,96},{128,112},... | collective-permute-start | bytes 884744 | tf_op jit(solution)/shard_map/ppermute | solution.py:618
  78.5 4.6 %collective-permute-start.4 = (f32[48,2,4,128]{3,2,1,0:T(4,128)S(1)}, f32[48,2,4,128]{3,2,1,0:T(4,128)S(1)}, u32[]{:S(2)}, u32[]{:S(2)}) collective-permute-start(f32[48,2,4,128]{3,2,1,0:T(4,128)S(1)} %slice.9), channel_id=1, source_target_pairs={{0,16},{16,32},{32,48},{48,64},{64,80},{80,96},{96,112},{112,128},... | collective-permute-start | bytes 589832 | tf_op jit(solution)/shard_map/ppermute | solution.py:618
  83.1 1.3 %collective-permute-start.5 = (f32[48,2,4,128]{3,2,1,0:T(4,128)S(1)}, f32[48,2,4,128]{3,2,1,0:T(4,128)S(1)}, u32[]{:S(2)}, u32[]{:S(2)}) collective-permute-start(f32[48,2,4,128]{3,2,1,0:T(4,128)S(1)} %slice.9), channel_id=1, source_target_pairs={{16,0},{32,16},{48,32},{64,48},{80,64},{96,80},{112,96},{128,112},... | collective-permute-start | bytes 589832 | tf_op jit(solution)/shard_map/ppermute | solution.py:618
  84.4 1.8 %collective-permute-done.4.shallow = f32[48,2,4,128]{3,2,1,0:T(4,128)S(1)} collective-permute-done((f32[48,2,4,128]{3,2,1,0:T(4,128)S(1)}, f32[48,2,4,128]{3,2,1,0:T(4,128)S(1)}, u32[]{:S(2)}, u32[]{:S(2)}) %collective-permute-start.4) | collective-permute-done | bytes 196640 | tf_op jit(solution)/shard_map/ppermute | solution.py:618
  86.3 4.4 %collective-permute-done.5.deep = f32[48,2,4,128]{3,2,1,0:T(4,128)S(1)} collective-permute-done((f32[48,2,4,128]{3,2,1,0:T(4,128)S(1)}, f32[48,2,4,128]{3,2,1,0:T(4,128)S(1)}, u32[]{:S(2)}, u32[]{:S(2)}) %collective-permute-start.5) | collective-permute-done | bytes 196640 | tf_op jit(solution)/shard_map/ppermute | solution.py:618
  90.7 0.0 copy-done
  90.7 4.6 %setup.1 = (f32[3,16,24,128]{3,2,1,0:T(8,128)S(1)}, f32[3,16,24,128]{3,2,1,0:T(8,128)S(1)}, f32[3,16,24,128]{3,2,1,0:T(8,128)S(1)}, f32[3,65,24,128]{3,2,1,0:T(8...) custom-call(s32[3]{0:T(128)S(1)} %copy-done, ...), custom_call_target="tpu_custom_call" | custom-call | flops 134217728 | tf_op jit(solution)/shard_map/setup/pallas_call | solution.py:561
  95.3 0.0 collective-permute-done.2.shallow
  95.3 0.0 collective-permute-done.3.deep
  95.3 10.7 %lines.1 = f32[16,3,4,128]{3,2,1,0:T(4,128)S(1)} custom-call(s32[3]{0:T(128)S(1)} %copy-done, f32[48,5,4,128]{3,2,1,0:T(4,128)S(1)} %constant_dynamic-update-slice_fusion.middle, f32[48,3,4,128]{3,2,1,0:T(4,128)S(1)} %collective-permute-done.2.shallow, f32[48,3,4,128]{3,2,1,0:T(4,128)S(1)} %collective-permute-done.3.deep, ...), custom_call_target="tpu_custom_call" | custom-call | flops 134217728 | tf_op jit(solution)/shard_map/lines/pallas_call | solution.py:575
  106.0 20.3 %all_to_all.11.packed = f32[16,3,4,128]{3,2,1,0:T(4,128)S(1)} all-to-all(f32[16,3,4,128]{3,2,1,0:T(4,128)S(1)} %lines.1), channel_id=1, replica_groups=mesh['period'=2,'gx'=16,'gy'=8,'gz'=2] {'gx'}, dimensions={0} | all-to-all | bytes 196608 | tf_op jit(solution)/shard_map/all_to_all | solution.py:597
  126.3 1.5 %unpack.1 = f32[2,3,4,8,128]{4,3,2,1,0:T(8,128)} custom-call(s32[3]{0:T(128)} %pad_add_fusion.place, f32[16,3,4,128]{3,2,1,0:T(4,128)S(1)} %all_to_all.11.packed), custom_call_target="tpu_custom_call" | custom-call | tf_op jit(solution)/shard_map/unpack/pallas_call | solution.py:543
  (5 shorter events, 0.1 us)
Async XLA Ops:
  0.6 90.1 %copy-start = (s32[3]{0:T(128)S(1)}, s32[3]{0:T(128)}, u32[]{:S(2)}) copy-start(s32[3]{0:T(128)} %pad_add_fusion.place) | copy-start | bytes 40
  60.5 7.6 %collective-permute-start = (f32[16,5,4,128]{3,2,1,0:T(4,128)S(1)}, f32[16,5,4,128]{3,2,1,0:T(4,128)S(1)}, u32[]{:S(2)}, u32[]{:S(2)}) collective-permute-start(f32[16,5,4,128]{3,2,1,0:T(4,128)S(1)} %all_to_all.10), channel_id=1, source_target_pairs={{0,2},{16,18},{32,34},{48,50},{64,66},{80,82},{96,98},{112,114},{1... | collective-permute-start | bytes 491528 | tf_op jit(solution)/shard_map/ppermute | solution.py:618
  65.3 8.5 %collective-permute-start.1 = (f32[16,5,4,128]{3,2,1,0:T(4,128)S(1)}, f32[16,5,4,128]{3,2,1,0:T(4,128)S(1)}, u32[]{:S(2)}, u32[]{:S(2)}) collective-permute-start(f32[16,5,4,128]{3,2,1,0:T(4,128)S(1)} %all_to_all.10), channel_id=1, source_target_pairs={{241,243},{225,227},{209,211},{193,195},{177,179},{161,163},{145,1... | collective-permute-start | bytes 491528 | tf_op jit(solution)/shard_map/ppermute | solution.py:618
  73.8 21.5 %collective-permute-start.2 = (f32[48,3,4,128]{3,2,1,0:T(4,128)S(1)}, f32[48,3,4,128]{3,2,1,0:T(4,128)S(1)}, u32[]{:S(2)}, u32[]{:S(2)}) collective-permute-start(f32[48,3,4,128]{3,2,1,0:T(4,128)S(1)} %slice.8), channel_id=1, source_target_pairs={{0,16},{16,32},{32,48},{48,64},{64,80},{80,96},{96,112},{112,128},... | collective-permute-start | bytes 884744 | tf_op jit(solution)/shard_map/ppermute | solution.py:618
  77.2 18.1 %collective-permute-start.3 = (f32[48,3,4,128]{3,2,1,0:T(4,128)S(1)}, f32[48,3,4,128]{3,2,1,0:T(4,128)S(1)}, u32[]{:S(2)}, u32[]{:S(2)}) collective-permute-start(f32[48,3,4,128]{3,2,1,0:T(4,128)S(1)} %slice.8), channel_id=1, source_target_pairs={{16,0},{32,16},{48,32},{64,48},{80,64},{96,80},{112,96},{128,112},... | collective-permute-start | bytes 884744 | tf_op jit(solution)/shard_map/ppermute | solution.py:618
  78.5 7.8 %collective-permute-start.4 = (f32[48,2,4,128]{3,2,1,0:T(4,128)S(1)}, f32[48,2,4,128]{3,2,1,0:T(4,128)S(1)}, u32[]{:S(2)}, u32[]{:S(2)}) collective-permute-start(f32[48,2,4,128]{3,2,1,0:T(4,128)S(1)} %slice.9), channel_id=1, source_target_pairs={{0,16},{16,32},{32,48},{48,64},{64,80},{80,96},{96,112},{112,128},... | collective-permute-start | bytes 589832 | tf_op jit(solution)/shard_map/ppermute | solution.py:618
  83.1 7.6 %collective-permute-start.5 = (f32[48,2,4,128]{3,2,1,0:T(4,128)S(1)}, f32[48,2,4,128]{3,2,1,0:T(4,128)S(1)}, u32[]{:S(2)}, u32[]{:S(2)}) collective-permute-start(f32[48,2,4,128]{3,2,1,0:T(4,128)S(1)} %slice.9), channel_id=1, source_target_pairs={{16,0},{32,16},{48,32},{64,48},{80,64},{96,80},{112,96},{128,112},... | collective-permute-start | bytes 589832 | tf_op jit(solution)/shard_map/ppermute | solution.py:618

commit v6 on v5

--- a/solution.py
+++ b/solution.py
@@ -26,6 +26,7 @@
 ROWS = 3 * TILE
 DEPTH = 32
 HALF = TILE // 2
+AXES = ("gx", "gy", "gz")
 
 
 def lanes(shape):
@@ -67,8 +68,8 @@
 row_next, row_back, lane_next, lane_back = y_next, y_back, z_next, z_back
 
 
-def position_facts(place, sizes):
-    x, y, z = place[0], place[1], place[2]
+def position_facts(sizes):
+    x, y, z = (lax.axis_index(name) for name in AXES)
     flip = z % 2
     along = x + flip * (sizes[0] - 1 - 2 * x)
     before = jnp.where(along == 0, 1 - flip, flip)
@@ -78,12 +79,13 @@
     return corner_y, corner_z, (before, flip, after)
 
 
-def mirrored(place, index, count):
-    return index + place[2] % 2 * (count - 1 - 2 * index)
-
-
-def pack_body(place, residual, classes, edge_mask, class_weight, out):
+def mirrored(flip, index, count):
+    return index + flip * (count - 1 - 2 * index)
+
+
+def pack_body(residual, classes, edge_mask, class_weight, out):
     thick = classes.shape[0]
+    flip = lax.axis_index("gz") % 2
     slots = []
     for i in range(thick):
         labels = classes[i]
@@ -99,7 +101,7 @@
     block = 0
     for start in range(0, len(slots), 16):
         group = jnp.concatenate(slots[start : start + 16], axis=0)
-        block = send_group(group, lambda target: mirrored(place, target, 16), out, block)
+        block = send_group(group, lambda target: mirrored(flip, target, 16), out, block)
 
 
 def send_group(group, device, out, block):
@@ -133,10 +135,11 @@
     return jnp.where(lanes((64, 128)) % TILE < half, moved[:64], upper)
 
 
-def unpack_body(place, packed, out):
+def unpack_body(packed, out):
+    flip = lax.axis_index("gz") % 2
     for part in range(2):
         moved = receive_group(
-            lambda window, block: packed[mirrored(place, window, 16), block], 2 * part, part == 0
+            lambda window, block: packed[mirrored(flip, window, 16), block], 2 * part, part == 0
         )
         for slot in range(moved.shape[0] // TILE):
             field, i = divmod(16 * part + slot, 4)
@@ -181,7 +184,6 @@
 
 def setup_body(
     sizes,
-    place,
     middle,
     shallow,
     deep,
@@ -198,7 +200,7 @@
     CQ,
     cells,
 ):
-    corner_y, corner_z, orders = position_facts(place, sizes)
+    corner_y, corner_z, orders = position_facts(sizes)
     extent_y, extent_z = sizes[1] * TILE, sizes[0] * sizes[2] * TILE
     shape = (ROWS, 128)
     lane = lanes(shape)
@@ -290,7 +292,6 @@
 
 def line_body(
     sizes,
-    place,
     middle,
     shallow,
     deep,
@@ -317,7 +318,7 @@
     OUT,
 ):
     shape = (ROWS, 128)
-    orders = position_facts(place, sizes)[2]
+    orders = position_facts(sizes)[2]
     even_row = lax.broadcasted_iota(jnp.int32, shape, 0) % 2 == 0
     even_lane = lanes(shape) % 2 == 0
     nothing = jnp.zeros(shape, f32)
@@ -528,54 +529,54 @@
     return pl.BlockSpec(memory_space=pltpu.SMEM)
 
 
-def pack(place, residual, classes, edge_mask, class_weight, **options):
+def pack(residual, classes, edge_mask, class_weight, **options):
     return pl.pallas_call(
         pack_body,
         out_shape=resident(16, 5, HALF, 128),
-        in_specs=[smem(), vmem(), vmem(), vmem(), smem()],
+        in_specs=[vmem(), vmem(), vmem(), smem()],
         out_specs=vmem(),
         name="pack",
         **options,
-    )(place, residual, classes, edge_mask, class_weight)
-
-
-def unpack(place, packed, shape, **options):
+    )(residual, classes, edge_mask, class_weight)
+
+
+def unpack(packed, shape, **options):
     return pl.pallas_call(
         unpack_body,
         out_shape=jax.ShapeDtypeStruct(shape, f32),
-        in_specs=[smem(), vmem()],
+        in_specs=[vmem()],
         out_specs=vmem(),
         name="unpack",
         **options,
-    )(place, packed)
+    )(packed)
 
 
 def resident(*shape):
     return pltpu.VMEM(shape, f32)
 
 
-def setup(sizes, place, middle, shallow, deep, **options):
+def setup(sizes, middle, shallow, deep, **options):
     line = resident(64, ROWS, 128)
     edge = resident(3, 16, ROWS, 128)
     weights = resident(3, 65, ROWS, 128)
     return pl.pallas_call(
         functools.partial(setup_body, sizes),
         out_shape=[edge, edge, edge, weights, weights] + [line] * 6,
-        in_specs=[smem(), vmem(), vmem(), vmem()],
+        in_specs=[vmem()] * 3,
         out_specs=[vmem()] * 11,
         scratch_shapes=[resident(1, 18, ROWS, 128)],
         name="setup",
         **options,
-    )(place, middle, shallow, deep)
-
-
-def lines(sizes, place, middle, shallow, deep, ready, **options):
+    )(middle, shallow, deep)
+
+
+def lines(sizes, middle, shallow, deep, ready, **options):
     edge = lambda count, levels: resident(count, levels, ROWS, 128)
     pair = resident(2, 64, ROWS, 128)
     return pl.pallas_call(
         functools.partial(line_body, sizes),
         out_shape=resident(16, 3, HALF, 128),
-        in_specs=[smem()] + [vmem()] * (3 + len(ready)),
+        in_specs=[vmem()] * (3 + len(ready)),
         out_specs=vmem(),
         scratch_shapes=[
             edge(6, 16),
@@ -590,7 +591,7 @@
         ],
         name="lines",
         **options,
-    )(place, middle, shallow, deep, *ready)
+    )(middle, shallow, deep, *ready)
 
 
 def swap(values):
@@ -598,8 +599,7 @@
 
 
 def per_device(residual, classes, edge_mask, class_weight):
-    size_x, size_y, size_z = (lax.axis_size(name) for name in ("gx", "gy", "gz"))
-    axes = ("gx", "gy", "gz")
+    size_x, size_y, size_z = (lax.axis_size(name) for name in AXES)
     tiles = size_x * size_z
 
     def position(y, tile):
@@ -615,11 +615,10 @@
                 next_y = y - step_y if tile // size_x % 2 else y + step_y
                 if 0 <= next_y < size_y and 0 <= tile + step_tile < tiles:
                     pairs.append((position(y, tile), position(next_y, tile + step_tile)))
-        return lax.ppermute(values, axes, pairs)
+        return lax.ppermute(values, AXES, pairs)
 
     sizes = (size_x, size_y, size_z)
-    place = jnp.stack([lax.axis_index(name) for name in axes]).astype(jnp.int32)
-    own = swap(pack(place, residual, classes, edge_mask, class_weight))
+    own = swap(pack(residual, classes, edge_mask, class_weight))
     middle = jnp.concatenate([from_side(own, 1, 0), own, from_side(own, -1, 0)], axis=0)
     material, source = middle[:, :2], middle[:, 2:]
     shallow_material = from_side(material, 0, 1)
@@ -630,10 +629,10 @@
         compiler_params=pltpu.CompilerParams(vmem_limit_bytes=size * 2**20),
         cost_estimate=pl.CostEstimate(flops=cost, bytes_accessed=0, transcendentals=0),
     )
-    ready = setup(sizes, place, middle, shallow_material, deep_material, **options(20, 2**27))
-    result = swap(lines(sizes, place, middle, shallow_source, deep_source, ready, **options(32, 2**27)))
+    ready = setup(sizes, middle, shallow_material, deep_material, **options(20, 2**27))
+    result = swap(lines(sizes, middle, shallow_source, deep_source, ready, **options(32, 2**27)))
     result = pltpu.with_memory_space_constraint(result, pltpu.VMEM)
-    return unpack(place, result, residual.shape)
+    return unpack(result, residual.shape)
 
 
 def solution(mesh):

time: 128 us -> 126 us (0.984)
  Pallas kernels: 17.9 us -> 15.9 us
  transfers between devices with their start and end apart: 6 -> 6, of which waited for: 4 -> 4; matrix products, arithmetic and copies ran while one was open for 0% -> 0% of each run, Pallas kernels for 4% -> 3%
where the time goes in v6:
time: 126 us; the launch traced here: 125 us
  blocking collectives  79.1 us (63%)
  starting transfers between devices  17.3 us (14%)
  Pallas kernels  15.9 us (13%)
  waiting for transfers between devices  12.7 us (10%)
    all_to_all x2, blocking collectives, swap(): return lax.all_to_all(values, 'gx', 0, 0, tiled=True)  79.1 us
    ppermute x6, starting transfers between devices, from_side(): return lax.ppermute(values, AXES, pairs)  17.3 us
    ppermute x6, waiting for transfers between devices, from_side(): return lax.ppermute(values, AXES, pairs)  12.7 us
    pallas_call x1, Pallas kernels, lines(): pl.pallas_call(functools.partial(line_body, sizes), out_shape=resident(16...  10 us
    pallas_call x1, Pallas kernels, setup(): pl.pallas_call(functools.partial(setup_body, sizes), out_shape=[edge, edg...  3.98 us
  transfers between devices with their start and end apart: 6, of which 4 were waited for; matrix products, arithmetic and copies ran while one was open for 0% of the time, Pallas kernels for 3%

profile of v6, /device:TPU:86, one launch (start us, length us, event | category | flops | bytes accessed | tf_op | source)
XLA Modules:
  0.0 125.2 jit_solution(1812427916878207378)
XLA Ops:
  0.0 1.1 pack.1
  1.1 58.8 %all_to_all.10 = f32[16,5,4,128]{3,2,1,0:T(4,128)S(1)} all-to-all(f32[16,5,4,128]{3,2,1,0:T(4,128)S(1)} %pack.1), channel_id=1, replica_groups=mesh['period'=2,'gx'=16,'gy'=8,'gz'=2] {'gx'}, dimensions={0} | all-to-all | bytes 327680 | tf_op jit(solution)/shard_map/all_to_all | solution.py:598
  59.9 4.8 %collective-permute-start = (f32[16,5,4,128]{3,2,1,0:T(4,128)S(1)}, f32[16,5,4,128]{3,2,1,0:T(4,128)S(1)}, u32[]{:S(2)}, u32[]{:S(2)}) collective-permute-start(f32[16,5,4,128]{3,2,1,0:T(4,128)S(1)} %all_to_all.10), channel_id=1, source_target_pairs={{0,2},{16,18},{32,34},{48,50},{64,66},{80,82},{96,98},{112,114},{1... | collective-permute-start | bytes 491528 | tf_op jit(solution)/shard_map/ppermute | solution.py:618
  64.6 2.0 %collective-permute-start.1 = (f32[16,5,4,128]{3,2,1,0:T(4,128)S(1)}, f32[16,5,4,128]{3,2,1,0:T(4,128)S(1)}, u32[]{:S(2)}, u32[]{:S(2)}) collective-permute-start(f32[16,5,4,128]{3,2,1,0:T(4,128)S(1)} %all_to_all.10), channel_id=1, source_target_pairs={{241,243},{225,227},{209,211},{193,195},{177,179},{161,163},{145,1... | collective-permute-start | bytes 491528 | tf_op jit(solution)/shard_map/ppermute | solution.py:618
  66.6 0.9 collective-permute-done
  67.5 5.6 %collective-permute-done.1 = f32[16,5,4,128]{3,2,1,0:T(4,128)S(1)} collective-permute-done((f32[16,5,4,128]{3,2,1,0:T(4,128)S(1)}, f32[16,5,4,128]{3,2,1,0:T(4,128)S(1)}, u32[]{:S(2)}, u32[]{:S(2)}) %collective-permute-start.1) | collective-permute-done | bytes 163872 | tf_op jit(solution)/shard_map/ppermute | solution.py:618
  73.2 3.4 %collective-permute-start.2 = (f32[48,3,4,128]{3,2,1,0:T(4,128)S(1)}, f32[48,3,4,128]{3,2,1,0:T(4,128)S(1)}, u32[]{:S(2)}, u32[]{:S(2)}) collective-permute-start(f32[48,3,4,128]{3,2,1,0:T(4,128)S(1)} %slice.8), channel_id=1, source_target_pairs={{0,16},{16,32},{32,48},{48,64},{64,80},{80,96},{96,112},{112,128},... | collective-permute-start | bytes 884744 | tf_op jit(solution)/shard_map/ppermute | solution.py:618
  76.5 1.3 %collective-permute-start.3 = (f32[48,3,4,128]{3,2,1,0:T(4,128)S(1)}, f32[48,3,4,128]{3,2,1,0:T(4,128)S(1)}, u32[]{:S(2)}, u32[]{:S(2)}) collective-permute-start(f32[48,3,4,128]{3,2,1,0:T(4,128)S(1)} %slice.8), channel_id=1, source_target_pairs={{16,0},{32,16},{48,32},{64,48},{80,64},{96,80},{112,96},{128,112},... | collective-permute-start | bytes 884744 | tf_op jit(solution)/shard_map/ppermute | solution.py:618
  77.9 4.6 %collective-permute-start.4 = (f32[48,2,4,128]{3,2,1,0:T(4,128)S(1)}, f32[48,2,4,128]{3,2,1,0:T(4,128)S(1)}, u32[]{:S(2)}, u32[]{:S(2)}) collective-permute-start(f32[48,2,4,128]{3,2,1,0:T(4,128)S(1)} %slice.9), channel_id=1, source_target_pairs={{0,16},{16,32},{32,48},{48,64},{64,80},{80,96},{96,112},{112,128},... | collective-permute-start | bytes 589832 | tf_op jit(solution)/shard_map/ppermute | solution.py:618
  82.5 1.3 %collective-permute-start.5 = (f32[48,2,4,128]{3,2,1,0:T(4,128)S(1)}, f32[48,2,4,128]{3,2,1,0:T(4,128)S(1)}, u32[]{:S(2)}, u32[]{:S(2)}) collective-permute-start(f32[48,2,4,128]{3,2,1,0:T(4,128)S(1)} %slice.9), channel_id=1, source_target_pairs={{16,0},{32,16},{48,32},{64,48},{80,64},{96,80},{112,96},{128,112},... | collective-permute-start | bytes 589832 | tf_op jit(solution)/shard_map/ppermute | solution.py:618
  83.8 1.8 %collective-permute-done.4.shallow = f32[48,2,4,128]{3,2,1,0:T(4,128)S(1)} collective-permute-done((f32[48,2,4,128]{3,2,1,0:T(4,128)S(1)}, f32[48,2,4,128]{3,2,1,0:T(4,128)S(1)}, u32[]{:S(2)}, u32[]{:S(2)}) %collective-permute-start.4) | collective-permute-done | bytes 196640 | tf_op jit(solution)/shard_map/ppermute | solution.py:618
  85.6 4.4 %collective-permute-done.5.deep = f32[48,2,4,128]{3,2,1,0:T(4,128)S(1)} collective-permute-done((f32[48,2,4,128]{3,2,1,0:T(4,128)S(1)}, f32[48,2,4,128]{3,2,1,0:T(4,128)S(1)}, u32[]{:S(2)}, u32[]{:S(2)}) %collective-permute-start.5) | collective-permute-done | bytes 196640 | tf_op jit(solution)/shard_map/ppermute | solution.py:618
  90.1 4.0 %setup.1 = (f32[3,16,24,128]{3,2,1,0:T(8,128)S(1)}, f32[3,16,24,128]{3,2,1,0:T(8,128)S(1)}, f32[3,16,24,128]{3,2,1,0:T(8,128)S(1)}, f32[3,65,24,128]{3,2,1,0:T(8...) custom-call(f32[48,5,4,128]{3,2,1,0:T(4,128)S(1)} %constant_dynamic-, ...), custom_call_target="tpu_custom_call" | custom-call | flops 134217728 | tf_op jit(solution)/shard_map/setup/pallas_call | solution.py:562
  94.1 0.0 collective-permute-done.2.shallow
  94.1 0.0 collective-permute-done.3.deep
  94.1 10.0 %lines.1 = f32[16,3,4,128]{3,2,1,0:T(4,128)S(1)} custom-call(f32[48,5,4,128]{3,2,1,0:T(4,128)S(1)} %constant_dynamic-update-slice_fusion.middle, f32[48,3,4,128]{3,2,1,0:T(4,128)S(1)} %collective-permute-done.2.shallow, f32[48,3,4,128]{3,2,1,0:T(4,128)S(1)} %collective-permute-done.3.deep, f32[3,16,24,128]{3,2,1,0:T(8,128)S(1)} %get-tuple-element.16.free, ...), custom_call_target="tpu_custom_call" | custom-call | flops 134217728 | tf_op jit(solution)/shard_map/lines/pallas_call | solution.py:576
  104.1 20.3 %all_to_all.11.packed = f32[16,3,4,128]{3,2,1,0:T(4,128)S(1)} all-to-all(f32[16,3,4,128]{3,2,1,0:T(4,128)S(1)} %lines.1), channel_id=1, replica_groups=mesh['period'=2,'gx'=16,'gy'=8,'gz'=2] {'gx'}, dimensions={0} | all-to-all | bytes 196608 | tf_op jit(solution)/shard_map/all_to_all | solution.py:598
  124.4 0.9 unpack.1
  (5 shorter events, 0.1 us)
Async XLA Ops:
  59.9 7.6 %collective-permute-start = (f32[16,5,4,128]{3,2,1,0:T(4,128)S(1)}, f32[16,5,4,128]{3,2,1,0:T(4,128)S(1)}, u32[]{:S(2)}, u32[]{:S(2)}) collective-permute-start(f32[16,5,4,128]{3,2,1,0:T(4,128)S(1)} %all_to_all.10), channel_id=1, source_target_pairs={{0,2},{16,18},{32,34},{48,50},{64,66},{80,82},{96,98},{112,114},{1... | collective-permute-start | bytes 491528 | tf_op jit(solution)/shard_map/ppermute | solution.py:618
  64.6 8.5 %collective-permute-start.1 = (f32[16,5,4,128]{3,2,1,0:T(4,128)S(1)}, f32[16,5,4,128]{3,2,1,0:T(4,128)S(1)}, u32[]{:S(2)}, u32[]{:S(2)}) collective-permute-start(f32[16,5,4,128]{3,2,1,0:T(4,128)S(1)} %all_to_all.10), channel_id=1, source_target_pairs={{241,243},{225,227},{209,211},{193,195},{177,179},{161,163},{145,1... | collective-permute-start | bytes 491528 | tf_op jit(solution)/shard_map/ppermute | solution.py:618
  73.2 20.9 %collective-permute-start.2 = (f32[48,3,4,128]{3,2,1,0:T(4,128)S(1)}, f32[48,3,4,128]{3,2,1,0:T(4,128)S(1)}, u32[]{:S(2)}, u32[]{:S(2)}) collective-permute-start(f32[48,3,4,128]{3,2,1,0:T(4,128)S(1)} %slice.8), channel_id=1, source_target_pairs={{0,16},{16,32},{32,48},{48,64},{64,80},{80,96},{96,112},{112,128},... | collective-permute-start | bytes 884744 | tf_op jit(solution)/shard_map/ppermute | solution.py:618
  76.5 17.5 %collective-permute-start.3 = (f32[48,3,4,128]{3,2,1,0:T(4,128)S(1)}, f32[48,3,4,128]{3,2,1,0:T(4,128)S(1)}, u32[]{:S(2)}, u32[]{:S(2)}) collective-permute-start(f32[48,3,4,128]{3,2,1,0:T(4,128)S(1)} %slice.8), channel_id=1, source_target_pairs={{16,0},{32,16},{48,32},{64,48},{80,64},{96,80},{112,96},{128,112},... | collective-permute-start | bytes 884744 | tf_op jit(solution)/shard_map/ppermute | solution.py:618
  77.9 7.8 %collective-permute-start.4 = (f32[48,2,4,128]{3,2,1,0:T(4,128)S(1)}, f32[48,2,4,128]{3,2,1,0:T(4,128)S(1)}, u32[]{:S(2)}, u32[]{:S(2)}) collective-permute-start(f32[48,2,4,128]{3,2,1,0:T(4,128)S(1)} %slice.9), channel_id=1, source_target_pairs={{0,16},{16,32},{32,48},{48,64},{64,80},{80,96},{96,112},{112,128},... | collective-permute-start | bytes 589832 | tf_op jit(solution)/shard_map/ppermute | solution.py:618
  82.5 7.6 %collective-permute-start.5 = (f32[48,2,4,128]{3,2,1,0:T(4,128)S(1)}, f32[48,2,4,128]{3,2,1,0:T(4,128)S(1)}, u32[]{:S(2)}, u32[]{:S(2)}) collective-permute-start(f32[48,2,4,128]{3,2,1,0:T(4,128)S(1)} %slice.9), channel_id=1, source_target_pairs={{16,0},{32,16},{48,32},{64,48},{80,64},{96,80},{112,96},{128,112},... | collective-permute-start | bytes 589832 | tf_op jit(solution)/shard_map/ppermute | solution.py:618

commit v7 on v6

--- a/solution.py
+++ b/solution.py
@@ -6,7 +6,6 @@
 from jax.experimental import pallas as pl
 from jax.experimental.pallas import tpu as pltpu
 from jax.sharding import PartitionSpec as P
-
 
 aspect = 2.0
 face_weight = (1.0 / (aspect * aspect), 1.0, 1.0)
@@ -24,6 +23,7 @@
 f32 = jnp.float32
 TILE = 8
 ROWS = 3 * TILE
+GROUPS = 4
 DEPTH = 32
 HALF = TILE // 2
 AXES = ("gx", "gy", "gz")
@@ -322,7 +322,6 @@
     even_row = lax.broadcasted_iota(jnp.int32, shape, 0) % 2 == 0
     even_lane = lanes(shape) % 2 == 0
     nothing = jnp.zeros(shape, f32)
-
     def put(field, level, y, values):
         rows = slice(TILE * y, TILE * y + TILE)
         source = values * free[field % 3, level, rows, :]
@@ -330,7 +329,7 @@
         E[field, level + 1, rows, :] = source * Dm[field % 3, level, rows, :]
 
     spread_out(
-        ((shallow, 0, orders[0]), (middle, 2, orders[1]), (deep, 0, orders[2])),
+        ((shallow, 2, orders[0]), (middle, 2, orders[1]), (deep, 2, orders[2])),
         (True, False),
         put,
     )
@@ -620,17 +619,13 @@
     sizes = (size_x, size_y, size_z)
     own = swap(pack(residual, classes, edge_mask, class_weight))
     middle = jnp.concatenate([from_side(own, 1, 0), own, from_side(own, -1, 0)], axis=0)
-    material, source = middle[:, :2], middle[:, 2:]
-    shallow_material = from_side(material, 0, 1)
-    deep_material = from_side(material, 0, -1)
-    shallow_source = from_side(source, 0, 1)
-    deep_source = from_side(source, 0, -1)
+    shallow, deep = from_side(middle, 0, 1), from_side(middle, 0, -1)
     options = lambda size, cost: dict(
         compiler_params=pltpu.CompilerParams(vmem_limit_bytes=size * 2**20),
         cost_estimate=pl.CostEstimate(flops=cost, bytes_accessed=0, transcendentals=0),
     )
-    ready = setup(sizes, middle, shallow_material, deep_material, **options(20, 2**27))
-    result = swap(lines(sizes, middle, shallow_source, deep_source, ready, **options(32, 2**27)))
+    ready = setup(sizes, middle, shallow, deep, **options(20, 2**27))
+    result = swap(lines(sizes, middle, shallow, deep, ready, **options(32, 2**27)))
     result = pltpu.with_memory_space_constraint(result, pltpu.VMEM)
     return unpack(result, residual.shape)
 

time: 126 us -> 122 us (0.968)
  starting transfers between devices: 17.3 us -> 12.6 us
  waiting for transfers between devices: 12.7 us -> 14.6 us
    ppermute x6 -> x4, starting transfers between devices: 17.3 us -> 12.6 us  [from_side(): return lax.ppermute(values, AXES, pairs)]
    ppermute x6 -> x4, waiting for transfers between devices: 12.7 us -> 14.6 us  [from_side(): return lax.ppermute(values, AXES, pairs)]
  transfers between devices with their start and end apart: 6 -> 4, of which waited for: 4 -> 3; matrix products, arithmetic and copies ran while one was open for 0% -> 0% of each run, Pallas kernels for 3% -> 0%
where the time goes in v7:
time: 122 us
  blocking collectives  78.5 us (64%)
  Pallas kernels  15.9 us (13%)
  waiting for transfers between devices  14.6 us (12%)
  starting transfers between devices  12.6 us (10%)
    all_to_all x2, blocking collectives, swap(): return lax.all_to_all(values, 'gx', 0, 0, tiled=True)  78.5 us
    ppermute x4, waiting for transfers between devices, from_side(): return lax.ppermute(values, AXES, pairs)  14.6 us
    ppermute x4, starting transfers between devices, from_side(): return lax.ppermute(values, AXES, pairs)  12.6 us
    pallas_call x1, Pallas kernels, lines(): pl.pallas_call(functools.partial(line_body, sizes), out_shape=resident(16...  10 us
    pallas_call x1, Pallas kernels, setup(): pl.pallas_call(functools.partial(setup_body, sizes), out_shape=[edge, edg...  3.98 us
  transfers between devices with their start and end apart: 4, of which 3 were waited for; matrix products, arithmetic and copies ran while one was open for 0% of the time, Pallas kernels for 0%

profile of v7, /device:TPU:86, one launch (start us, length us, event | category | flops | bytes accessed | tf_op | source)
XLA Modules:
  0.0 121.8 jit_solution(15092660649206088900)
XLA Ops:
  0.0 1.1 pack.1
  1.1 58.8 %all_to_all.10 = f32[16,5,4,128]{3,2,1,0:T(4,128)S(1)} all-to-all(f32[16,5,4,128]{3,2,1,0:T(4,128)S(1)} %pack.1), channel_id=1, replica_groups=mesh['period'=2,'gx'=16,'gy'=8,'gz'=2] {'gx'}, dimensions={0} | all-to-all | bytes 327680 | tf_op jit(solution)/shard_map/all_to_all | solution.py:597
  59.9 4.8 %collective-permute-start = (f32[16,5,4,128]{3,2,1,0:T(4,128)S(1)}, f32[16,5,4,128]{3,2,1,0:T(4,128)S(1)}, u32[]{:S(2)}, u32[]{:S(2)}) collective-permute-start(f32[16,5,4,128]{3,2,1,0:T(4,128)S(1)} %all_to_all.10), channel_id=1, source_target_pairs={{0,2},{16,18},{32,34},{48,50},{64,66},{80,82},{96,98},{112,114},{1... | collective-permute-start | bytes 491528 | tf_op jit(solution)/shard_map/ppermute | solution.py:617
  64.6 2.0 %collective-permute-start.1 = (f32[16,5,4,128]{3,2,1,0:T(4,128)S(1)}, f32[16,5,4,128]{3,2,1,0:T(4,128)S(1)}, u32[]{:S(2)}, u32[]{:S(2)}) collective-permute-start(f32[16,5,4,128]{3,2,1,0:T(4,128)S(1)} %all_to_all.10), channel_id=1, source_target_pairs={{241,243},{225,227},{209,211},{193,195},{177,179},{161,163},{145,1... | collective-permute-start | bytes 491528 | tf_op jit(solution)/shard_map/ppermute | solution.py:617
  66.6 0.9 collective-permute-done
  67.5 5.6 %collective-permute-done.1 = f32[16,5,4,128]{3,2,1,0:T(4,128)S(1)} collective-permute-done((f32[16,5,4,128]{3,2,1,0:T(4,128)S(1)}, f32[16,5,4,128]{3,2,1,0:T(4,128)S(1)}, u32[]{:S(2)}, u32[]{:S(2)}) %collective-permute-start.1) | collective-permute-done | bytes 163872 | tf_op jit(solution)/shard_map/ppermute | solution.py:617
  73.1 1.3 %collective-permute-start.3 = (f32[48,5,4,128]{3,2,1,0:T(4,128)S(1)}, f32[48,5,4,128]{3,2,1,0:T(4,128)S(1)}, u32[]{:S(2)}, u32[]{:S(2)}) collective-permute-start(f32[48,5,4,128]{3,2,1,0:T(4,128)S(1)} %constant_dynamic-update-slice_fusion.middle), channel_id=1, source_target_pairs={{16,0},{32,16},{48,32},{64,48},{80,64},{96,80},{112,96},{128,112},... | collective-permute-start | bytes 1474568 | tf_op jit(solution)/shard_map/ppermute | solution.py:617
  74.4 4.6 %collective-permute-start.2 = (f32[48,5,4,128]{3,2,1,0:T(4,128)S(1)}, f32[48,5,4,128]{3,2,1,0:T(4,128)S(1)}, u32[]{:S(2)}, u32[]{:S(2)}) collective-permute-start(f32[48,5,4,128]{3,2,1,0:T(4,128)S(1)} %constant_dynamic-update-slice_fusion.middle), channel_id=1, source_target_pairs={{0,16},{16,32},{32,48},{48,64},{64,80},{80,96},{96,112},{112,128},... | collective-permute-start | bytes 1474568 | tf_op jit(solution)/shard_map/ppermute | solution.py:617
  79.1 8.2 %collective-permute-done.3.deep = f32[48,5,4,128]{3,2,1,0:T(4,128)S(1)} collective-permute-done((f32[48,5,4,128]{3,2,1,0:T(4,128)S(1)}, f32[48,5,4,128]{3,2,1,0:T(4,128)S(1)}, u32[]{:S(2)}, u32[]{:S(2)}) %collective-permute-start.3) | collective-permute-done | bytes 491552 | tf_op jit(solution)/shard_map/ppermute | solution.py:617
  87.2 0.0 collective-permute-done.2.shallow
  87.2 4.0 %setup.1 = (f32[3,16,24,128]{3,2,1,0:T(8,128)S(1)}, f32[3,16,24,128]{3,2,1,0:T(8,128)S(1)}, f32[3,16,24,128]{3,2,1,0:T(8,128)S(1)}, f32[3,65,24,128]{3,2,1,0:T(8...) custom-call(f32[48,5,4,128]{3,2,1,0:T(4,128)S(1)} %constant_dynamic-, ...), custom_call_target="tpu_custom_call" | custom-call | flops 134217728 | tf_op jit(solution)/shard_map/setup/pallas_call | solution.py:561
  91.2 10.0 %lines.1 = f32[16,3,4,128]{3,2,1,0:T(4,128)S(1)} custom-call(f32[48,5,4,128]{3,2,1,0:T(4,128)S(1)} %constant_dynamic-update-slice_fusion.middle, f32[48,5,4,128]{3,2,1,0:T(4,128)S(1)} %collective-permute-done.2.shallow, f32[48,5,4,128]{3,2,1,0:T(4,128)S(1)} %collective-permute-done.3.deep, f32[3,16,24,128]{3,2,1,0:T(8,128)S(1)} %get-tuple-element.16.free, ...), custom_call_target="tpu_custom_call" | custom-call | flops 134217728 | tf_op jit(solution)/shard_map/lines/pallas_call | solution.py:575
  101.3 19.7 %all_to_all.11.packed = f32[16,3,4,128]{3,2,1,0:T(4,128)S(1)} all-to-all(f32[16,3,4,128]{3,2,1,0:T(4,128)S(1)} %lines.1), channel_id=1, replica_groups=mesh['period'=2,'gx'=16,'gy'=8,'gz'=2] {'gx'}, dimensions={0} | all-to-all | bytes 196608 | tf_op jit(solution)/shard_map/all_to_all | solution.py:597
  121.0 0.9 unpack.1
  (3 shorter events, 0.1 us)
Async XLA Ops:
  59.9 7.6 %collective-permute-start = (f32[16,5,4,128]{3,2,1,0:T(4,128)S(1)}, f32[16,5,4,128]{3,2,1,0:T(4,128)S(1)}, u32[]{:S(2)}, u32[]{:S(2)}) collective-permute-start(f32[16,5,4,128]{3,2,1,0:T(4,128)S(1)} %all_to_all.10), channel_id=1, source_target_pairs={{0,2},{16,18},{32,34},{48,50},{64,66},{80,82},{96,98},{112,114},{1... | collective-permute-start | bytes 491528 | tf_op jit(solution)/shard_map/ppermute | solution.py:617
  64.6 8.5 %collective-permute-start.1 = (f32[16,5,4,128]{3,2,1,0:T(4,128)S(1)}, f32[16,5,4,128]{3,2,1,0:T(4,128)S(1)}, u32[]{:S(2)}, u32[]{:S(2)}) collective-permute-start(f32[16,5,4,128]{3,2,1,0:T(4,128)S(1)} %all_to_all.10), channel_id=1, source_target_pairs={{241,243},{225,227},{209,211},{193,195},{177,179},{161,163},{145,1... | collective-permute-start | bytes 491528 | tf_op jit(solution)/shard_map/ppermute | solution.py:617
  73.1 14.1 %collective-permute-start.3 = (f32[48,5,4,128]{3,2,1,0:T(4,128)S(1)}, f32[48,5,4,128]{3,2,1,0:T(4,128)S(1)}, u32[]{:S(2)}, u32[]{:S(2)}) collective-permute-start(f32[48,5,4,128]{3,2,1,0:T(4,128)S(1)} %constant_dynamic-update-slice_fusion.middle), channel_id=1, source_target_pairs={{16,0},{32,16},{48,32},{64,48},{80,64},{96,80},{112,96},{128,112},... | collective-permute-start | bytes 1474568 | tf_op jit(solution)/shard_map/ppermute | solution.py:617
  74.4 12.8 %collective-permute-start.2 = (f32[48,5,4,128]{3,2,1,0:T(4,128)S(1)}, f32[48,5,4,128]{3,2,1,0:T(4,128)S(1)}, u32[]{:S(2)}, u32[]{:S(2)}) collective-permute-start(f32[48,5,4,128]{3,2,1,0:T(4,128)S(1)} %constant_dynamic-update-slice_fusion.middle), channel_id=1, source_target_pairs={{0,16},{16,32},{32,48},{48,64},{64,80},{80,96},{96,112},{112,128},... | collective-permute-start | bytes 1474568 | tf_op jit(solution)/shard_map/ppermute | solution.py:617

commit v8 on v7

--- a/solution.py
+++ b/solution.py
@@ -6,6 +6,7 @@
 from jax.experimental import pallas as pl
 from jax.experimental.pallas import tpu as pltpu
 from jax.sharding import PartitionSpec as P
+
 
 aspect = 2.0
 face_weight = (1.0 / (aspect * aspect), 1.0, 1.0)
@@ -23,7 +24,6 @@
 f32 = jnp.float32
 TILE = 8
 ROWS = 3 * TILE
-GROUPS = 4
 DEPTH = 32
 HALF = TILE // 2
 AXES = ("gx", "gy", "gz")
@@ -322,6 +322,7 @@
     even_row = lax.broadcasted_iota(jnp.int32, shape, 0) % 2 == 0
     even_lane = lanes(shape) % 2 == 0
     nothing = jnp.zeros(shape, f32)
+
     def put(field, level, y, values):
         rows = slice(TILE * y, TILE * y + TILE)
         source = values * free[field % 3, level, rows, :]
@@ -329,7 +330,7 @@
         E[field, level + 1, rows, :] = source * Dm[field % 3, level, rows, :]
 
     spread_out(
-        ((shallow, 2, orders[0]), (middle, 2, orders[1]), (deep, 2, orders[2])),
+        ((shallow, 2, orders[0]), (middle, 2, orders[1]), (deep, 0, orders[2])),
         (True, False),
         put,
     )
@@ -619,13 +620,15 @@
     sizes = (size_x, size_y, size_z)
     own = swap(pack(residual, classes, edge_mask, class_weight))
     middle = jnp.concatenate([from_side(own, 1, 0), own, from_side(own, -1, 0)], axis=0)
-    shallow, deep = from_side(middle, 0, 1), from_side(middle, 0, -1)
+    shallow = from_side(middle, 0, 1)
+    deep_material = from_side(middle[:, :2], 0, -1)
+    deep_source = from_side(middle[:, 2:], 0, -1)
     options = lambda size, cost: dict(
         compiler_params=pltpu.CompilerParams(vmem_limit_bytes=size * 2**20),
         cost_estimate=pl.CostEstimate(flops=cost, bytes_accessed=0, transcendentals=0),
     )
-    ready = setup(sizes, middle, shallow, deep, **options(20, 2**27))
-    result = swap(lines(sizes, middle, shallow, deep, ready, **options(32, 2**27)))
+    ready = setup(sizes, middle, shallow, deep_material, **options(20, 2**27))
+    result = swap(lines(sizes, middle, shallow, deep_source, ready, **options(32, 2**27)))
     result = pltpu.with_memory_space_constraint(result, pltpu.VMEM)
     return unpack(result, residual.shape)
 

time: 122 us -> 123 us (level)
    ppermute x4 -> x5, waiting for transfers between devices: 14.6 us -> 14.5 us  [from_side(): return lax.ppermute(values, AXES, pairs)]
    ppermute x4 -> x5, starting transfers between devices: 12.6 us -> 12.7 us  [from_side(): return lax.ppermute(values, AXES, pairs)]
  transfers between devices with their start and end apart: 4 -> 5, of which waited for: 3 -> 3; matrix products, arithmetic and copies ran while one was open for 0% -> 0% of each run, Pallas kernels for 0% -> 3%
where the time goes in v8:
time: 123 us
  blocking collectives  79.3 us (64%)
  Pallas kernels  15.9 us (13%)
  waiting for transfers between devices  14.5 us (12%)
  starting transfers between devices  12.7 us (10%)
    all_to_all x2, blocking collectives, swap(): return lax.all_to_all(values, 'gx', 0, 0, tiled=True)  79.3 us
    ppermute x5, waiting for transfers between devices, from_side(): return lax.ppermute(values, AXES, pairs)  14.5 us
    ppermute x5, starting transfers between devices, from_side(): return lax.ppermute(values, AXES, pairs)  12.7 us
    pallas_call x1, Pallas kernels, lines(): pl.pallas_call(functools.partial(line_body, sizes), out_shape=resident(16...  10 us
    pallas_call x1, Pallas kernels, setup(): pl.pallas_call(functools.partial(setup_body, sizes), out_shape=[edge, edg...  3.98 us
  transfers between devices with their start and end apart: 5, of which 3 were waited for; matrix products, arithmetic and copies ran while one was open for 0% of the time, Pallas kernels for 3%

profile of v8, /device:TPU:86, one launch (start us, length us, event | category | flops | bytes accessed | tf_op | source)
XLA Modules:
  0.0 122.7 jit_solution(10473139322498314653)
XLA Ops:
  0.0 1.1 pack.1
  1.1 58.8 %all_to_all.10 = f32[16,5,4,128]{3,2,1,0:T(4,128)S(1)} all-to-all(f32[16,5,4,128]{3,2,1,0:T(4,128)S(1)} %pack.1), channel_id=1, replica_groups=mesh['period'=2,'gx'=16,'gy'=8,'gz'=2] {'gx'}, dimensions={0} | all-to-all | bytes 327680 | tf_op jit(solution)/shard_map/all_to_all | solution.py:598
  59.9 4.8 %collective-permute-start = (f32[16,5,4,128]{3,2,1,0:T(4,128)S(1)}, f32[16,5,4,128]{3,2,1,0:T(4,128)S(1)}, u32[]{:S(2)}, u32[]{:S(2)}) collective-permute-start(f32[16,5,4,128]{3,2,1,0:T(4,128)S(1)} %all_to_all.10), channel_id=1, source_target_pairs={{0,2},{16,18},{32,34},{48,50},{64,66},{80,82},{96,98},{112,114},{1... | collective-permute-start | bytes 491528 | tf_op jit(solution)/shard_map/ppermute | solution.py:618
  64.6 2.0 %collective-permute-start.1 = (f32[16,5,4,128]{3,2,1,0:T(4,128)S(1)}, f32[16,5,4,128]{3,2,1,0:T(4,128)S(1)}, u32[]{:S(2)}, u32[]{:S(2)}) collective-permute-start(f32[16,5,4,128]{3,2,1,0:T(4,128)S(1)} %all_to_all.10), channel_id=1, source_target_pairs={{241,243},{225,227},{209,211},{193,195},{177,179},{161,163},{145,1... | collective-permute-start | bytes 491528 | tf_op jit(solution)/shard_map/ppermute | solution.py:618
  66.6 0.9 collective-permute-done
  67.5 5.6 %collective-permute-done.1 = f32[16,5,4,128]{3,2,1,0:T(4,128)S(1)} collective-permute-done((f32[16,5,4,128]{3,2,1,0:T(4,128)S(1)}, f32[16,5,4,128]{3,2,1,0:T(4,128)S(1)}, u32[]{:S(2)}, u32[]{:S(2)}) %collective-permute-start.1) | collective-permute-done | bytes 163872 | tf_op jit(solution)/shard_map/ppermute | solution.py:618
  73.1 3.4 %collective-permute-start.2 = (f32[48,5,4,128]{3,2,1,0:T(4,128)S(1)}, f32[48,5,4,128]{3,2,1,0:T(4,128)S(1)}, u32[]{:S(2)}, u32[]{:S(2)}) collective-permute-start(f32[48,5,4,128]{3,2,1,0:T(4,128)S(1)} %constant_dynamic-update-slice_fusion.middle), channel_id=1, source_target_pairs={{0,16},{16,32},{32,48},{48,64},{64,80},{80,96},{96,112},{112,128},... | collective-permute-start | bytes 1474568 | tf_op jit(solution)/shard_map/ppermute | solution.py:618
  76.5 1.3 %collective-permute-start.3 = (f32[48,3,4,128]{3,2,1,0:T(4,128)S(1)}, f32[48,3,4,128]{3,2,1,0:T(4,128)S(1)}, u32[]{:S(2)}, u32[]{:S(2)}) collective-permute-start(f32[48,3,4,128]{3,2,1,0:T(4,128)S(1)} %slice.8), channel_id=1, source_target_pairs={{16,0},{32,16},{48,32},{64,48},{80,64},{96,80},{112,96},{128,112},... | collective-permute-start | bytes 884744 | tf_op jit(solution)/shard_map/ppermute | solution.py:618
  77.9 1.3 %collective-permute-start.4 = (f32[48,2,4,128]{3,2,1,0:T(4,128)S(1)}, f32[48,2,4,128]{3,2,1,0:T(4,128)S(1)}, u32[]{:S(2)}, u32[]{:S(2)}) collective-permute-start(f32[48,2,4,128]{3,2,1,0:T(4,128)S(1)} %slice.9), channel_id=1, source_target_pairs={{16,0},{32,16},{48,32},{64,48},{80,64},{96,80},{112,96},{128,112},... | collective-permute-start | bytes 589832 | tf_op jit(solution)/shard_map/ppermute | solution.py:618
  79.2 8.1 %collective-permute-done.4.deep = f32[48,2,4,128]{3,2,1,0:T(4,128)S(1)} collective-permute-done((f32[48,2,4,128]{3,2,1,0:T(4,128)S(1)}, f32[48,2,4,128]{3,2,1,0:T(4,128)S(1)}, u32[]{:S(2)}, u32[]{:S(2)}) %collective-permute-start.4) | collective-permute-done | bytes 196640 | tf_op jit(solution)/shard_map/ppermute | solution.py:618
  87.3 0.0 collective-permute-done.2.shallow
  87.3 4.0 %setup.1 = (f32[3,16,24,128]{3,2,1,0:T(8,128)S(1)}, f32[3,16,24,128]{3,2,1,0:T(8,128)S(1)}, f32[3,16,24,128]{3,2,1,0:T(8,128)S(1)}, f32[3,65,24,128]{3,2,1,0:T(8...) custom-call(f32[48,5,4,128]{3,2,1,0:T(4,128)S(1)} %constant_dynamic-, ...), custom_call_target="tpu_custom_call" | custom-call | flops 134217728 | tf_op jit(solution)/shard_map/setup/pallas_call | solution.py:562
  91.3 0.0 collective-permute-done.3.deep
  91.3 10.0 %lines.1 = f32[16,3,4,128]{3,2,1,0:T(4,128)S(1)} custom-call(f32[48,5,4,128]{3,2,1,0:T(4,128)S(1)} %constant_dynamic-update-slice_fusion.middle, f32[48,5,4,128]{3,2,1,0:T(4,128)S(1)} %collective-permute-done.2.shallow, f32[48,3,4,128]{3,2,1,0:T(4,128)S(1)} %collective-permute-done.3.deep, f32[3,16,24,128]{3,2,1,0:T(8,128)S(1)} %get-tuple-element.16.free, ...), custom_call_target="tpu_custom_call" | custom-call | flops 134217728 | tf_op jit(solution)/shard_map/lines/pallas_call | solution.py:576
  101.3 20.5 %all_to_all.11.packed = f32[16,3,4,128]{3,2,1,0:T(4,128)S(1)} all-to-all(f32[16,3,4,128]{3,2,1,0:T(4,128)S(1)} %lines.1), channel_id=1, replica_groups=mesh['period'=2,'gx'=16,'gy'=8,'gz'=2] {'gx'}, dimensions={0} | all-to-all | bytes 196608 | tf_op jit(solution)/shard_map/all_to_all | solution.py:598
  121.8 0.9 unpack.1
  (5 shorter events, 0.1 us)
Async XLA Ops:
  59.9 7.6 %collective-permute-start = (f32[16,5,4,128]{3,2,1,0:T(4,128)S(1)}, f32[16,5,4,128]{3,2,1,0:T(4,128)S(1)}, u32[]{:S(2)}, u32[]{:S(2)}) collective-permute-start(f32[16,5,4,128]{3,2,1,0:T(4,128)S(1)} %all_to_all.10), channel_id=1, source_target_pairs={{0,2},{16,18},{32,34},{48,50},{64,66},{80,82},{96,98},{112,114},{1... | collective-permute-start | bytes 491528 | tf_op jit(solution)/shard_map/ppermute | solution.py:618
  64.6 8.5 %collective-permute-start.1 = (f32[16,5,4,128]{3,2,1,0:T(4,128)S(1)}, f32[16,5,4,128]{3,2,1,0:T(4,128)S(1)}, u32[]{:S(2)}, u32[]{:S(2)}) collective-permute-start(f32[16,5,4,128]{3,2,1,0:T(4,128)S(1)} %all_to_all.10), channel_id=1, source_target_pairs={{241,243},{225,227},{209,211},{193,195},{177,179},{161,163},{145,1... | collective-permute-start | bytes 491528 | tf_op jit(solution)/shard_map/ppermute | solution.py:618
  73.1 14.2 %collective-permute-start.2 = (f32[48,5,4,128]{3,2,1,0:T(4,128)S(1)}, f32[48,5,4,128]{3,2,1,0:T(4,128)S(1)}, u32[]{:S(2)}, u32[]{:S(2)}) collective-permute-start(f32[48,5,4,128]{3,2,1,0:T(4,128)S(1)} %constant_dynamic-update-slice_fusion.middle), channel_id=1, source_target_pairs={{0,16},{16,32},{32,48},{48,64},{64,80},{80,96},{96,112},{112,128},... | collective-permute-start | bytes 1474568 | tf_op jit(solution)/shard_map/ppermute | solution.py:618
  76.5 14.7 %collective-permute-start.3 = (f32[48,3,4,128]{3,2,1,0:T(4,128)S(1)}, f32[48,3,4,128]{3,2,1,0:T(4,128)S(1)}, u32[]{:S(2)}, u32[]{:S(2)}) collective-permute-start(f32[48,3,4,128]{3,2,1,0:T(4,128)S(1)} %slice.8), channel_id=1, source_target_pairs={{16,0},{32,16},{48,32},{64,48},{80,64},{96,80},{112,96},{128,112},... | collective-permute-start | bytes 884744 | tf_op jit(solution)/shard_map/ppermute | solution.py:618
  77.9 9.4 %collective-permute-start.4 = (f32[48,2,4,128]{3,2,1,0:T(4,128)S(1)}, f32[48,2,4,128]{3,2,1,0:T(4,128)S(1)}, u32[]{:S(2)}, u32[]{:S(2)}) collective-permute-start(f32[48,2,4,128]{3,2,1,0:T(4,128)S(1)} %slice.9), channel_id=1, source_target_pairs={{16,0},{32,16},{48,32},{64,48},{80,64},{96,80},{112,96},{128,112},... | collective-permute-start | bytes 589832 | tf_op jit(solution)/shard_map/ppermute | solution.py:618

commit v9 on v7

--- a/solution.py
+++ b/solution.py
@@ -179,7 +179,7 @@
                     put(field, 4 * a + i, y, moved[TILE * slot : TILE * slot + TILE])
         return state
 
-    loop(4, step, 0, unroll=2)
+    loop(4, step, 0, unroll=4)
 
 
 def setup_body(
@@ -387,7 +387,7 @@
                 NS[part, 16 * g + l] = values
         return state
 
-    loop(16, to_nodes, 0, unroll=8)
+    loop(16, to_nodes, 0, unroll=16)
 
     def eliminate(source, inverse, back, parts, unroll=4):
         def step(x, state):
@@ -475,7 +475,7 @@
                 )
         return state
 
-    loop(16, from_nodes, 0, unroll=8)
+    loop(16, from_nodes, 0, unroll=16)
     for part in range(2):
         pad_high(Rm, 3 * part)
         pad_high(Rm, 3 * part + 1)

time: 122 us -> 121 us (level)
  no operation moved by 1% of the time
where the time goes in v9:
time: 121 us
  blocking collectives  78.5 us (65%)
  Pallas kernels  15.3 us (13%)
  waiting for transfers between devices  14.6 us (12%)
  starting transfers between devices  12.6 us (10%)
    all_to_all x2, blocking collectives, swap(): return lax.all_to_all(values, 'gx', 0, 0, tiled=True)  78.5 us
    ppermute x4, waiting for transfers between devices, from_side(): return lax.ppermute(values, AXES, pairs)  14.6 us
    ppermute x4, starting transfers between devices, from_side(): return lax.ppermute(values, AXES, pairs)  12.6 us
    pallas_call x1, Pallas kernels, lines(): pl.pallas_call(functools.partial(line_body, sizes), out_shape=resident(16...  9.51 us
    pallas_call x1, Pallas kernels, setup(): pl.pallas_call(functools.partial(setup_body, sizes), out_shape=[edge, edg...  3.9 us
  transfers between devices with their start and end apart: 4, of which 3 were waited for; matrix products, arithmetic and copies ran while one was open for 0% of the time, Pallas kernels for 0%

profile of v9, /device:TPU:86, one launch (start us, length us, event | category | flops | bytes accessed | tf_op | source)
XLA Modules:
  0.0 121.2 jit_solution(5072304125405388204)
XLA Ops:
  0.0 1.1 pack.1
  1.1 58.8 %all_to_all.10 = f32[16,5,4,128]{3,2,1,0:T(4,128)S(1)} all-to-all(f32[16,5,4,128]{3,2,1,0:T(4,128)S(1)} %pack.1), channel_id=1, replica_groups=mesh['period'=2,'gx'=16,'gy'=8,'gz'=2] {'gx'}, dimensions={0} | all-to-all | bytes 327680 | tf_op jit(solution)/shard_map/all_to_all | solution.py:597
  59.9 4.8 %collective-permute-start = (f32[16,5,4,128]{3,2,1,0:T(4,128)S(1)}, f32[16,5,4,128]{3,2,1,0:T(4,128)S(1)}, u32[]{:S(2)}, u32[]{:S(2)}) collective-permute-start(f32[16,5,4,128]{3,2,1,0:T(4,128)S(1)} %all_to_all.10), channel_id=1, source_target_pairs={{0,2},{16,18},{32,34},{48,50},{64,66},{80,82},{96,98},{112,114},{1... | collective-permute-start | bytes 491528 | tf_op jit(solution)/shard_map/ppermute | solution.py:617
  64.6 2.0 %collective-permute-start.1 = (f32[16,5,4,128]{3,2,1,0:T(4,128)S(1)}, f32[16,5,4,128]{3,2,1,0:T(4,128)S(1)}, u32[]{:S(2)}, u32[]{:S(2)}) collective-permute-start(f32[16,5,4,128]{3,2,1,0:T(4,128)S(1)} %all_to_all.10), channel_id=1, source_target_pairs={{241,243},{225,227},{209,211},{193,195},{177,179},{161,163},{145,1... | collective-permute-start | bytes 491528 | tf_op jit(solution)/shard_map/ppermute | solution.py:617
  66.6 0.9 collective-permute-done
  67.5 5.6 %collective-permute-done.1 = f32[16,5,4,128]{3,2,1,0:T(4,128)S(1)} collective-permute-done((f32[16,5,4,128]{3,2,1,0:T(4,128)S(1)}, f32[16,5,4,128]{3,2,1,0:T(4,128)S(1)}, u32[]{:S(2)}, u32[]{:S(2)}) %collective-permute-start.1) | collective-permute-done | bytes 163872 | tf_op jit(solution)/shard_map/ppermute | solution.py:617
  73.1 1.3 %collective-permute-start.3 = (f32[48,5,4,128]{3,2,1,0:T(4,128)S(1)}, f32[48,5,4,128]{3,2,1,0:T(4,128)S(1)}, u32[]{:S(2)}, u32[]{:S(2)}) collective-permute-start(f32[48,5,4,128]{3,2,1,0:T(4,128)S(1)} %constant_dynamic-update-slice_fusion.middle), channel_id=1, source_target_pairs={{16,0},{32,16},{48,32},{64,48},{80,64},{96,80},{112,96},{128,112},... | collective-permute-start | bytes 1474568 | tf_op jit(solution)/shard_map/ppermute | solution.py:617
  74.4 4.6 %collective-permute-start.2 = (f32[48,5,4,128]{3,2,1,0:T(4,128)S(1)}, f32[48,5,4,128]{3,2,1,0:T(4,128)S(1)}, u32[]{:S(2)}, u32[]{:S(2)}) collective-permute-start(f32[48,5,4,128]{3,2,1,0:T(4,128)S(1)} %constant_dynamic-update-slice_fusion.middle), channel_id=1, source_target_pairs={{0,16},{16,32},{32,48},{48,64},{64,80},{80,96},{96,112},{112,128},... | collective-permute-start | bytes 1474568 | tf_op jit(solution)/shard_map/ppermute | solution.py:617
  79.1 8.2 %collective-permute-done.3.deep = f32[48,5,4,128]{3,2,1,0:T(4,128)S(1)} collective-permute-done((f32[48,5,4,128]{3,2,1,0:T(4,128)S(1)}, f32[48,5,4,128]{3,2,1,0:T(4,128)S(1)}, u32[]{:S(2)}, u32[]{:S(2)}) %collective-permute-start.3) | collective-permute-done | bytes 491552 | tf_op jit(solution)/shard_map/ppermute | solution.py:617
  87.2 0.0 collective-permute-done.2.shallow
  87.2 3.9 %setup.1 = (f32[3,16,24,128]{3,2,1,0:T(8,128)S(1)}, f32[3,16,24,128]{3,2,1,0:T(8,128)S(1)}, f32[3,16,24,128]{3,2,1,0:T(8,128)S(1)}, f32[3,65,24,128]{3,2,1,0:T(8...) custom-call(f32[48,5,4,128]{3,2,1,0:T(4,128)S(1)} %constant_dynamic-, ...), custom_call_target="tpu_custom_call" | custom-call | flops 134217728 | tf_op jit(solution)/shard_map/setup/pallas_call | solution.py:561
  91.2 9.5 %lines.1 = f32[16,3,4,128]{3,2,1,0:T(4,128)S(1)} custom-call(f32[48,5,4,128]{3,2,1,0:T(4,128)S(1)} %constant_dynamic-update-slice_fusion.middle, f32[48,5,4,128]{3,2,1,0:T(4,128)S(1)} %collective-permute-done.2.shallow, f32[48,5,4,128]{3,2,1,0:T(4,128)S(1)} %collective-permute-done.3.deep, f32[3,16,24,128]{3,2,1,0:T(8,128)S(1)} %get-tuple-element.16.free, ...), custom_call_target="tpu_custom_call" | custom-call | flops 134217728 | tf_op jit(solution)/shard_map/lines/pallas_call | solution.py:575
  100.7 19.7 %all_to_all.11.packed = f32[16,3,4,128]{3,2,1,0:T(4,128)S(1)} all-to-all(f32[16,3,4,128]{3,2,1,0:T(4,128)S(1)} %lines.1), channel_id=1, replica_groups=mesh['period'=2,'gx'=16,'gy'=8,'gz'=2] {'gx'}, dimensions={0} | all-to-all | bytes 196608 | tf_op jit(solution)/shard_map/all_to_all | solution.py:597
  120.4 0.9 unpack.1
  (3 shorter events, 0.1 us)
Async XLA Ops:
  59.9 7.6 %collective-permute-start = (f32[16,5,4,128]{3,2,1,0:T(4,128)S(1)}, f32[16,5,4,128]{3,2,1,0:T(4,128)S(1)}, u32[]{:S(2)}, u32[]{:S(2)}) collective-permute-start(f32[16,5,4,128]{3,2,1,0:T(4,128)S(1)} %all_to_all.10), channel_id=1, source_target_pairs={{0,2},{16,18},{32,34},{48,50},{64,66},{80,82},{96,98},{112,114},{1... | collective-permute-start | bytes 491528 | tf_op jit(solution)/shard_map/ppermute | solution.py:617
  64.6 8.5 %collective-permute-start.1 = (f32[16,5,4,128]{3,2,1,0:T(4,128)S(1)}, f32[16,5,4,128]{3,2,1,0:T(4,128)S(1)}, u32[]{:S(2)}, u32[]{:S(2)}) collective-permute-start(f32[16,5,4,128]{3,2,1,0:T(4,128)S(1)} %all_to_all.10), channel_id=1, source_target_pairs={{241,243},{225,227},{209,211},{193,195},{177,179},{161,163},{145,1... | collective-permute-start | bytes 491528 | tf_op jit(solution)/shard_map/ppermute | solution.py:617
  73.1 14.1 %collective-permute-start.3 = (f32[48,5,4,128]{3,2,1,0:T(4,128)S(1)}, f32[48,5,4,128]{3,2,1,0:T(4,128)S(1)}, u32[]{:S(2)}, u32[]{:S(2)}) collective-permute-start(f32[48,5,4,128]{3,2,1,0:T(4,128)S(1)} %constant_dynamic-update-slice_fusion.middle), channel_id=1, source_target_pairs={{16,0},{32,16},{48,32},{64,48},{80,64},{96,80},{112,96},{128,112},... | collective-permute-start | bytes 1474568 | tf_op jit(solution)/shard_map/ppermute | solution.py:617
  74.4 12.8 %collective-permute-start.2 = (f32[48,5,4,128]{3,2,1,0:T(4,128)S(1)}, f32[48,5,4,128]{3,2,1,0:T(4,128)S(1)}, u32[]{:S(2)}, u32[]{:S(2)}) collective-permute-start(f32[48,5,4,128]{3,2,1,0:T(4,128)S(1)} %constant_dynamic-update-slice_fusion.middle), channel_id=1, source_target_pairs={{0,16},{16,32},{32,48},{48,64},{64,80},{80,96},{96,112},{112,128},... | collective-permute-start | bytes 1474568 | tf_op jit(solution)/shard_map/ppermute | solution.py:617
